TPU v7x, 512 devices: a whole 4x8x8 slice. The times are simulated.
512 devices in a mesh: gx: 4 (over x), gy: 8 (over y), gz: 16 (over z, core).
Axes of the slice: x: 4, y: 8, z: 8, core: 2. Of those that a mesh axis runs over, the one named last changes fastest.
Arguments:
- right_side: float32 [32, 128, 2048], P('gx', 'gy', 'gz'), may hold values from -6 to 6
- conductance: float32 [32, 128, 2048], P('gx', 'gy', 'gz'), may hold values from 0.25 to 4
- extents: int32 [4, 8, 16], P('gx', 'gy', 'gz'), may hold values from 64 to 128, as said below
- coarse_factor: bfloat16 [512, 512], replicated, may hold values from -1 to 3, as said below
Outputs:
- solution_field: float32 [32, 128, 2048], P('gx', 'gy', 'gz')
- residual: float32 [32, 128, 2048], P('gx', 'gy', 'gz')
Inputs may be any that keep to these rules, and one draw needn't show every extreme that they name: `extents`: cells of a block whose third local index is below its count are fluid, the others padding; in every draw some block has all 128 layers fluid. `coarse_factor`: lower triangular with a positive diagonal.
All inputs are finite; a program needn't handle non-finite values.
Results may differ from a plain program's by a relative error of at most 0.0003.
Values sent between devices are 32-bit elements; how exact they have to be, the bound alone decides.
No kernel may reach another device: no remote copies, remote signals or barrier semaphores. Data moves between devices by JAX's collectives and lax.ppermute only.
A program may use at most 64 MiB of HBM per device.

v0:
```python
import jax
import jax.numpy as jnp
from jax import lax
from jax.sharding import Mesh
from jax.sharding import PartitionSpec as P

ITERS = 2
GZ = ("gz_0", "gz_1")


OMEGA = 0.8


def with_halo(x, sides, width):
    edges = {}
    for axis, dim in sides:
        size, length = (lax.axis_size(axis), x.shape[dim])
        up = [(i, (i + 1) % size) for i in range(size - 1)]
        last = lax.slice_in_dim(x, length - width, length, axis=dim)
        initial = lax.slice_in_dim(x, 0, width, axis=dim)
        edges[dim] = (
            lax.ppermute(last, axis, up),
            lax.ppermute(initial, axis, [(b, a) for a, b in up]),
        )
    done = []
    for _, dim in sides:
        low, high = edges[dim]
        around = [(width, width) if d in done else (0, 0) for d in range(x.ndim)]
        x = jnp.concatenate([jnp.pad(low, around), x, jnp.pad(high, around)], axis=dim)
        done.append(dim)
    return x


def from_everyone(x, axis):
    copies = jnp.broadcast_to(x, (lax.axis_size(axis), *x.shape))
    return lax.all_to_all(copies, axis, split_axis=0, concat_axis=0, tiled=True)


def laid_out(parts, dim):
    lengths = list(parts.shape[1:])
    lengths[dim] *= parts.shape[0]
    return jnp.moveaxis(parts, 0, dim).reshape(lengths)


def gathered_by_axis(x, axes, dim):
    far, near = axes
    initial = from_everyone(x, far)
    parts = jnp.swapaxes(from_everyone(initial, near), 0, 1)
    return laid_out(parts.reshape(-1, *x.shape), dim)


def taken_together(x, axis):
    everything = from_everyone(x, axis)
    return jnp.sum(everything, axis=0)


def by_axis(x, axes):
    far, near = axes
    nearer = taken_together(x, near)
    return taken_together(nearer, far)


def neighbour_slices():
    inner = slice(1, -1)
    return [
        (slice(2, None), inner, inner),
        (slice(None, -2), inner, inner),
        (inner, slice(2, None), inner),
        (inner, slice(None, -2), inner),
        (inner, inner, slice(2, None)),
        (inner, inner, slice(None, -2)),
    ]


def face_terms(padded, cond_padded):
    centre = (slice(1, -1), slice(1, -1), slice(1, -1))
    value_mid = padded[centre]
    cond_mid = cond_padded[centre]
    summed = jnp.zeros_like(value_mid)
    for place in neighbour_slices():
        summed = summed + 0.5 * (cond_mid + cond_padded[place]) * (value_mid - padded[place])
    return summed


def coef_total(cond_padded):
    centre = (slice(1, -1), slice(1, -1), slice(1, -1))
    cond_mid = cond_padded[centre]
    summed = jnp.zeros_like(cond_mid)
    for place in neighbour_slices():
        summed = summed + 0.5 * (cond_mid + cond_padded[place])
    return summed


def pool_sum(field):
    first, second, third = field.shape
    return field.reshape(first // 2, 2, second // 2, 2, third // 2, 2).sum(axis=(1, 3, 5))


def pool_max(field):
    first, second, third = field.shape
    return field.reshape(first // 2, 2, second // 2, 2, third // 2, 2).max(axis=(1, 3, 5))


def expand(field):
    first, second, third = field.shape
    wide = jnp.broadcast_to(field[:, None, :, None, :, None], (first, 2, second, 2, third, 2))
    return wide.reshape(2 * first, 2 * second, 2 * third)


def make_level(cond_padded, fluid, scale):
    inverse = fluid / (scale * coef_total(cond_padded) + 1.0 - fluid)
    return (cond_padded, fluid, scale, inverse)


def apply_level(field, level):
    padded = with_halo(field, (("gx", 0), ("gy", 1), (GZ, 2)), 1)
    return level[2] * level[1] * face_terms(padded, level[0])


def cycle(resid, levels):
    fine = levels[0]
    coarse_level = levels[1]
    first = OMEGA * fine[3] * resid
    image = apply_level(first, fine)
    below = OMEGA * coarse_level[3] * pool_sum(resid - image)
    return first + fine[1] * expand(below)


def on_device(right_side, conductance, extents, coarse_factor):
    factor = coarse_factor.astype(jnp.float32)
    size_x, size_y, size_z = right_side.shape
    block_cells = size_x * size_y * size_z
    layer = lax.broadcasted_iota(jnp.int32, right_side.shape, 2)
    fluid = (layer < extents[0, 0, 0]).astype(jnp.float32)
    fluid_mid = pool_max(fluid)
    cond_mid = pool_sum(conductance) / 8.0
    cond_padded = with_halo(cond_mid, (("gx", 0), ("gy", 1), (GZ, 2)), 1)
    coarse_level = make_level(cond_padded, fluid_mid, 4.0)
    fine_padded = with_halo(conductance, (("gx", 0), ("gy", 1), (GZ, 2)), 1)
    fine_level = make_level(fine_padded, fluid, 1.0)
    levels = [fine_level, coarse_level]
    index_x = lax.axis_index("gx")
    index_y = lax.axis_index("gy")
    index_z = lax.axis_index(GZ)
    count_x = lax.axis_size("gx")
    count_y = lax.axis_size("gy")
    count_z = lax.axis_size(GZ)
    offsets = jnp.arange(3, dtype=jnp.int32) - 1
    near_x = jnp.clip(index_x + offsets, 0, count_x - 1)
    near_y = jnp.clip(index_y + offsets, 0, count_y - 1)
    near_z = jnp.clip(index_z + offsets, 0, count_z - 1)
    near_flat = (near_x[:, None, None] * count_y + near_y[None, :, None]) * count_z + near_z[
        None, None, :
    ]

    def precondition(resid):
        second = cycle(resid, levels)
        padded = with_halo(second, (("gx", 0), ("gy", 1), (GZ, 2)), 1)
        smoothed = second + OMEGA * fine_level[3] * (
            resid - fluid * face_terms(padded, fine_level[0])
        )
        block_mean = jnp.sum(resid) / block_cells
        local_product = jnp.sum(resid * smoothed)
        means, products = (
            gathered_by_axis(block_mean.reshape(1), (("gx", "gy"), ("gz_0", "gz_1")), 0),
            gathered_by_axis(local_product.reshape(1), (("gx", "gy"), ("gz_0", "gz_1")), 0),
        )
        product = jnp.sum(products)
        coarse = jax.scipy.linalg.cho_solve((factor, True), means)
        table = coarse[near_flat]
        precond = smoothed + fluid * table[1, 1, 1]
        inner_value = product + block_cells * jnp.sum(means * coarse)
        precond_wide = None
        return (precond_wide, precond, inner_value)

    resid = fluid * right_side
    solution = jnp.zeros_like(resid)
    precond_wide, precond, inner_now = precondition(resid)
    direction = precond
    for step in range(ITERS):
        padded = with_halo(direction, (("gx", 0), ("gy", 1), (GZ, 2)), 1)
        image = fluid * face_terms(padded, fine_level[0])
        alpha = inner_now / by_axis(jnp.sum(direction * image), (("gx", "gy"), ("gz_0", "gz_1")))
        solution = solution + alpha * direction
        resid = resid - alpha * image
        if step + 1 < ITERS:
            precond_wide, precond, inner_next = precondition(resid)
            ratio = inner_next / inner_now
            direction = precond + ratio * direction
            inner_now = inner_next
    return (solution, resid)


def solution(mesh):
    split = Mesh(
        mesh.devices.reshape(mesh.shape["gx"], mesh.shape["gy"], 8, 2), ("gx", "gy", "gz_0", "gz_1")
    )
    in_specs = (P("gx", "gy", GZ), P("gx", "gy", GZ), P("gx", "gy", GZ), P())
    out_specs = (P("gx", "gy", GZ), P("gx", "gy", GZ))
    return jax.shard_map(
        on_device, mesh=split, in_specs=in_specs, out_specs=out_specs, check_vma=False
    )
```

profile of v0, /device:TPU:1, one launch (start us, length us, event | category | flops | bytes accessed | tf_op | source)
XLA Modules:
  0.0 432.7 jit_solution(4136253935926898240)
XLA Ops:
  1.4 4.0 collective-permute-start.3
  8.7 4.0 collective-permute-start.1
  13.7 5.4 %collective-permute-start.5 = (f32[8,16,1]{2,1,0:T(8,128)S(1)}, f32[8,16,1]{2,1,0:T(8,128)S(1)}, u32[]{:S(2)}, u32[]{:S(2)}) collective-permute-start(f32[8,16,1]{2,1,0:T(8,128)S(1)} %get-tuple-element.85), channel_id=1, source_target_pairs={{0,1},{1,2},{2,3},{3,4},{4,5},{5,6},{6,7},{7,8},{8,9},{9,10},{10,1... | collective-permute-start | bytes 1544 | tf_op jit(solution)/shard_map/ppermute | solution.py:22
  19.2 6.3 %reshape.190 = f32[4,2,8,2,64,2]{5,4,3,2,1,0:T(8,128)} reshape(f32[8,16,128]{2,1,0:T(8,128)} %param.7) | data formatting | bytes 131072 | tf_op jit(solution)/shard_map/reshape | solution.py:96
  25.5 2.6 reduce_sum.153
  29.1 8.1 %while.4 = (s32[]{:T(128)}, f32[512,512]{1,0:T(8,128)S(1)}, s32[4,2]{0,1:T(2,128)S(1)}, f32[4,128,128]{2,1,0:T(8,128)S(1)}, s32[]{:T(128)}) while((s32[]{:T(128)}, f32[512,512]{1,0:T(8,128)S(1)}, s32[4,2]{0,1:T(2,128)S(1)}, f32[4,128,128]{2,1,0:T(8,128)S(1)}, s32[]{:T(128)}) %tuple.66), condition=%wide.while_cond, body=%wide.while_body.sunk | while | flops 2 | bytes 131189 | solution.py:169
  39.7 4.3 collective-permute-start.9
  45.6 4.0 collective-permute-start.15
  50.9 2.6 collective-permute-start.13
  56.8 4.8 %collective-permute-start.17 = (f32[8,16,1]{2,1,0:T(8,128)S(1)}, f32[8,16,1]{2,1,0:T(8,128)S(1)}, u32[]{:S(2)}, u32[]{:S(2)}) collective-permute-start(f32[8,16,1]{2,1,0:T(8,128)S(1)} %get-tuple-element.80), channel_id=1, source_target_pairs={{0,1},{1,2},{2,3},{3,4},{4,5},{5,6},{6,7},{7,8},{8,9},{9,10},{10,1... | collective-permute-start | bytes 1544 | tf_op jit(solution)/shard_map/ppermute | solution.py:22
  61.7 4.3 collective-permute-start.7
  69.2 3.6 collective-permute-start.11
  73.0 5.5 %reshape.191 = f32[4,2,8,2,64,2]{5,4,3,2,1,0:T(8,128)} reshape(f32[8,16,128]{2,1,0:T(8,128)S(1)} %fusion.144) | data formatting | bytes 131072 | tf_op jit(solution)/shard_map/reshape | solution.py:96
  81.3 2.6 broadcast_in_dim.54
  83.8 4.0 reshape.192
  88.0 4.3 collective-permute-start.21
  93.5 4.0 collective-permute-start.19
  100.8 3.6 collective-permute-start.23
  107.8 16.3 %all-to-all-start.2 = ((f32[32,1,1]{2,1,0:T(1,128)}), f32[32,1,1]{2,1,0:T(1,128)S(1)}, u32[]{:S(2)}, u32[]{:S(2)}) async-start(f32[32,1,1]{2,1,0:T(1,128)} %broadcast_in_dim.57), calls=%async_computation.2 | async-start | bytes 32768 | tf_op jit(solution)/shard_map/all_to_all | solution.py:36
  124.3 8.4 %all-to-all-done.2 = f32[32,1,1]{2,1,0:T(1,128)S(1)} async-done(((f32[32,1,1]{2,1,0:T(1,128)}), f32[32,1,1]{2,1,0:T(1,128)S(1)}, u32[]{:S(2)}, u32[]{:S(2)}) %all-to-all-start.2) | async-done | bytes 160 | tf_op jit(solution)/shard_map/all_to_all | solution.py:36
  133.7 16.8 %all-to-all-start.3 = ((f32[16,32,1]{1,2,0:T(1,128)}), f32[16,32,1]{1,2,0:T(1,128)S(1)}, u32[]{:S(2)}, u32[]{:S(2)}) async-start(f32[16,32,1]{1,2,0:T(1,128)} %broadcast_in_dim.58), calls=%async_computation.3 | async-start | bytes 16384 | tf_op jit(solution)/shard_map/all_to_all | solution.py:36
  150.5 39.3 %custom-call.6 = f32[4,128,128]{1,2,0:T(8,128)S(1)} custom-call(f32[4,128,128]{2,1,0:T(8,128)S(1)} %get-tuple-element.17), custom_call_target="InvertDiagBlocksLowerTriangular" | custom-call | tf_op jit(solution)/shard_map/jit(_cho_solve)/triangular_solve | solution.py:169
  202.4 2.6 collective-permute-start.28
  205.0 3.4 collective-permute-start.29
  209.8 8.0 %all-to-all-start = ((f32[32,1,1]{2,1,0:T(1,128)}), f32[32,1,1]{2,1,0:T(1,128)S(1)}, u32[]{:S(2)}, u32[]{:S(2)}) async-start(f32[32,1,1]{2,1,0:T(1,128)} %broadcast_in_dim.55), calls=%async_computation | async-start | bytes 32768 | tf_op jit(solution)/shard_map/all_to_all | solution.py:36
  218.7 7.7 %all-to-all-done = f32[32,1,1]{2,1,0:T(1,128)S(1)} async-done(((f32[32,1,1]{2,1,0:T(1,128)}), f32[32,1,1]{2,1,0:T(1,128)S(1)}, u32[]{:S(2)}, u32[]{:S(2)}) %all-to-all-start) | async-done | bytes 160 | tf_op jit(solution)/shard_map/all_to_all | solution.py:36
  227.6 7.5 %all-to-all-start.4 = ((f32[16,1,1]{2,1,0:T(1,128)}), f32[16,1,1]{2,1,0:T(1,128)S(1)}, u32[]{:S(2)}, u32[]{:S(2)}) async-start(f32[16,1,1]{2,1,0:T(1,128)} %broadcast_in_dim.59), calls=%async_computation.4 | async-start | bytes 16384 | tf_op jit(solution)/shard_map/all_to_all | solution.py:36
  235.5 6.6 %all-to-all-done.4 = f32[16,1,1]{2,1,0:T(1,128)S(1)} async-done(((f32[16,1,1]{2,1,0:T(1,128)}), f32[16,1,1]{2,1,0:T(1,128)S(1)}, u32[]{:S(2)}, u32[]{:S(2)}) %all-to-all-start.4) | async-done | bytes 96 | tf_op jit(solution)/shard_map/all_to_all | solution.py:36
  242.7 3.9 all-to-all-start.1
  247.3 6.3 %all-to-all-done.1 = f32[16,32,1]{1,2,0:T(1,128)S(1)} async-done(((f32[16,32,1]{1,2,0:T(1,128)}), f32[16,32,1]{1,2,0:T(1,128)S(1)}, u32[]{:S(2)}, u32[]{:S(2)}) %all-to-all-start.1) | async-done | bytes 2080 | tf_op jit(solution)/shard_map/all_to_all | solution.py:36
  254.9 3.8 all-to-all-start.5
  261.5 5.9 %all-to-all-done.5 = f32[32,1,1]{2,1,0:T(1,128)S(1)} async-done(((f32[32,1,1]{2,1,0:T(1,128)}), f32[32,1,1]{2,1,0:T(1,128)S(1)}, u32[]{:S(2)}, u32[]{:S(2)}) %all-to-all-start.5) | async-done | bytes 160 | tf_op jit(solution)/shard_map/all_to_all | solution.py:36
  275.9 4.3 collective-permute-start.34
  283.8 5.5 %reshape.193 = f32[4,2,8,2,64,2]{5,4,3,2,1,0:T(8,128)} reshape(f32[8,16,128]{2,1,0:T(8,128)S(1)} %fusion.80) | data formatting | bytes 131072 | tf_op jit(solution)/shard_map/reshape | solution.py:96
  291.9 2.6 broadcast_in_dim.61
  294.5 4.0 reshape.194
  298.5 4.3 collective-permute-start.39
  304.1 4.3 collective-permute-start.37
  312.2 4.4 %collective-permute-start.41 = (f32[8,16,1]{2,1,0:T(8,128)S(1)}, f32[8,16,1]{2,1,0:T(8,128)S(1)}, u32[]{:S(2)}, u32[]{:S(2)}) collective-permute-start(f32[8,16,1]{2,1,0:T(8,128)S(1)} %get-tuple-element.56), channel_id=1, source_target_pairs={{0,1},{1,2},{2,3},{3,4},{4,5},{5,6},{6,7},{7,8},{8,9},{9,10},{10,1... | collective-permute-start | bytes 1544 | tf_op jit(solution)/shard_map/ppermute | solution.py:22
  319.3 17.7 %all_to_all.80 = f32[32,1,1]{2,1,0:T(1,128)S(1)} all-to-all(f32[32,1,1]{2,1,0:T(1,128)S(1)} %broadcast_in_dim.64), channel_id=1, replica_groups=mesh['gx'=4,'gy'=8,'gz_0'=8,'gz_1'=2] {'gx','gy'}, dimensions={0} | all-to-all | bytes 256 | tf_op jit(solution)/shard_map/all_to_all | solution.py:36
  338.3 3.8 all-to-all-start.6
  342.4 8.3 %all-to-all-done.6 = f32[32,1,1]{2,1,0:T(1,128)S(1)} async-done(((f32[32,1,1]{2,1,0:T(1,128)}), f32[32,1,1]{2,1,0:T(1,128)S(1)}, u32[]{:S(2)}, u32[]{:S(2)}) %all-to-all-start.6) | async-done | bytes 160 | tf_op jit(solution)/shard_map/all_to_all | solution.py:36
  351.3 9.6 %all-to-all-start.9 = ((f32[16,32,1]{1,2,0:T(1,128)}), f32[16,32,1]{1,2,0:T(1,128)S(1)}, u32[]{:S(2)}, u32[]{:S(2)}) async-start(f32[16,32,1]{1,2,0:T(1,128)} %broadcast_in_dim.65), calls=%async_computation.9 | async-start | bytes 16384 | tf_op jit(solution)/shard_map/all_to_all | solution.py:36
  361.2 6.6 %all-to-all-done.9 = f32[16,32,1]{1,2,0:T(1,128)S(1)} async-done(((f32[16,32,1]{1,2,0:T(1,128)}), f32[16,32,1]{1,2,0:T(1,128)S(1)}, u32[]{:S(2)}, u32[]{:S(2)}) %all-to-all-start.9) | async-done | bytes 2080 | tf_op jit(solution)/shard_map/all_to_all | solution.py:36
  368.5 3.9 all-to-all-start.7
  388.6 3.1 collective-permute-start.46
  396.9 15.4 %all_to_all.81 = f32[16,1,1]{2,1,0:T(1,128)S(1)} all-to-all(f32[16,1,1]{2,1,0:T(1,128)S(1)} %broadcast_in_dim.66), channel_id=1, replica_groups=mesh['gx'=4,'gy'=8,'gz_0'=8,'gz_1'=2] {'gz_0','gz_1'}, dimensions={0} | all-to-all | bytes 128 | tf_op jit(solution)/shard_map/all_to_all | solution.py:36
  413.6 16.5 %all_to_all.82 = f32[32,1,1]{2,1,0:T(1,128)S(1)} all-to-all(f32[32,1,1]{2,1,0:T(1,128)S(1)} %broadcast_in_dim.67), channel_id=1, replica_groups=mesh['gx'=4,'gy'=8,'gz_0'=8,'gz_1'=2] {'gx','gy'}, dimensions={0} | all-to-all | bytes 256 | tf_op jit(solution)/shard_map/all_to_all | solution.py:36
  (239 shorter events, 103.9 us)
Async XLA Ops:
  1.4 35.8 %collective-permute-start.3 = (f32[8,1,128]{2,1,0:T(1,128)S(1)}, f32[8,1,128]{2,1,0:T(1,128)S(1)}, u32[]{:S(2)}, u32[]{:S(2)}) collective-permute-start(f32[8,1,128]{2,1,0:T(1,128)S(1)} %get-tuple-element.87), channel_id=1, source_target_pairs={{0,16},{16,32},{32,48},{48,64},{64,80},{80,96},{96,112},{1,17},{17... | collective-permute-start | bytes 12296 | tf_op jit(solution)/shard_map/ppermute | solution.py:22
  5.4 34.3 %collective-permute-start.2 = (f32[8,1,128]{2,1,0:T(1,128)S(1)}, f32[8,1,128]{2,1,0:T(1,128)S(1)}, u32[]{:S(2)}, u32[]{:S(2)}) collective-permute-start(f32[8,1,128]{2,1,0:T(1,128)S(1)} %get-tuple-element.88), channel_id=1, source_target_pairs={{16,0},{32,16},{48,32},{64,48},{80,64},{96,80},{112,96},{17,1},{33... | collective-permute-start | bytes 12296 | tf_op jit(solution)/shard_map/ppermute | solution.py:23
  7.5 37.9 %collective-permute-start = (f32[1,16,128]{2,1,0:T(8,128)S(1)}, f32[1,16,128]{2,1,0:T(8,128)S(1)}, u32[]{:S(2)}, u32[]{:S(2)}) collective-permute-start(f32[1,16,128]{2,1,0:T(8,128)S(1)} %get-tuple-element.89), channel_id=1, source_target_pairs={{128,0},{256,128},{384,256},{129,1},{257,129},{385,257},{130,2},{2... | collective-permute-start | bytes 24584 | tf_op jit(solution)/shard_map/ppermute | solution.py:23
  8.7 35.3 %collective-permute-start.1 = (f32[1,16,128]{2,1,0:T(8,128)S(1)}, f32[1,16,128]{2,1,0:T(8,128)S(1)}, u32[]{:S(2)}, u32[]{:S(2)}) collective-permute-start(f32[1,16,128]{2,1,0:T(8,128)S(1)} %get-tuple-element.90), channel_id=1, source_target_pairs={{0,128},{128,256},{256,384},{1,129},{129,257},{257,385},{2,130},{1... | collective-permute-start | bytes 24584 | tf_op jit(solution)/shard_map/ppermute | solution.py:22
  13.7 31.7 %collective-permute-start.5 = (f32[8,16,1]{2,1,0:T(8,128)S(1)}, f32[8,16,1]{2,1,0:T(8,128)S(1)}, u32[]{:S(2)}, u32[]{:S(2)}) collective-permute-start(f32[8,16,1]{2,1,0:T(8,128)S(1)} %get-tuple-element.85), channel_id=1, source_target_pairs={{0,1},{1,2},{2,3},{3,4},{4,5},{5,6},{6,7},{7,8},{8,9},{9,10},{10,1... | collective-permute-start | bytes 1544 | tf_op jit(solution)/shard_map/ppermute | solution.py:22
  39.7 13.8 %collective-permute-start.9 = (f32[4,1,64]{2,1,0:T(1,128)S(1)}, f32[4,1,64]{2,1,0:T(1,128)S(1)}, u32[]{:S(2)}, u32[]{:S(2)}) collective-permute-start(f32[4,1,64]{2,1,0:T(1,128)S(1)} %get-tuple-element.93), channel_id=1, source_target_pairs={{0,16},{16,32},{32,48},{48,64},{64,80},{80,96},{96,112},{1,17},{17... | collective-permute-start | bytes 3080 | tf_op jit(solution)/shard_map/ppermute | solution.py:22
  44.0 10.8 %collective-permute-start.8 = (f32[4,1,64]{2,1,0:T(1,128)S(1)}, f32[4,1,64]{2,1,0:T(1,128)S(1)}, u32[]{:S(2)}, u32[]{:S(2)}) collective-permute-start(f32[4,1,64]{2,1,0:T(1,128)S(1)} %get-tuple-element.94), channel_id=1, source_target_pairs={{16,0},{32,16},{48,32},{64,48},{80,64},{96,80},{112,96},{17,1},{33... | collective-permute-start | bytes 3080 | tf_op jit(solution)/shard_map/ppermute | solution.py:23
  45.6 11.2 %collective-permute-start.15 = (f32[8,1,128]{2,1,0:T(1,128)S(1)}, f32[8,1,128]{2,1,0:T(1,128)S(1)}, u32[]{:S(2)}, u32[]{:S(2)}) collective-permute-start(f32[8,1,128]{2,1,0:T(1,128)S(1)} %get-tuple-element.83), channel_id=1, source_target_pairs={{0,16},{16,32},{32,48},{48,64},{64,80},{80,96},{96,112},{1,17},{17... | collective-permute-start | bytes 12296 | tf_op jit(solution)/shard_map/ppermute | solution.py:22
  49.6 12.0 %collective-permute-start.14 = (f32[8,1,128]{2,1,0:T(1,128)S(1)}, f32[8,1,128]{2,1,0:T(1,128)S(1)}, u32[]{:S(2)}, u32[]{:S(2)}) collective-permute-start(f32[8,1,128]{2,1,0:T(1,128)S(1)} %get-tuple-element.84), channel_id=1, source_target_pairs={{16,0},{32,16},{48,32},{64,48},{80,64},{96,80},{112,96},{17,1},{33... | collective-permute-start | bytes 12296 | tf_op jit(solution)/shard_map/ppermute | solution.py:23
  50.9 18.3 %collective-permute-start.13 = (f32[1,16,128]{2,1,0:T(8,128)S(1)}, f32[1,16,128]{2,1,0:T(8,128)S(1)}, u32[]{:S(2)}, u32[]{:S(2)}) collective-permute-start(f32[1,16,128]{2,1,0:T(8,128)S(1)} %get-tuple-element.81), channel_id=1, source_target_pairs={{0,128},{128,256},{256,384},{1,129},{129,257},{257,385},{2,130},{1... | collective-permute-start | bytes 24584 | tf_op jit(solution)/shard_map/ppermute | solution.py:22
  53.5 19.4 %collective-permute-start.12 = (f32[1,16,128]{2,1,0:T(8,128)S(1)}, f32[1,16,128]{2,1,0:T(8,128)S(1)}, u32[]{:S(2)}, u32[]{:S(2)}) collective-permute-start(f32[1,16,128]{2,1,0:T(8,128)S(1)} %get-tuple-element.82), channel_id=1, source_target_pairs={{128,0},{256,128},{384,256},{129,1},{257,129},{385,257},{130,2},{2... | collective-permute-start | bytes 24584 | tf_op jit(solution)/shard_map/ppermute | solution.py:23
  54.9 11.1 %collective-permute-start.16 = (f32[8,16,1]{2,1,0:T(8,128)S(1)}, f32[8,16,1]{2,1,0:T(8,128)S(1)}, u32[]{:S(2)}, u32[]{:S(2)}) collective-permute-start(f32[8,16,1]{2,1,0:T(8,128)S(1)} %get-tuple-element.79), channel_id=1, source_target_pairs={{1,0},{2,1},{3,2},{4,3},{5,4},{6,5},{7,6},{8,7},{9,8},{10,9},{11,1... | collective-permute-start | bytes 1544 | tf_op jit(solution)/shard_map/ppermute | solution.py:23
  56.8 10.4 %collective-permute-start.17 = (f32[8,16,1]{2,1,0:T(8,128)S(1)}, f32[8,16,1]{2,1,0:T(8,128)S(1)}, u32[]{:S(2)}, u32[]{:S(2)}) collective-permute-start(f32[8,16,1]{2,1,0:T(8,128)S(1)} %get-tuple-element.80), channel_id=1, source_target_pairs={{0,1},{1,2},{2,3},{3,4},{4,5},{5,6},{6,7},{7,8},{8,9},{9,10},{10,1... | collective-permute-start | bytes 1544 | tf_op jit(solution)/shard_map/ppermute | solution.py:22
  61.7 19.5 %collective-permute-start.7 = (f32[1,8,64]{2,1,0:T(8,128)S(1)}, f32[1,8,64]{2,1,0:T(8,128)S(1)}, u32[]{:S(2)}, u32[]{:S(2)}) collective-permute-start(f32[1,8,64]{2,1,0:T(8,128)S(1)} %get-tuple-element.95), channel_id=1, source_target_pairs={{0,128},{128,256},{256,384},{1,129},{129,257},{257,385},{2,130},{1... | collective-permute-start | bytes 6152 | tf_op jit(solution)/shard_map/ppermute | solution.py:22
  66.0 15.2 %collective-permute-start.6 = (f32[1,8,64]{2,1,0:T(8,128)S(1)}, f32[1,8,64]{2,1,0:T(8,128)S(1)}, u32[]{:S(2)}, u32[]{:S(2)}) collective-permute-start(f32[1,8,64]{2,1,0:T(8,128)S(1)} %get-tuple-element.96), channel_id=1, source_target_pairs={{128,0},{256,128},{384,256},{129,1},{257,129},{385,257},{130,2},{2... | collective-permute-start | bytes 6152 | tf_op jit(solution)/shard_map/ppermute | solution.py:23
  67.3 13.9 %collective-permute-start.10 = (f32[4,8,1]{2,1,0:T(8,128)S(1)}, f32[4,8,1]{2,1,0:T(8,128)S(1)}, u32[]{:S(2)}, u32[]{:S(2)}) collective-permute-start(f32[4,8,1]{2,1,0:T(8,128)S(1)} %get-tuple-element.91), channel_id=1, source_target_pairs={{1,0},{2,1},{3,2},{4,3},{5,4},{6,5},{7,6},{8,7},{9,8},{10,9},{11,1... | collective-permute-start | bytes 392 | tf_op jit(solution)/shard_map/ppermute | solution.py:23
  69.2 11.9 %collective-permute-start.11 = (f32[4,8,1]{2,1,0:T(8,128)S(1)}, f32[4,8,1]{2,1,0:T(8,128)S(1)}, u32[]{:S(2)}, u32[]{:S(2)}) collective-permute-start(f32[4,8,1]{2,1,0:T(8,128)S(1)} %get-tuple-element.92), channel_id=1, source_target_pairs={{0,1},{1,2},{2,3},{3,4},{4,5},{5,6},{6,7},{7,8},{8,9},{9,10},{10,1... | collective-permute-start | bytes 392 | tf_op jit(solution)/shard_map/ppermute | solution.py:22
  88.0 12.8 %collective-permute-start.21 = (f32[8,1,128]{2,1,0:T(1,128)S(1)}, f32[8,1,128]{2,1,0:T(1,128)S(1)}, u32[]{:S(2)}, u32[]{:S(2)}) collective-permute-start(f32[8,1,128]{2,1,0:T(1,128)S(1)} %get-tuple-element.75), channel_id=1, source_target_pairs={{0,16},{16,32},{32,48},{48,64},{64,80},{80,96},{96,112},{1,17},{17... | collective-permute-start | bytes 12296 | tf_op jit(solution)/shard_map/ppermute | solution.py:22
  92.2 12.2 %collective-permute-start.20 = (f32[8,1,128]{2,1,0:T(1,128)S(1)}, f32[8,1,128]{2,1,0:T(1,128)S(1)}, u32[]{:S(2)}, u32[]{:S(2)}) collective-permute-start(f32[8,1,128]{2,1,0:T(1,128)S(1)} %get-tuple-element.76), channel_id=1, source_target_pairs={{16,0},{32,16},{48,32},{64,48},{80,64},{96,80},{112,96},{17,1},{33... | collective-permute-start | bytes 12296 | tf_op jit(solution)/shard_map/ppermute | solution.py:23
  93.5 12.2 %collective-permute-start.19 = (f32[1,16,128]{2,1,0:T(8,128)S(1)}, f32[1,16,128]{2,1,0:T(8,128)S(1)}, u32[]{:S(2)}, u32[]{:S(2)}) collective-permute-start(f32[1,16,128]{2,1,0:T(8,128)S(1)} %get-tuple-element.77), channel_id=1, source_target_pairs={{0,128},{128,256},{256,384},{1,129},{129,257},{257,385},{2,130},{1... | collective-permute-start | bytes 24584 | tf_op jit(solution)/shard_map/ppermute | solution.py:22
  97.5 8.2 %collective-permute-start.18 = (f32[1,16,128]{2,1,0:T(8,128)S(1)}, f32[1,16,128]{2,1,0:T(8,128)S(1)}, u32[]{:S(2)}, u32[]{:S(2)}) collective-permute-start(f32[1,16,128]{2,1,0:T(8,128)S(1)} %get-tuple-element.78), channel_id=1, source_target_pairs={{128,0},{256,128},{384,256},{129,1},{257,129},{385,257},{130,2},{2... | collective-permute-start | bytes 24584 | tf_op jit(solution)/shard_map/ppermute | solution.py:23
  107.8 24.9 %all-to-all-start.2 = ((f32[32,1,1]{2,1,0:T(1,128)}), f32[32,1,1]{2,1,0:T(1,128)S(1)}, u32[]{:S(2)}, u32[]{:S(2)}) async-start(f32[32,1,1]{2,1,0:T(1,128)} %broadcast_in_dim.57), calls=%async_computation.2 | async-start | bytes 32768 | tf_op jit(solution)/shard_map/all_to_all | solution.py:36
  133.7 56.1 %all-to-all-start.3 = ((f32[16,32,1]{1,2,0:T(1,128)}), f32[16,32,1]{1,2,0:T(1,128)S(1)}, u32[]{:S(2)}, u32[]{:S(2)}) async-start(f32[16,32,1]{1,2,0:T(1,128)} %broadcast_in_dim.58), calls=%async_computation.3 | async-start | bytes 16384 | tf_op jit(solution)/shard_map/all_to_all | solution.py:36
  195.1 9.9 %collective-permute-start.27 = (f32[8,1,128]{2,1,0:T(1,128)S(1)}, f32[8,1,128]{2,1,0:T(1,128)S(1)}, u32[]{:S(2)}, u32[]{:S(2)}) collective-permute-start(f32[8,1,128]{2,1,0:T(1,128)S(1)} %get-tuple-element.69), channel_id=1, source_target_pairs={{0,16},{16,32},{32,48},{48,64},{64,80},{80,96},{96,112},{1,17},{17... | collective-permute-start | bytes 12296 | tf_op jit(solution)/shard_map/ppermute | solution.py:22
  197.5 20.3 %collective-permute-start.26 = (f32[8,1,128]{2,1,0:T(1,128)S(1)}, f32[8,1,128]{2,1,0:T(1,128)S(1)}, u32[]{:S(2)}, u32[]{:S(2)}) collective-permute-start(f32[8,1,128]{2,1,0:T(1,128)S(1)} %get-tuple-element.70), channel_id=1, source_target_pairs={{16,0},{32,16},{48,32},{64,48},{80,64},{96,80},{112,96},{17,1},{33... | collective-permute-start | bytes 12296 | tf_op jit(solution)/shard_map/ppermute | solution.py:23
  198.8 19.0 %collective-permute-start.25 = (f32[1,16,128]{2,1,0:T(8,128)S(1)}, f32[1,16,128]{2,1,0:T(8,128)S(1)}, u32[]{:S(2)}, u32[]{:S(2)}) collective-permute-start(f32[1,16,128]{2,1,0:T(8,128)S(1)} %get-tuple-element.71), channel_id=1, source_target_pairs={{0,128},{128,256},{256,384},{1,129},{129,257},{257,385},{2,130},{1... | collective-permute-start | bytes 24584 | tf_op jit(solution)/shard_map/ppermute | solution.py:22
  201.0 16.8 %collective-permute-start.24 = (f32[1,16,128]{2,1,0:T(8,128)S(1)}, f32[1,16,128]{2,1,0:T(8,128)S(1)}, u32[]{:S(2)}, u32[]{:S(2)}) collective-permute-start(f32[1,16,128]{2,1,0:T(8,128)S(1)} %get-tuple-element.72), channel_id=1, source_target_pairs={{128,0},{256,128},{384,256},{129,1},{257,129},{385,257},{130,2},{2... | collective-permute-start | bytes 24584 | tf_op jit(solution)/shard_map/ppermute | solution.py:23
  202.4 15.4 %collective-permute-start.28 = (f32[8,16,1]{2,1,0:T(8,128)S(1)}, f32[8,16,1]{2,1,0:T(8,128)S(1)}, u32[]{:S(2)}, u32[]{:S(2)}) collective-permute-start(f32[8,16,1]{2,1,0:T(8,128)S(1)} %get-tuple-element.67), channel_id=1, source_target_pairs={{1,0},{2,1},{3,2},{4,3},{5,4},{6,5},{7,6},{8,7},{9,8},{10,9},{11,1... | collective-permute-start | bytes 1544 | tf_op jit(solution)/shard_map/ppermute | solution.py:23
  205.0 12.8 %collective-permute-start.29 = (f32[8,16,1]{2,1,0:T(8,128)S(1)}, f32[8,16,1]{2,1,0:T(8,128)S(1)}, u32[]{:S(2)}, u32[]{:S(2)}) collective-permute-start(f32[8,16,1]{2,1,0:T(8,128)S(1)} %get-tuple-element.68), channel_id=1, source_target_pairs={{0,1},{1,2},{2,3},{3,4},{4,5},{5,6},{6,7},{7,8},{8,9},{9,10},{10,1... | collective-permute-start | bytes 1544 | tf_op jit(solution)/shard_map/ppermute | solution.py:22
  209.8 16.6 %all-to-all-start = ((f32[32,1,1]{2,1,0:T(1,128)}), f32[32,1,1]{2,1,0:T(1,128)S(1)}, u32[]{:S(2)}, u32[]{:S(2)}) async-start(f32[32,1,1]{2,1,0:T(1,128)} %broadcast_in_dim.55), calls=%async_computation | async-start | bytes 32768 | tf_op jit(solution)/shard_map/all_to_all | solution.py:36
  227.6 14.5 %all-to-all-start.4 = ((f32[16,1,1]{2,1,0:T(1,128)}), f32[16,1,1]{2,1,0:T(1,128)S(1)}, u32[]{:S(2)}, u32[]{:S(2)}) async-start(f32[16,1,1]{2,1,0:T(1,128)} %broadcast_in_dim.59), calls=%async_computation.4 | async-start | bytes 16384 | tf_op jit(solution)/shard_map/all_to_all | solution.py:36
  242.7 10.9 %all-to-all-start.1 = ((f32[16,32,1]{1,2,0:T(1,128)}), f32[16,32,1]{1,2,0:T(1,128)S(1)}, u32[]{:S(2)}, u32[]{:S(2)}) async-start(f32[16,32,1]{1,2,0:T(1,128)} %broadcast_in_dim.56), calls=%async_computation.1 | async-start | bytes 16384 | tf_op jit(solution)/shard_map/all_to_all | solution.py:36
  254.9 12.4 %all-to-all-start.5 = ((f32[32,1,1]{2,1,0:T(1,128)}), f32[32,1,1]{2,1,0:T(1,128)S(1)}, u32[]{:S(2)}, u32[]{:S(2)}) async-start(f32[32,1,1]{2,1,0:T(1,128)} %broadcast_in_dim.60), calls=%async_computation.5 | async-start | bytes 32768 | tf_op jit(solution)/shard_map/all_to_all | solution.py:36
  268.8 11.5 %collective-permute-start.33 = (f32[8,1,128]{2,1,0:T(1,128)S(1)}, f32[8,1,128]{2,1,0:T(1,128)S(1)}, u32[]{:S(2)}, u32[]{:S(2)}) collective-permute-start(f32[8,1,128]{2,1,0:T(1,128)S(1)} %get-tuple-element.65), channel_id=1, source_target_pairs={{0,16},{16,32},{32,48},{48,64},{64,80},{80,96},{96,112},{1,17},{17... | collective-permute-start | bytes 12296 | tf_op jit(solution)/shard_map/ppermute | solution.py:22
  271.0 11.3 %collective-permute-start.32 = (f32[8,1,128]{2,1,0:T(1,128)S(1)}, f32[8,1,128]{2,1,0:T(1,128)S(1)}, u32[]{:S(2)}, u32[]{:S(2)}) collective-permute-start(f32[8,1,128]{2,1,0:T(1,128)S(1)} %get-tuple-element.66), channel_id=1, source_target_pairs={{16,0},{32,16},{48,32},{64,48},{80,64},{96,80},{112,96},{17,1},{33... | collective-permute-start | bytes 12296 | tf_op jit(solution)/shard_map/ppermute | solution.py:23
  272.3 11.3 %collective-permute-start.31 = (f32[1,16,128]{2,1,0:T(8,128)S(1)}, f32[1,16,128]{2,1,0:T(8,128)S(1)}, u32[]{:S(2)}, u32[]{:S(2)}) collective-permute-start(f32[1,16,128]{2,1,0:T(8,128)S(1)} %get-tuple-element.63), channel_id=1, source_target_pairs={{0,128},{128,256},{256,384},{1,129},{129,257},{257,385},{2,130},{1... | collective-permute-start | bytes 24584 | tf_op jit(solution)/shard_map/ppermute | solution.py:22
  274.6 9.1 %collective-permute-start.30 = (f32[1,16,128]{2,1,0:T(8,128)S(1)}, f32[1,16,128]{2,1,0:T(8,128)S(1)}, u32[]{:S(2)}, u32[]{:S(2)}) collective-permute-start(f32[1,16,128]{2,1,0:T(8,128)S(1)} %get-tuple-element.64), channel_id=1, source_target_pairs={{128,0},{256,128},{384,256},{129,1},{257,129},{385,257},{130,2},{2... | collective-permute-start | bytes 24584 | tf_op jit(solution)/shard_map/ppermute | solution.py:23
  298.5 13.6 %collective-permute-start.39 = (f32[8,1,128]{2,1,0:T(1,128)S(1)}, f32[8,1,128]{2,1,0:T(1,128)S(1)}, u32[]{:S(2)}, u32[]{:S(2)}) collective-permute-start(f32[8,1,128]{2,1,0:T(1,128)S(1)} %get-tuple-element.57), channel_id=1, source_target_pairs={{0,16},{16,32},{32,48},{48,64},{64,80},{80,96},{96,112},{1,17},{17... | collective-permute-start | bytes 12296 | tf_op jit(solution)/shard_map/ppermute | solution.py:22
  302.8 13.7 %collective-permute-start.38 = (f32[8,1,128]{2,1,0:T(1,128)S(1)}, f32[8,1,128]{2,1,0:T(1,128)S(1)}, u32[]{:S(2)}, u32[]{:S(2)}) collective-permute-start(f32[8,1,128]{2,1,0:T(1,128)S(1)} %get-tuple-element.58), channel_id=1, source_target_pairs={{16,0},{32,16},{48,32},{64,48},{80,64},{96,80},{112,96},{17,1},{33... | collective-permute-start | bytes 12296 | tf_op jit(solution)/shard_map/ppermute | solution.py:23
  304.1 13.7 %collective-permute-start.37 = (f32[1,16,128]{2,1,0:T(8,128)S(1)}, f32[1,16,128]{2,1,0:T(8,128)S(1)}, u32[]{:S(2)}, u32[]{:S(2)}) collective-permute-start(f32[1,16,128]{2,1,0:T(8,128)S(1)} %get-tuple-element.59), channel_id=1, source_target_pairs={{0,128},{128,256},{256,384},{1,129},{129,257},{257,385},{2,130},{1... | collective-permute-start | bytes 24584 | tf_op jit(solution)/shard_map/ppermute | solution.py:22
  308.4 9.5 %collective-permute-start.36 = (f32[1,16,128]{2,1,0:T(8,128)S(1)}, f32[1,16,128]{2,1,0:T(8,128)S(1)}, u32[]{:S(2)}, u32[]{:S(2)}) collective-permute-start(f32[1,16,128]{2,1,0:T(8,128)S(1)} %get-tuple-element.60), channel_id=1, source_target_pairs={{128,0},{256,128},{384,256},{129,1},{257,129},{385,257},{130,2},{2... | collective-permute-start | bytes 24584 | tf_op jit(solution)/shard_map/ppermute | solution.py:23
  338.3 12.4 %all-to-all-start.6 = ((f32[32,1,1]{2,1,0:T(1,128)}), f32[32,1,1]{2,1,0:T(1,128)S(1)}, u32[]{:S(2)}, u32[]{:S(2)}) async-start(f32[32,1,1]{2,1,0:T(1,128)} %broadcast_in_dim.62), calls=%async_computation.6 | async-start | bytes 32768 | tf_op jit(solution)/shard_map/all_to_all | solution.py:36
  351.3 16.5 %all-to-all-start.9 = ((f32[16,32,1]{1,2,0:T(1,128)}), f32[16,32,1]{1,2,0:T(1,128)S(1)}, u32[]{:S(2)}, u32[]{:S(2)}) async-start(f32[16,32,1]{1,2,0:T(1,128)} %broadcast_in_dim.65), calls=%async_computation.9 | async-start | bytes 16384 | tf_op jit(solution)/shard_map/all_to_all | solution.py:36
  368.5 10.9 %all-to-all-start.7 = ((f32[16,32,1]{1,2,0:T(1,128)}), f32[16,32,1]{1,2,0:T(1,128)S(1)}, u32[]{:S(2)}, u32[]{:S(2)}) async-start(f32[16,32,1]{1,2,0:T(1,128)} %broadcast_in_dim.63), calls=%async_computation.7 | async-start | bytes 16384 | tf_op jit(solution)/shard_map/all_to_all | solution.py:36
  381.4 10.3 %collective-permute-start.45 = (f32[8,1,128]{2,1,0:T(1,128)S(1)}, f32[8,1,128]{2,1,0:T(1,128)S(1)}, u32[]{:S(2)}, u32[]{:S(2)}) collective-permute-start(f32[8,1,128]{2,1,0:T(1,128)S(1)} %get-tuple-element.51), channel_id=1, source_target_pairs={{0,16},{16,32},{32,48},{48,64},{64,80},{80,96},{96,112},{1,17},{17... | collective-permute-start | bytes 12296 | tf_op jit(solution)/shard_map/ppermute | solution.py:22
  383.7 10.5 %collective-permute-start.44 = (f32[8,1,128]{2,1,0:T(1,128)S(1)}, f32[8,1,128]{2,1,0:T(1,128)S(1)}, u32[]{:S(2)}, u32[]{:S(2)}) collective-permute-start(f32[8,1,128]{2,1,0:T(1,128)S(1)} %get-tuple-element.52), channel_id=1, source_target_pairs={{16,0},{32,16},{48,32},{64,48},{80,64},{96,80},{112,96},{17,1},{33... | collective-permute-start | bytes 12296 | tf_op jit(solution)/shard_map/ppermute | solution.py:23
  385.0 10.5 %collective-permute-start.43 = (f32[1,16,128]{2,1,0:T(8,128)S(1)}, f32[1,16,128]{2,1,0:T(8,128)S(1)}, u32[]{:S(2)}, u32[]{:S(2)}) collective-permute-start(f32[1,16,128]{2,1,0:T(8,128)S(1)} %get-tuple-element.53), channel_id=1, source_target_pairs={{0,128},{128,256},{256,384},{1,129},{129,257},{257,385},{2,130},{1... | collective-permute-start | bytes 24584 | tf_op jit(solution)/shard_map/ppermute | solution.py:22
  387.2 8.3 %collective-permute-start.42 = (f32[1,16,128]{2,1,0:T(8,128)S(1)}, f32[1,16,128]{2,1,0:T(8,128)S(1)}, u32[]{:S(2)}, u32[]{:S(2)}) collective-permute-start(f32[1,16,128]{2,1,0:T(8,128)S(1)} %get-tuple-element.54), channel_id=1, source_target_pairs={{128,0},{256,128},{384,256},{129,1},{257,129},{385,257},{130,2},{2... | collective-permute-start | bytes 24584 | tf_op jit(solution)/shard_map/ppermute | solution.py:23
  (12 other events, 100.0 us)
where the time goes:
time: 435 us; the launch traced here: 433 us
  starting transfers between devices  198 us (46%)
  other arithmetic  60.3 us (14%)
  waiting for transfers between devices  56.1 us (13%)
  local copies, waits for them, and re-layouts  54.6 us (13%)
  blocking collectives  49.6 us (11%)
  between operations  8.02 us (2%)
  matrix products  5.82 us (1%)
    ppermute x24, starting transfers between devices, with_halo(): lax.ppermute(last, axis, up)  83.3 us
    all_to_all x9, starting transfers between devices, from_everyone(): return lax.all_to_all(copies, axis, split_axis=0, concat_axis=0, tiled=True)  73.7 us
    all_to_all x9, waiting for transfers between devices, from_everyone(): return lax.all_to_all(copies, axis, split_axis=0, concat_axis=0, tiled=True)  51 us
    all_to_all x3, blocking collectives, from_everyone(): return lax.all_to_all(copies, axis, split_axis=0, concat_axis=0, tiled=True)  49.6 us
    ppermute x24, starting transfers between devices, with_halo(): lax.ppermute(initial, axis, [(b, a) for a, b in up])  41.3 us
    another operation x6, other arithmetic, precondition(): coarse = jax.scipy.linalg.cho_solve((factor, True), means)  39.5 us
    reshape x3, local copies, waits for them, and re-layouts, pool_sum(): field.reshape(first // 2, 2, second // 2, 2, third // 2, 2)  17.4 us
    broadcast_in_dim x12, local copies, waits for them, and re-layouts, from_everyone(): copies = jnp.broadcast_to(x, (lax.axis_size(axis), *x.shape))  9.5 us
  transfers between devices with their start and end apart: 57, of which 12 were waited for; matrix products, arithmetic and copies ran while one was open for 18% of the time, Pallas kernels for 0%

commit v1 on v0

v1 whole, which is shorter than its diff:
```python
import functools

import jax
import jax.numpy as jnp
from jax import lax
from jax.experimental import pallas as pl
from jax.experimental.pallas import tpu as pltpu
from jax.sharding import PartitionSpec as P

F32 = jnp.float32
OMEGA = 0.8
CX, CY, CZ = 8, 16, 128
CELLS = CX * CY * CZ
H = 8
EX, EY, EZ = CX + 2 * H, CY + 2 * H, 2 * CZ
SLOT = 16
VMEM = pl.BlockSpec(memory_space=pltpu.VMEM)
SMEM = pl.BlockSpec(memory_space=pltpu.SMEM)


def call(kernel, out_shapes, n_in, scratch=(), in_specs=None, name=None):
    outs = [jax.ShapeDtypeStruct(s, F32) for s in out_shapes]
    return pl.pallas_call(
        kernel,
        out_shape=outs,
        in_specs=in_specs or [VMEM] * n_in,
        out_specs=[VMEM] * len(outs),
        scratch_shapes=[pltpu.VMEM(s, F32) for s in scratch],
        compiler_params=pltpu.CompilerParams(vmem_limit_bytes=48 * 1024 * 1024),
        name=name,
    )


def roll(x, shift, axis):
    return pltpu.roll(x, shift % x.shape[axis], axis)


def iota(shape, dim):
    return lax.broadcasted_iota(jnp.int32, shape, dim)


def total(x):
    return jnp.sum(jnp.sum(x, axis=0, keepdims=True), axis=1, keepdims=True)


def pack_kernel(rhs, cond, ext, to_low, to_high, msg):
    lane = iota((CY, CZ), 1)
    a = jnp.zeros((CY, CZ), F32)
    b = jnp.zeros((CY, CZ), F32)
    acc = jnp.zeros((CY, CZ), F32)
    inside = lane < ext[0, 0, 0]
    for x in range(CX):
        k = cond[x]
        r = rhs[x]
        acc = acc + jnp.where(inside, r, 0.0)
        hi = (lane >= 16 * x) & (lane < 16 * x + H)
        start = (16 * x - H) % CZ
        lo = (lane >= start) & (lane < start + H)
        a = jnp.where(hi, roll(k, 16 * x, 1), jnp.where(lo, roll(r, 16 * x - H, 1), a))
        b = jnp.where(lo, roll(k, 16 * x, 1), jnp.where(hi, roll(r, 16 * x + H, 1), b))
    to_low[...] = a
    to_high[...] = b
    mean = total(acc) / CELLS
    at = iota((1, CZ), 1)
    z = lax.axis_index("gz")
    count = jnp.full((1, CZ), ext[0, 0, 0], jnp.int32).astype(F32)
    row = jnp.where(at == z, mean, 0.0) + jnp.where(at == SLOT + z, count, 0.0)
    msg[...] = jnp.broadcast_to(row[None], msg.shape)


def y_kernel(rhs, cond, from_high, from_low, zh, to_low, to_high):
    low_half = iota((CY, CZ), 1) % 16 < H
    a = from_high[...]
    b = from_low[...]
    zk = jnp.where(low_half, a, b)
    zr = jnp.where(low_half, roll(a, H, 1), roll(b, -H, 1))
    zh[0] = zk
    zh[1] = zr
    to_low[0:CX] = cond[:, 0:H, :]
    to_low[CX : 2 * CX] = rhs[:, 0:H, :]
    to_low[2 * CX] = zk[0:H]
    to_low[2 * CX + 1] = zr[0:H]
    to_high[0:CX] = cond[:, CY - H : CY, :]
    to_high[CX : 2 * CX] = rhs[:, CY - H : CY, :]
    to_high[2 * CX] = zk[CY - H : CY]
    to_high[2 * CX + 1] = zr[CY - H : CY]


def x_kernel(rhs, cond, zh, from_high, from_low, slab):
    slab[0:CX, 0:CY] = cond[...]
    slab[CX : 2 * CX, 0:CY] = rhs[...]
    slab[2 * CX : 2 * CX + 2, 0:CY] = zh[...]
    slab[:, CY : CY + H] = from_high[...]
    slab[:, CY + H : EY] = from_low[...]


def spread_kernel(rows, nz, part, msg):
    at = iota((1, CZ), 1)
    s = jnp.sum(part[...], axis=0)
    y = lax.axis_index("gy")
    here = (at >= y * nz) & (at < y * nz + nz)
    out = []
    for i in range(min(rows, 6)):
        moved = pltpu.roll(s, (y * nz + CZ - SLOT * i) % CZ, 1)
        out.append(jnp.where(here, moved, 0.0))
    if rows > 6:
        out.append(jnp.where(at >= 6 * SLOT, s, 0.0))
        out.append(jnp.zeros((1, CZ), F32))
    for i, row in enumerate(out):
        msg[:, i : i + 1, :] = jnp.broadcast_to(row[None], (msg.shape[0], 1, CZ))


def dot(a, b):
    return jnp.dot(a, b, precision=lax.Precision.HIGHEST, preferred_element_type=F32)


def inverse_kernel(factor, out):
    n = factor.shape[0]
    bs = CZ
    nb = n // bs
    i = iota((bs, bs), 0)
    j = iota((bs, bs), 1)
    eye = i == j
    low = [factor[b * bs : (b + 1) * bs, b * bs : (b + 1) * bs].astype(F32) for b in range(nb)]
    inv = []
    for lb in low:
        diag = jnp.where(eye, lb, 0.0)
        col = 1.0 / jnp.sum(diag, axis=1, keepdims=True)
        row = 1.0 / jnp.sum(diag, axis=0, keepdims=True)
        pair = (i // 2 == j // 2) & (i > j)
        inv.append(jnp.where(eye, col, 0.0) - jnp.where(pair, col * lb * row, 0.0))
    s = 2
    while s < bs:
        mask = (i // (2 * s) == j // (2 * s)) & (i // s > j // s)
        mid = [dot(jnp.where(mask, lb, 0.0), x) for lb, x in zip(low, inv)]
        inv = [x - dot(x, m) for x, m in zip(inv, mid)]
        s *= 2
    out[...] = jnp.zeros((n, n), F32)
    for b in range(nb):
        out[b * bs : (b + 1) * bs, b * bs : (b + 1) * bs] = inv[b]
    s = bs
    while s < n:
        for at in range(0, n, 2 * s):
            mid = dot(factor[at + s : at + 2 * s, at : at + s].astype(F32), out[at : at + s, at : at + s])
            out[at + s : at + 2 * s, at : at + s] = -dot(out[at + s : at + 2 * s, at + s : at + 2 * s], mid)
        s *= 2


def coarse_inverse(factor, gx):
    n = factor.shape[0]
    return call(inverse_kernel, [(n, n)], 1, name="inverse")(factor)[0]


def coarse_solve(inv, means):
    nb = len(means)
    bs = CZ
    rows = [jnp.zeros((1, bs), F32) for _ in range(nb)]
    for a in range(nb):
        acc = inv[a * bs : (a + 1) * bs, 0:bs] * means[0]
        for c in range(1, a + 1):
            acc = acc + inv[a * bs : (a + 1) * bs, c * bs : (c + 1) * bs] * means[c]
        u = jnp.sum(acc, axis=1, keepdims=True)
        for c in range(a + 1):
            rows[c] = rows[c] + jnp.sum(inv[a * bs : (a + 1) * bs, c * bs : (c + 1) * bs] * u, axis=0, keepdims=True)
    return rows


def neighbours(rows, nz, ny):
    nx = len(rows)
    x = lax.axis_index("gx")
    y = lax.axis_index("gy")
    z = lax.axis_index("gz")
    zero = jnp.zeros((1, CZ), F32)
    picked = []
    for dx in (-1, 0, 1):
        v = zero
        for r in range(nx):
            v = v + jnp.where(jnp.full((1, CZ), x + dx, jnp.int32) == r, rows[r], 0.0)
        picked.append(v)
    row = iota((8, CZ), 0)
    stack = jnp.where(row == 0, picked[0], jnp.where(row == 1, picked[1], jnp.where(row == 2, picked[2], 0.0)))
    lane = iota((8, CZ), 1)
    out = {}
    for dy in (-1, 0, 1):
        for dz in (-1, 0, 1):
            ok = (y + dy >= 0) & (y + dy < ny) & (z + dz >= 0) & (z + dz < nz)
            target = jnp.where(ok, (y + dy) * nz + z + dz, -1)
            out[dy, dz] = jnp.sum(jnp.where(lane == target, stack, 0.0), axis=1, keepdims=True)
    return out


def planes(low, high, body, unroll=2):
    assert (high - low) % unroll == 0

    def step(i, carry):
        for u in range(unroll):
            body(low + i * unroll + u)
        return carry

    lax.fori_loop(0, (high - low) // unroll, step, 0)


ROW_PARTS = ((0, 0), (8, 0), (16, 1), (24, -1))


def main_kernel(
    nx, ny, nz, left, own, right, gathered, inv,
    d_out, t_out, n_out, an_out, r_out, e0_out, ey_out, ez_out, ex_out, f_out, msg,
    kap, rr, cx, cy, cz, i0, k1, i1, u1, u2, dd, tt, ff, f1, fy,
):
    means, counts = [], []
    for x in range(nx):
        both = jnp.sum(gathered[x * ny : (x + 1) * ny], axis=0)
        means.append(both[0:1])
        counts.append(both[1:2])
    lane8 = iota((8, CZ), 1)
    lane8f = lane8.astype(F32)
    even8f = (lane8 - lane8 % 2).astype(F32)
    valid = (lane8 < H) | (lane8 >= CZ - H)
    ext = neighbours(counts, nz, ny)
    y0 = neighbours(coarse_solve(inv, means), nz, ny)
    for bx in range(3):
        for r, dy in ROW_PARTS:
            e = {dz: jnp.broadcast_to(ext[dy, dz][bx : bx + 1], (8, CZ)) for dz in (-1, 0, 1)}
            v = {dz: jnp.broadcast_to(y0[dy, dz][bx : bx + 1], (8, CZ)) for dz in (-1, 0, 1)}
            far = jnp.where(lane8 < CZ // 2, e[1], e[-1])
            m0 = jnp.where(lane8f < e[0], 1.0, 0.0)
            m1 = jnp.where(valid & (lane8f < far), 1.0, 0.0)
            ff[bx, r : r + 8, 0:CZ] = m0
            ff[bx, r : r + 8, CZ:EZ] = m1
            f1[bx, r : r + 8, 0:CZ] = jnp.where(even8f < e[0], 1.0, 0.0)
            f1[bx, r : r + 8, CZ:EZ] = jnp.where(valid & (even8f < far), 1.0, 0.0)
            fy[bx, r : r + 8, 0:CZ] = m0 * v[0]
            fy[bx, r : r + 8, CZ:EZ] = m1 * jnp.where(lane8 < CZ // 2, v[1], v[-1])
    for bx, src in enumerate((left, own, right)):
        for x in range(CX):
            at = bx * CX + x
            kap[at, :, 0:CZ] = src[x]
            kap[at, :, CZ:EZ] = roll(src[2 * CX], -16 * x, 1)
            rr[at, :, 0:CZ] = src[CX + x] * ff[bx, :, 0:CZ]
            rr[at, :, CZ:EZ] = roll(src[2 * CX + 1], -16 * x, 1) * ff[bx, :, CZ:EZ]
    row_even = iota((EY, EZ), 0) % 2 == 0
    lane_even = iota((EY, EZ), 1) % 2 == 0

    def pooled(s):
        s = s + jnp.where(row_even, roll(s, -1, 0), roll(s, 1, 0))
        return s + jnp.where(lane_even, roll(s, -1, 1), roll(s, 1, 1))

    def coefs(x):
        k = kap[x]
        cx[x] = 0.5 * (k + kap[jnp.minimum(x + 1, EX - 1)])
        cy[x] = 0.5 * (k + roll(k, -1, 0))
        cz[x] = 0.5 * (k + roll(k, -1, 1))

    planes(0, EX, coefs)

    def inverses(x):
        f = ff[x >> 3]
        b, c = cy[x], cz[x]
        s = cx[x] + cx[x - 1] + b + roll(b, 1, 0) + c + roll(c, 1, 1)
        i0[x] = OMEGA * f / (s + 1.0 - f)

    planes(1, EX - 1, inverses)

    def coarse_cond(i):
        k1[i] = pooled(kap[2 * i] + kap[2 * i + 1]) * 0.125

    planes(0, EX // 2, coarse_cond)

    def coarse_inv(i):
        k = k1[i]
        f = f1[i >> 2]
        s = k1[i - 1] + k1[i + 1] + roll(k, 2, 0) + roll(k, -2, 0) + roll(k, 2, 1) + roll(k, -2, 1)
        s = 3.0 * k + 0.5 * s
        i1[i] = OMEGA * f / (4.0 * s + 1.0 - f)

    planes(1, EX // 2 - 1, coarse_inv)

    def image(u, x):
        c = u[x]
        gx = cx[x] * (c - u[x + 1]) - cx[x - 1] * (u[x - 1] - c)
        gy = cy[x] * (c - roll(c, -1, 0))
        gz = cz[x] * (c - roll(c, -1, 1))
        return ff[x >> 3] * (gx + (gy - roll(gy, 1, 0)) + (gz - roll(gz, 1, 1)))

    def smooth(src, first_range, pair_range, out_range, put):
        def first(x):
            u1[x] = i0[x] * src[x]

        planes(*first_range, first)

        def pair(i):
            x = 2 * i
            s = (src[x] - image(u1, x)) + (src[x + 1] - image(u1, x + 1))
            below = ff[x >> 3] * (i1[i] * pooled(s))
            u2[x] = u1[x] + below
            u2[x + 1] = u1[x + 1] + below

        planes(*pair_range, pair, 1)

        def last(x):
            put(x, u2[x] + i0[x] * (src[x] - image(u2, x)))

        planes(*out_range, last)

    def put_d(x, v):
        dd[x] = v + fy[x >> 3]

    smooth(rr, (1, EX - 1), (1, EX // 2 - 1), (3, EX - 3), put_d)

    def put_t(x):
        tt[x] = image(dd, x)

    planes(4, EX - 4, put_t)
    for x in range(CX):
        d_out[x] = dd[H + x, 0:CY, 0:CZ]

    def put_n(x, v):
        dd[x] = v

    zero = jnp.zeros((CY, CZ), F32)
    s_rz, s_dad = zero, zero
    for x in range(CX):
        s_rz = s_rz + rr[H + x, 0:CY, 0:CZ] * d_out[x]
        s_dad = s_dad + tt[H + x, 0:CY, 0:CZ] * d_out[x]
    smooth(tt, (4, EX - 4), (3, EX // 2 - 3), (7, EX - 7), put_n)
    s_x, s_y, s_tau, s_om, s_d, s_cy, s_cz = (zero,) * 7
    f = ff[1]
    row = iota((EY, EZ), 0)
    lane = iota((EY, EZ), 1)
    mine = jnp.where((row < CY) & (lane < CZ), f, 0.0)
    own_f = f[0:CY, 0:CZ]
    row_o = iota((CY, CZ), 0)
    lane_o = iota((CY, CZ), 1)
    f_out[...] = own_f
    f_up_y = roll(f, -1, 0)
    f_up_z = roll(f, -1, 1)
    dif_y = mine - roll(mine, -1, 0)
    dif_z = mine - roll(mine, -1, 1)
    for x in range(CX):
        at = H + x
        an = image(dd, at)[0:CY, 0:CZ]
        n = dd[at, 0:CY, 0:CZ]
        t = tt[at, 0:CY, 0:CZ]
        an_out[x] = an
        n_out[x] = n
        t_out[x] = t
        r_out[x] = rr[at, 0:CY, 0:CZ]
        b, c = cy[at], cz[at]
        gy = b * dif_y
        gz = c * dif_z
        e = ((gy - roll(gy, 1, 0)) + (gz - roll(gz, 1, 1)))[0:CY, 0:CZ]
        if x == 0:
            e = e + cx[H - 1, 0:CY, 0:CZ] * own_f
        if x == CX - 1:
            e = e + cx[at, 0:CY, 0:CZ] * own_f
        e = e * own_f
        e0_out[x] = e
        cut_y = jnp.where(
            row_o == CY - 1, (b * f_up_y)[0:CY, 0:CZ], jnp.where(row_o == 0, roll(b * f, 1, 0)[0:CY, 0:CZ], 0.0)
        ) * own_f
        cut_z = jnp.where(
            lane_o == CZ - 1, (c * f_up_z)[0:CY, 0:CZ], jnp.where(lane_o == 0, roll(c * f, 1, 1)[0:CY, 0:CZ], 0.0)
        ) * own_f
        ey_out[x] = cut_y
        ez_out[x] = cut_z
        s_x = s_x + t * n
        s_y = s_y + n * an
        s_tau = s_tau + t
        s_om = s_om + an
        s_d = s_d + e * own_f
        s_cy = s_cy + cut_y
        s_cz = s_cz + cut_z
    ex0 = cx[H - 1, 0:CY, 0:CZ] * own_f * ff[0, 0:CY, 0:CZ]
    ex1 = cx[H + CX - 1, 0:CY, 0:CZ] * own_f * ff[2, 0:CY, 0:CZ]
    ex_out[0] = ex0
    ex_out[1] = ex1
    at = iota((1, CZ), 1)
    z = lax.axis_index("gz")
    vectors = (
        s_tau, s_om, s_d, ex1,
        jnp.where(row_o == CY - 1, s_cy, 0.0), jnp.where(lane_o == CZ - 1, s_cz, 0.0),
    )
    line = jnp.zeros((1, CZ), F32)
    for i, v in enumerate(vectors):
        line = line + jnp.where(at == SLOT * i + z, total(v), 0.0)
    for i, v in enumerate((s_rz, s_dad, s_x, s_y)):
        line = line + jnp.where(at == 6 * SLOT + i, total(v), 0.0)
    msg[...] = jnp.broadcast_to(line[None], msg.shape)


def final_kernel(nx, ny, nz, gathered, inv, d_in, t_in, n_in, an_in, r_in, e0, ey, ez, ex, f_in, sol, res):
    tables = [jnp.sum(gathered[x * ny : (x + 1) * ny], axis=0) for x in range(nx)]
    sums = tables[0][6:7]
    for t in tables[1:]:
        sums = sums + t[6:7]
    at = iota((1, CZ), 1)

    def scalar(i):
        return jnp.sum(jnp.where(at == 6 * SLOT + i, sums, 0.0), axis=1, keepdims=True)

    rz, dad, xx, yy = (scalar(i) for i in range(4))
    tau = [t[0:1] for t in tables]
    yt = coarse_solve(inv, [v * (1.0 / CELLS) for v in tau])
    add_x = jnp.zeros((1, CZ), F32)
    add_y = jnp.zeros((1, CZ), F32)
    for x in range(nx):
        y = yt[x]
        t = tables[x]
        add_x = add_x + t[0:1] * y
        cross = t[4:5] * roll(y, -nz, 1) + t[5:6] * roll(y, -1, 1)
        if x + 1 < nx:
            cross = cross + t[3:4] * yt[x + 1]
        add_y = add_y + y * (2.0 * t[1:2] + t[2:3] * y - 2.0 * cross)
    xx = xx + jnp.sum(add_x, axis=1, keepdims=True)
    yy = yy + jnp.sum(add_y, axis=1, keepdims=True)
    a0 = rz / dad
    new = a0 * a0 * xx - rz
    beta = new / rz
    zaz = dad - 2.0 * a0 * xx + a0 * a0 * yy
    a1 = new / (zaz - beta * beta * dad)
    near = neighbours(yt, nz, ny)
    shape = (CY, CZ)

    def wide(v, bx=1):
        return jnp.broadcast_to(v[bx : bx + 1], shape)

    y_own = wide(near[0, 0])
    y_y = jnp.where(iota(shape, 0) < CY // 2, wide(near[-1, 0]), wide(near[1, 0]))
    y_z = jnp.where(iota(shape, 1) < CZ // 2, wide(near[0, -1]), wide(near[0, 1]))
    f = f_in[...]
    c_d = jnp.broadcast_to(a0 + a1 * (1.0 + beta), shape)
    c_n = jnp.broadcast_to(a0 * a1, shape)
    for x in range(CX):
        n = n_in[x] + f * y_own
        an = an_in[x] + e0[x] * y_own - ey[x] * y_y - ez[x] * y_z
        if x == 0:
            an = an - ex[0] * wide(near[0, 0], 0)
        if x == CX - 1:
            an = an - ex[1] * wide(near[0, 0], 2)
        sol[x] = c_d * d_in[x] - c_n * n
        res[x] = r_in[x] - c_d * t_in[x] + c_n * an


def exchange(axis, to_low, to_high):
    size = lax.axis_size(axis)
    up = [(i, i + 1) for i in range(size - 1)]
    down = [(b, a) for a, b in up]
    return lax.ppermute(to_low, axis, down), lax.ppermute(to_high, axis, up)


def gathered_rows(msg, rows, nx, ny, nz):
    part = lax.all_to_all(msg, "gz", 0, 0, tiled=True)
    spread = call(functools.partial(spread_kernel, rows, nz), [(nx * ny, rows, CZ)], 1, name="spread")(part)[0]
    return lax.all_to_all(spread, ("gx", "gy"), 0, 0, tiled=True)


def on_device(right_side, conductance, extents, coarse_factor):
    nx, ny, nz = (lax.axis_size(a) for a in ("gx", "gy", "gz"))
    inv = coarse_inverse(coarse_factor, nx)
    to_low, to_high, msg = call(
        pack_kernel, [(CY, CZ), (CY, CZ), (nz, 1, CZ)], 3, in_specs=[VMEM, VMEM, SMEM], name="pack"
    )(right_side, conductance, extents)
    z_high, z_low = exchange("gz", to_low, to_high)
    first = gathered_rows(msg, 2, nx, ny, nz)
    depth = 2 * CX + 2
    zh, to_low, to_high = call(y_kernel, [(2, CY, CZ), (depth, H, CZ), (depth, H, CZ)], 4, name="rows")(
        right_side, conductance, z_high, z_low
    )
    y_high, y_low = exchange("gy", to_low, to_high)
    slab = call(x_kernel, [(depth, EY, CZ)], 5, name="slab")(right_side, conductance, zh, y_high, y_low)[0]
    x_high, x_low = exchange("gx", slab, slab)
    block = (CX, CY, CZ)
    wide = (EX, EY, EZ)
    half = (EX // 2, EY, EZ)
    third = (3, EY, EZ)
    outs = call(
        functools.partial(main_kernel, nx, ny, nz),
        [block] * 8 + [(2, CY, CZ), (CY, CZ), (nz, 1, CZ)],
        5,
        scratch=[wide] * 6 + [half] * 2 + [wide] * 4 + [third] * 3,
        name="fields",
    )(x_low, slab, x_high, first, inv)
    second = gathered_rows(outs[-1], 8, nx, ny, nz)
    sol, res = call(functools.partial(final_kernel, nx, ny, nz), [block] * 2, 12, name="final")(
        second, inv, *outs[:-1]
    )
    return sol, res


def solution(mesh):
    spec = P("gx", "gy", "gz")
    return jax.shard_map(
        on_device, mesh=mesh, in_specs=(spec, spec, spec, P()), out_specs=(spec, spec), check_vma=False
    )
```

time: 435 us -> 104 us (0.24)
  starting transfers between devices: 198 us -> 33 us
  other arithmetic: 60.3 us -> 0 us
  local copies, waits for them, and re-layouts: 54.6 us -> 1.68 us
  waiting for transfers between devices: 56.1 us -> 6.89 us
  Pallas kernels: 0 us -> 18.7 us
  blocking collectives: 49.6 us -> 41.1 us
  between operations: 8.02 us -> 1.39 us
  matrix products: 5.82 us -> 0 us
    ppermute x48 -> x6, starting transfers between devices: 125 us -> 21.4 us  [exchange(): return (lax.ppermute(to_low, axis, down), lax.ppermute(to_high, axis, up))]
    all_to_all x9 -> x1, starting transfers between devices: 73.7 us -> 11.7 us  [gathered_rows(): return lax.all_to_all(spread, ('gx', 'gy'), 0, 0, tiled=True)]
    all_to_all x9 -> x1, waiting for transfers between devices: 51 us -> 4.36 us  [gathered_rows(): return lax.all_to_all(spread, ('gx', 'gy'), 0, 0, tiled=True)]
    another operation x6 -> x0, other arithmetic: 39.5 us -> none  [precondition(): coarse = jax.scipy.linalg.cho_solve((factor, True), means)]
    reshape x5 -> x0, local copies, waits for them, and re-layouts: 25.4 us -> none  [the longest x3 17.4 us: pool_sum(): field.reshape(first // 2, 2, second // 2, 2, third // 2, 2)]
    pallas_call x0 -> x8, Pallas kernels: none -> 18.7 us  [the longest x1 12.2 us: on_device(): call(functools.partial(main_kernel, nx, ny, nz), [block] * 8 + [(2, CY, C...]
    reduce_sum x15 -> x0, other arithmetic: 16.1 us -> none  [the longest x3 7.67 us: pool_sum(): field.reshape(first // 2, 2, second // 2, 2, third // 2, 2)]
    broadcast_in_dim x14 -> x0, local copies, waits for them, and re-layouts: 14.6 us -> none  [the longest x12 9.5 us: from_everyone(): copies = jnp.broadcast_to(x, (lax.axis_size(axis), *x.shape))]
  transfers between devices with their start and end apart: 57 -> 7, of which waited for: 12 -> 4; matrix products, arithmetic and copies ran while one was open for 18% -> 0% of each run, Pallas kernels for 0% -> 5%
where the time goes in v1:
time: 104 us; the launch traced here: 103 us
  blocking collectives  41.1 us (40%)
  starting transfers between devices  33 us (32%)
  Pallas kernels  18.7 us (18%)
  waiting for transfers between devices  6.89 us (7%)
  local copies, waits for them, and re-layouts  1.68 us (2%)
  between operations  1.39 us (1%)
    all_to_all x2, blocking collectives, gathered_rows(): part = lax.all_to_all(msg, 'gz', 0, 0, tiled=True)  28.2 us
    ppermute x6, starting transfers between devices, exchange(): return (lax.ppermute(to_low, axis, down), lax.ppermute(to_high, axis, up))  21.4 us
    all_to_all x1, blocking collectives, gathered_rows(): return lax.all_to_all(spread, ('gx', 'gy'), 0, 0, tiled=True)  13 us
    pallas_call x1, Pallas kernels, on_device(): call(functools.partial(main_kernel, nx, ny, nz), [block] * 8 + [(2, CY, C...  12.2 us
    all_to_all x1, starting transfers between devices, gathered_rows(): return lax.all_to_all(spread, ('gx', 'gy'), 0, 0, tiled=True)  11.7 us
    pallas_call x1, Pallas kernels, coarse_inverse(): return call(inverse_kernel, [(n, n)], 1, name='inverse')(factor)[0]  4.39 us
    all_to_all x1, waiting for transfers between devices, gathered_rows(): return lax.all_to_all(spread, ('gx', 'gy'), 0, 0, tiled=True)  4.36 us
    ppermute x6, waiting for transfers between devices, exchange(): return (lax.ppermute(to_low, axis, down), lax.ppermute(to_high, axis, up))  2.52 us
  transfers between devices with their start and end apart: 7, of which 4 were waited for; matrix products, arithmetic and copies ran while one was open for 0% of the time, Pallas kernels for 5%

profile of v1, /device:TPU:1, one launch (start us, length us, event | category | flops | bytes accessed | tf_op | source)
XLA Modules:
  0.0 102.9 jit_solution(8986711871181286516)
XLA Ops:
  1.3 0.0 copy-start
  1.3 0.8 copy-done
  2.1 0.0 copy-start.1
  2.1 0.8 copy-done.1
  3.0 0.0 copy-start.2
  3.0 0.1 pack.1
  3.1 8.9 %collective-permute-start = (f32[16,128]{1,0:T(8,128)S(1)}, f32[16,128]{1,0:T(8,128)S(1)}, u32[]{:S(2)}, u32[]{:S(2)}) collective-permute-start(f32[16,128]{1,0:T(8,128)S(1)} %get-tuple-element.19), channel_id=1, source_target_pairs={{1,0},{2,1},{3,2},{4,3},{5,4},{6,5},{7,6},{8,7},{9,8},{10,9},{11,1... | collective-permute-start | bytes 24584 | tf_op jit(solution)/shard_map/ppermute | solution.py:449
  12.0 1.9 %collective-permute-start.1 = (f32[16,128]{1,0:T(8,128)S(1)}, f32[16,128]{1,0:T(8,128)S(1)}, u32[]{:S(2)}, u32[]{:S(2)}) collective-permute-start(f32[16,128]{1,0:T(8,128)S(1)} %get-tuple-element.20), channel_id=1, source_target_pairs={{0,1},{1,2},{2,3},{3,4},{4,5},{5,6},{6,7},{7,8},{8,9},{9,10},{10,1... | collective-permute-start | bytes 24584 | tf_op jit(solution)/shard_map/ppermute | solution.py:449
  13.9 0.0 collective-permute-done.from_high
  13.9 1.1 %collective-permute-done.1.from_low = f32[16,128]{1,0:T(8,128)S(1)} collective-permute-done((f32[16,128]{1,0:T(8,128)S(1)}, f32[16,128]{1,0:T(8,128)S(1)}, u32[]{:S(2)}, u32[]{:S(2)}) %collective-permute-start.1) | collective-permute-done | bytes 8224 | tf_op jit(solution)/shard_map/ppermute | solution.py:449
  15.0 0.1 rows.1
  15.1 1.3 %collective-permute-start.2 = (f32[18,8,128]{2,1,0:T(8,128)S(1)}, f32[18,8,128]{2,1,0:T(8,128)S(1)}, u32[]{:S(2)}, u32[]{:S(2)}) collective-permute-start(f32[18,8,128]{2,1,0:T(8,128)S(1)} %get-tuple-element.22), channel_id=1, source_target_pairs={{16,0},{32,16},{48,32},{64,48},{80,64},{96,80},{112,96},{17,1},{33... | collective-permute-start | bytes 221192 | tf_op jit(solution)/shard_map/ppermute | solution.py:449
  16.4 4.0 %collective-permute-start.3 = (f32[18,8,128]{2,1,0:T(8,128)S(1)}, f32[18,8,128]{2,1,0:T(8,128)S(1)}, u32[]{:S(2)}, u32[]{:S(2)}) collective-permute-start(f32[18,8,128]{2,1,0:T(8,128)S(1)} %get-tuple-element.23), channel_id=1, source_target_pairs={{0,16},{16,32},{32,48},{48,64},{64,80},{80,96},{96,112},{1,17},{17... | collective-permute-start | bytes 221192 | tf_op jit(solution)/shard_map/ppermute | solution.py:449
  20.4 0.3 collective-permute-done.2.from_high
  20.7 1.1 %collective-permute-done.3.from_low = f32[18,8,128]{2,1,0:T(8,128)S(1)} collective-permute-done((f32[18,8,128]{2,1,0:T(8,128)S(1)}, f32[18,8,128]{2,1,0:T(8,128)S(1)}, u32[]{:S(2)}, u32[]{:S(2)}) %collective-permute-start.3) | collective-permute-done | bytes 73760 | tf_op jit(solution)/shard_map/ppermute | solution.py:449
  21.8 1.3 %collective-permute-start.5 = (f32[18,32,128]{2,1,0:T(8,128)S(1)}, f32[18,32,128]{2,1,0:T(8,128)S(1)}, u32[]{:S(2)}, u32[]{:S(2)}) collective-permute-start(f32[18,32,128]{2,1,0:T(8,128)S(1)} %slab.1.own), channel_id=1, source_target_pairs={{128,0},{256,128},{384,256},{129,1},{257,129},{385,257},{130,2},{2... | collective-permute-start | bytes 884744 | tf_op jit(solution)/shard_map/ppermute | solution.py:449
  23.1 4.0 %collective-permute-start.4 = (f32[18,32,128]{2,1,0:T(8,128)S(1)}, f32[18,32,128]{2,1,0:T(8,128)S(1)}, u32[]{:S(2)}, u32[]{:S(2)}) collective-permute-start(f32[18,32,128]{2,1,0:T(8,128)S(1)} %slab.1.own), channel_id=1, source_target_pairs={{0,128},{128,256},{256,384},{1,129},{129,257},{257,385},{2,130},{1... | collective-permute-start | bytes 884744 | tf_op jit(solution)/shard_map/ppermute | solution.py:449
  27.1 16.6 %all_to_all.20.part = f32[16,1,128]{2,1,0:T(1,128)S(1)} all-to-all(f32[16,1,128]{2,1,0:T(1,128)S(1)} %get-tuple-element.24), channel_id=1, replica_groups=mesh['gx'=4,'gy'=8,'gz'=16] {'gz'}, dimensions={0} | all-to-all | bytes 16384 | tf_op jit(solution)/shard_map/all_to_all | solution.py:453
  43.7 0.7 spread.2
  44.5 11.7 %all-to-all-start.1 = ((f32[32,2,128]{2,1,0:T(2,128)}), f32[32,2,128]{2,1,0:T(2,128)S(1)}, u32[]{:S(2)}, u32[]{:S(2)}) async-start(f32[32,2,128]{2,1,0:T(2,128)} %spread.2), calls=%async_computation.1 | async-start | bytes 65536 | tf_op jit(solution)/shard_map/all_to_all | solution.py:455
  56.1 0.0 copy-done.2
  56.1 4.4 %inverse.1.inv = f32[512,512]{1,0:T(8,128)S(1)} custom-call(bf16[512,512]{1,0:T(8,128)(2,1)S(1)} %copy-done.2), custom_call_target="tpu_custom_call" | custom-call | tf_op jit(solution)/shard_map/inverse/pallas_call | solution.py:151
  60.5 4.4 %all-to-all-done.1.gathered = f32[32,2,128]{2,1,0:T(2,128)S(1)} async-done(((f32[32,2,128]{2,1,0:T(2,128)}), f32[32,2,128]{2,1,0:T(2,128)S(1)}, u32[]{:S(2)}, u32[]{:S(2)}) %all-to-all-start.1) | async-done | bytes 32800 | tf_op jit(solution)/shard_map/all_to_all | solution.py:455
  64.9 0.0 collective-permute-done.5.right
  64.9 0.0 collective-permute-done.4.left
  64.9 12.2 %fields.1 = (f32[8,16,128]{2,1,0:T(8,128)S(1)}, f32[8,16,128]{2,1,0:T(8,128)S(1)}, f32[8,16,128]{2,1,0:T(8,128)S(1)}, f32[8,16,128]{2,1,0:T(8,128)S(1)}, f32[8,1...) custom-call(f32[18,32,128]{2,1,0:T(8,128)S(1)} %collective-permute-d, ...), custom_call_target="tpu_custom_call" | custom-call | tf_op jit(solution)/shard_map/fields/pallas_call | solution.py:477
  77.1 11.6 %all_to_all.21.part = f32[16,1,128]{2,1,0:T(1,128)S(1)} all-to-all(f32[16,1,128]{2,1,0:T(1,128)S(1)} %get-tuple-element.25), channel_id=1, replica_groups=mesh['gx'=4,'gy'=8,'gz'=16] {'gz'}, dimensions={0} | all-to-all | bytes 16384 | tf_op jit(solution)/shard_map/all_to_all | solution.py:453
  88.7 0.1 spread.3
  88.8 13.0 %all_to_all.22.gathered = f32[32,8,128]{2,1,0:T(8,128)S(1)} all-to-all(f32[32,8,128]{2,1,0:T(8,128)S(1)} %spread.3), channel_id=1, replica_groups=mesh['gx'=4,'gy'=8,'gz'=16] {'gx','gy'}, dimensions={0} | all-to-all | bytes 262144 | tf_op jit(solution)/shard_map/all_to_all | solution.py:455
  101.8 1.0 %final.1 = (f32[8,16,128]{2,1,0:T(8,128)}, f32[8,16,128]{2,1,0:T(8,128)}) custom-call(f32[32,8,128]{2,1,0:T(8,128)S(1)} %all_to_all.22.gathered, f32[512,512]{1,0:T(8,128)S(1)} %inverse.1.inv, f32[8,16,128]{2,1,0:T(8,128)S(1)} %get-tuple-element.26.d_in, f32[8,16,128]{2,1,0:T(8,128)S(1)} %get-tuple-element.27.t_in, ...), custom_call_target="tpu_custom_call" | custom-call | tf_op jit(solution)/shard_map/final/pallas_call | solution.py:485
  (1 shorter events, 0.0 us)
Async XLA Ops:
  1.3 0.8 copy-start
  2.1 0.8 copy-start.1
  3.0 53.2 %copy-start.2 = (bf16[512,512]{1,0:T(8,128)(2,1)S(1)}, bf16[512,512]{1,0:T(8,128)(2,1)}, u32[]{:S(2)}) copy-start(bf16[512,512]{1,0:T(8,128)(2,1)} %factor.1) | copy-start | bytes 1572868
  3.1 10.8 %collective-permute-start = (f32[16,128]{1,0:T(8,128)S(1)}, f32[16,128]{1,0:T(8,128)S(1)}, u32[]{:S(2)}, u32[]{:S(2)}) collective-permute-start(f32[16,128]{1,0:T(8,128)S(1)} %get-tuple-element.19), channel_id=1, source_target_pairs={{1,0},{2,1},{3,2},{4,3},{5,4},{6,5},{7,6},{8,7},{9,8},{10,9},{11,1... | collective-permute-start | bytes 24584 | tf_op jit(solution)/shard_map/ppermute | solution.py:449
  12.0 3.1 %collective-permute-start.1 = (f32[16,128]{1,0:T(8,128)S(1)}, f32[16,128]{1,0:T(8,128)S(1)}, u32[]{:S(2)}, u32[]{:S(2)}) collective-permute-start(f32[16,128]{1,0:T(8,128)S(1)} %get-tuple-element.20), channel_id=1, source_target_pairs={{0,1},{1,2},{2,3},{3,4},{4,5},{5,6},{6,7},{7,8},{8,9},{9,10},{10,1... | collective-permute-start | bytes 24584 | tf_op jit(solution)/shard_map/ppermute | solution.py:449
  15.1 5.5 %collective-permute-start.2 = (f32[18,8,128]{2,1,0:T(8,128)S(1)}, f32[18,8,128]{2,1,0:T(8,128)S(1)}, u32[]{:S(2)}, u32[]{:S(2)}) collective-permute-start(f32[18,8,128]{2,1,0:T(8,128)S(1)} %get-tuple-element.22), channel_id=1, source_target_pairs={{16,0},{32,16},{48,32},{64,48},{80,64},{96,80},{112,96},{17,1},{33... | collective-permute-start | bytes 221192 | tf_op jit(solution)/shard_map/ppermute | solution.py:449
  16.4 5.4 %collective-permute-start.3 = (f32[18,8,128]{2,1,0:T(8,128)S(1)}, f32[18,8,128]{2,1,0:T(8,128)S(1)}, u32[]{:S(2)}, u32[]{:S(2)}) collective-permute-start(f32[18,8,128]{2,1,0:T(8,128)S(1)} %get-tuple-element.23), channel_id=1, source_target_pairs={{0,16},{16,32},{32,48},{48,64},{64,80},{80,96},{96,112},{1,17},{17... | collective-permute-start | bytes 221192 | tf_op jit(solution)/shard_map/ppermute | solution.py:449
  21.8 43.1 %collective-permute-start.5 = (f32[18,32,128]{2,1,0:T(8,128)S(1)}, f32[18,32,128]{2,1,0:T(8,128)S(1)}, u32[]{:S(2)}, u32[]{:S(2)}) collective-permute-start(f32[18,32,128]{2,1,0:T(8,128)S(1)} %slab.1.own), channel_id=1, source_target_pairs={{128,0},{256,128},{384,256},{129,1},{257,129},{385,257},{130,2},{2... | collective-permute-start | bytes 884744 | tf_op jit(solution)/shard_map/ppermute | solution.py:449
  23.1 41.8 %collective-permute-start.4 = (f32[18,32,128]{2,1,0:T(8,128)S(1)}, f32[18,32,128]{2,1,0:T(8,128)S(1)}, u32[]{:S(2)}, u32[]{:S(2)}) collective-permute-start(f32[18,32,128]{2,1,0:T(8,128)S(1)} %slab.1.own), channel_id=1, source_target_pairs={{0,128},{128,256},{256,384},{1,129},{129,257},{257,385},{2,130},{1... | collective-permute-start | bytes 884744 | tf_op jit(solution)/shard_map/ppermute | solution.py:449
  44.5 20.5 %all-to-all-start.1 = ((f32[32,2,128]{2,1,0:T(2,128)}), f32[32,2,128]{2,1,0:T(2,128)S(1)}, u32[]{:S(2)}, u32[]{:S(2)}) async-start(f32[32,2,128]{2,1,0:T(2,128)} %spread.2), calls=%async_computation.1 | async-start | bytes 65536 | tf_op jit(solution)/shard_map/all_to_all | solution.py:455

commit v2 on v1

--- a/solution.py
+++ b/solution.py
@@ -43,78 +43,97 @@
     return jnp.sum(jnp.sum(x, axis=0, keepdims=True), axis=1, keepdims=True)
 
 
-def pack_kernel(rhs, cond, ext, to_low, to_high, msg):
+def pack_kernel(ext, rhs, cond, own, msg, sems):
+    copies = [
+        pltpu.make_async_copy(cond, own.at[0:CX], sems.at[0]),
+        pltpu.make_async_copy(rhs, own.at[CX : 2 * CX], sems.at[1]),
+    ]
+    for c in copies:
+        c.start()
+    nz = msg.shape[0]
     lane = iota((CY, CZ), 1)
+    row = iota((CY, CZ), 0)
     a = jnp.zeros((CY, CZ), F32)
     b = jnp.zeros((CY, CZ), F32)
     acc = jnp.zeros((CY, CZ), F32)
     inside = lane < ext[0, 0, 0]
+    count = jnp.full((CY, CZ), ext[0, 0, 0], jnp.int32).astype(F32)
+    z = lax.axis_index("gz")
+    for c in copies:
+        c.wait()
     for x in range(CX):
-        k = cond[x]
-        r = rhs[x]
+        k = own[x]
+        r = own[CX + x]
         acc = acc + jnp.where(inside, r, 0.0)
         hi = (lane >= 16 * x) & (lane < 16 * x + H)
         start = (16 * x - H) % CZ
         lo = (lane >= start) & (lane < start + H)
         a = jnp.where(hi, roll(k, 16 * x, 1), jnp.where(lo, roll(r, 16 * x - H, 1), a))
         b = jnp.where(lo, roll(k, 16 * x, 1), jnp.where(hi, roll(r, 16 * x + H, 1), b))
-    to_low[...] = a
-    to_high[...] = b
-    mean = total(acc) / CELLS
-    at = iota((1, CZ), 1)
+    info = jnp.where(row == 0, total(acc) / CELLS, count)
+    a = jnp.where((lane == CZ - 1) & (row < 2), info, a)
+    b = jnp.where((lane == 0) & (row < 2), info, b)
+    for i in range(nz):
+        msg[i] = b
+
+    @pl.when(z > 0)
+    def _():
+        msg[z - 1] = a
+
+
+def rows_kernel(own, got, zh, to_low, to_high, line):
+    nz = got.shape[0]
     z = lax.axis_index("gz")
-    count = jnp.full((1, CZ), ext[0, 0, 0], jnp.int32).astype(F32)
-    row = jnp.where(at == z, mean, 0.0) + jnp.where(at == SLOT + z, count, 0.0)
-    msg[...] = jnp.broadcast_to(row[None], msg.shape)
-
-
-def y_kernel(rhs, cond, from_high, from_low, zh, to_low, to_high):
     low_half = iota((CY, CZ), 1) % 16 < H
-    a = from_high[...]
-    b = from_low[...]
+    up = jnp.minimum(z + 1, nz - 1)
+    a = jnp.where(jnp.full((CY, CZ), z, jnp.int32) < nz - 1, got[up], 0.0)
+    b = jnp.where(jnp.full((CY, CZ), z, jnp.int32) > 0, got[jnp.maximum(z - 1, 0)], 0.0)
+    lane = iota((8, CZ), 1)
+    info = jnp.zeros((8, CZ), F32)
+    for i in range(nz):
+        v = got[i, 0:8]
+        info = jnp.where(lane == i, roll(v, i, 1), info)
+    info = jnp.where(lane == z + 1, pltpu.roll(a[0:8], z + 2, 1), info)
+    info = jnp.where(lane < nz, info, 0.0)
+    line[...] = jnp.broadcast_to((info[0:1] + roll(info[1:2], SLOT, 1))[None], line.shape)
     zk = jnp.where(low_half, a, b)
     zr = jnp.where(low_half, roll(a, H, 1), roll(b, -H, 1))
     zh[0] = zk
     zh[1] = zr
-    to_low[0:CX] = cond[:, 0:H, :]
-    to_low[CX : 2 * CX] = rhs[:, 0:H, :]
+    to_low[0 : 2 * CX] = own[:, 0:H, :]
     to_low[2 * CX] = zk[0:H]
     to_low[2 * CX + 1] = zr[0:H]
-    to_high[0:CX] = cond[:, CY - H : CY, :]
-    to_high[CX : 2 * CX] = rhs[:, CY - H : CY, :]
+    to_high[0 : 2 * CX] = own[:, CY - H : CY, :]
     to_high[2 * CX] = zk[CY - H : CY]
     to_high[2 * CX + 1] = zr[CY - H : CY]
 
 
-def x_kernel(rhs, cond, zh, from_high, from_low, slab):
-    slab[0:CX, 0:CY] = cond[...]
-    slab[CX : 2 * CX, 0:CY] = rhs[...]
+def slab_kernel(own, zh, from_high, from_low, after, slab):
+    slab[0 : 2 * CX, 0:CY] = own[...]
     slab[2 * CX : 2 * CX + 2, 0:CY] = zh[...]
     slab[:, CY : CY + H] = from_high[...]
     slab[:, CY + H : EY] = from_low[...]
 
 
-def spread_kernel(rows, nz, part, msg):
-    at = iota((1, CZ), 1)
-    s = jnp.sum(part[...], axis=0)
-    y = lax.axis_index("gy")
-    here = (at >= y * nz) & (at < y * nz + nz)
+def sum_kernel(part, line):
+    line[...] = jnp.broadcast_to(jnp.sum(part[...], axis=0, keepdims=True), line.shape)
+
+
+def table(rows, i, nx, ny, nz):
     out = []
-    for i in range(min(rows, 6)):
-        moved = pltpu.roll(s, (y * nz + CZ - SLOT * i) % CZ, 1)
-        out.append(jnp.where(here, moved, 0.0))
-    if rows > 6:
-        out.append(jnp.where(at >= 6 * SLOT, s, 0.0))
-        out.append(jnp.zeros((1, CZ), F32))
-    for i, row in enumerate(out):
-        msg[:, i : i + 1, :] = jnp.broadcast_to(row[None], (msg.shape[0], 1, CZ))
+    for x in range(nx):
+        v = rows[x * ny : (x + 1) * ny].reshape(ny, CZ)
+        v = jnp.where(iota((ny, CZ), 1) < nz, roll(v, -SLOT * i, 1), 0.0)
+        v = pltpu.roll(v, 0, 1, stride=nz, stride_axis=0)
+        out.append(jnp.sum(v, axis=0, keepdims=True))
+    return out
 
 
 def dot(a, b):
     return jnp.dot(a, b, precision=lax.Precision.HIGHEST, preferred_element_type=F32)
 
 
-def inverse_kernel(factor, out):
+def diagonal_kernel(factor, out):
     n = factor.shape[0]
     bs = CZ
     nb = n // bs
@@ -135,20 +154,28 @@
         mid = [dot(jnp.where(mask, lb, 0.0), x) for lb, x in zip(low, inv)]
         inv = [x - dot(x, m) for x, m in zip(inv, mid)]
         s *= 2
-    out[...] = jnp.zeros((n, n), F32)
     for b in range(nb):
-        out[b * bs : (b + 1) * bs, b * bs : (b + 1) * bs] = inv[b]
+        out[b] = inv[b]
+
+
+def inverse_of(factor, diagonal, out):
+    n = factor.shape[0]
+    bs = CZ
+    for b in range(n // bs):
+        out[b * bs : (b + 1) * bs, b * bs : (b + 1) * bs] = diagonal[b]
     s = bs
     while s < n:
         for at in range(0, n, 2 * s):
+            for lo in range(s, 2 * s, bs):
+                for hi in range(lo - s + bs, s, bs):
+                    out[at + lo - s : at + lo - s + bs, at + hi : at + hi + bs] = jnp.zeros((bs, bs), F32)
+            if s > bs:
+                for lo in range(s, 2 * s, bs):
+                    for hi in range(lo + bs, 2 * s, bs):
+                        out[at + lo : at + lo + bs, at + hi : at + hi + bs] = jnp.zeros((bs, bs), F32)
             mid = dot(factor[at + s : at + 2 * s, at : at + s].astype(F32), out[at : at + s, at : at + s])
             out[at + s : at + 2 * s, at : at + s] = -dot(out[at + s : at + 2 * s, at + s : at + 2 * s], mid)
         s *= 2
-
-
-def coarse_inverse(factor, gx):
-    n = factor.shape[0]
-    return call(inverse_kernel, [(n, n)], 1, name="inverse")(factor)[0]
 
 
 def coarse_solve(inv, means):
@@ -189,8 +216,8 @@
     return out
 
 
-def planes(low, high, body, unroll=2):
-    assert (high - low) % unroll == 0
+def planes(low, high, body, most=4):
+    unroll = next(u for u in (most, 5, 4, 3, 2, 1) if (high - low) % u == 0)
 
     def step(i, carry):
         for u in range(unroll):
@@ -203,22 +230,14 @@
 ROW_PARTS = ((0, 0), (8, 0), (16, 1), (24, -1))
 
 
-def main_kernel(
-    nx, ny, nz, left, own, right, gathered, inv,
-    d_out, t_out, n_out, an_out, r_out, e0_out, ey_out, ez_out, ex_out, f_out, msg,
-    kap, rr, cx, cy, cz, i0, k1, i1, u1, u2, dd, tt, ff, f1, fy,
-):
-    means, counts = [], []
-    for x in range(nx):
-        both = jnp.sum(gathered[x * ny : (x + 1) * ny], axis=0)
-        means.append(both[0:1])
-        counts.append(both[1:2])
+def coarse_kernel(nx, ny, nz, factor, diagonal, gathered, after, inv, ff, f1, fy):
+    inverse_of(factor, diagonal, inv)
     lane8 = iota((8, CZ), 1)
     lane8f = lane8.astype(F32)
     even8f = (lane8 - lane8 % 2).astype(F32)
     valid = (lane8 < H) | (lane8 >= CZ - H)
-    ext = neighbours(counts, nz, ny)
-    y0 = neighbours(coarse_solve(inv, means), nz, ny)
+    ext = neighbours(table(gathered, 1, nx, ny, nz), nz, ny)
+    y0 = neighbours(coarse_solve(inv, table(gathered, 0, nx, ny, nz)), nz, ny)
     for bx in range(3):
         for r, dy in ROW_PARTS:
             e = {dz: jnp.broadcast_to(ext[dy, dz][bx : bx + 1], (8, CZ)) for dz in (-1, 0, 1)}
@@ -232,6 +251,13 @@
             f1[bx, r : r + 8, CZ:EZ] = jnp.where(valid & (even8f < far), 1.0, 0.0)
             fy[bx, r : r + 8, 0:CZ] = m0 * v[0]
             fy[bx, r : r + 8, CZ:EZ] = m1 * jnp.where(lane8 < CZ // 2, v[1], v[-1])
+
+
+def main_kernel(
+    left, own, right, ff, f1, fy,
+    d_out, t_out, n_out, an_out, r_out, e0_out, ey_out, ez_out, ex_out, f_out, msg,
+    kap, rr, cx, cy, cz, i0, k1, i1, u1, u2, dd, tt,
+):
     for bx, src in enumerate((left, own, right)):
         for x in range(CX):
             at = bx * CX + x
@@ -296,7 +322,7 @@
             u2[x] = u1[x] + below
             u2[x + 1] = u1[x + 1] + below
 
-        planes(*pair_range, pair, 1)
+        planes(*pair_range, pair, 2)
 
         def last(x):
             put(x, u2[x] + i0[x] * (src[x] - image(u2, x)))
@@ -390,28 +416,27 @@
 
 
 def final_kernel(nx, ny, nz, gathered, inv, d_in, t_in, n_in, an_in, r_in, e0, ey, ez, ex, f_in, sol, res):
-    tables = [jnp.sum(gathered[x * ny : (x + 1) * ny], axis=0) for x in range(nx)]
-    sums = tables[0][6:7]
-    for t in tables[1:]:
-        sums = sums + t[6:7]
+    vectors = [table(gathered, i, nx, ny, nz) for i in range(6)]
+    tables = list(zip(*vectors))
+    sums = jnp.sum(gathered[...], axis=0)
     at = iota((1, CZ), 1)
 
     def scalar(i):
         return jnp.sum(jnp.where(at == 6 * SLOT + i, sums, 0.0), axis=1, keepdims=True)
 
     rz, dad, xx, yy = (scalar(i) for i in range(4))
-    tau = [t[0:1] for t in tables]
+    tau = vectors[0]
     yt = coarse_solve(inv, [v * (1.0 / CELLS) for v in tau])
     add_x = jnp.zeros((1, CZ), F32)
     add_y = jnp.zeros((1, CZ), F32)
     for x in range(nx):
         y = yt[x]
         t = tables[x]
-        add_x = add_x + t[0:1] * y
-        cross = t[4:5] * roll(y, -nz, 1) + t[5:6] * roll(y, -1, 1)
+        add_x = add_x + t[0] * y
+        cross = t[4] * roll(y, -nz, 1) + t[5] * roll(y, -1, 1)
         if x + 1 < nx:
-            cross = cross + t[3:4] * yt[x + 1]
-        add_y = add_y + y * (2.0 * t[1:2] + t[2:3] * y - 2.0 * cross)
+            cross = cross + t[3] * yt[x + 1]
+        add_y = add_y + y * (2.0 * t[1] + t[2] * y - 2.0 * cross)
     xx = xx + jnp.sum(add_x, axis=1, keepdims=True)
     yy = yy + jnp.sum(add_y, axis=1, keepdims=True)
     a0 = rz / dad
@@ -449,40 +474,52 @@
     return lax.ppermute(to_low, axis, down), lax.ppermute(to_high, axis, up)
 
 
-def gathered_rows(msg, rows, nx, ny, nz):
-    part = lax.all_to_all(msg, "gz", 0, 0, tiled=True)
-    spread = call(functools.partial(spread_kernel, rows, nz), [(nx * ny, rows, CZ)], 1, name="spread")(part)[0]
-    return lax.all_to_all(spread, ("gx", "gy"), 0, 0, tiled=True)
-
-
 def on_device(right_side, conductance, extents, coarse_factor):
     nx, ny, nz = (lax.axis_size(a) for a in ("gx", "gy", "gz"))
-    inv = coarse_inverse(coarse_factor, nx)
-    to_low, to_high, msg = call(
-        pack_kernel, [(CY, CZ), (CY, CZ), (nz, 1, CZ)], 3, in_specs=[VMEM, VMEM, SMEM], name="pack"
-    )(right_side, conductance, extents)
-    z_high, z_low = exchange("gz", to_low, to_high)
-    first = gathered_rows(msg, 2, nx, ny, nz)
+    sizes = (nx, ny, nz)
+    any_space = pl.BlockSpec(memory_space=pl.ANY)
+    own, msg = pl.pallas_call(
+        pack_kernel,
+        out_shape=[jax.ShapeDtypeStruct(s, F32) for s in ((2 * CX, CY, CZ), (nz, CY, CZ))],
+        in_specs=[SMEM, pl.BlockSpec(memory_space=pltpu.HBM), pl.BlockSpec(memory_space=pltpu.HBM)],
+        out_specs=[VMEM, VMEM],
+        scratch_shapes=[pltpu.SemaphoreType.DMA((2,))],
+        compiler_params=pltpu.CompilerParams(vmem_limit_bytes=8 * 1024 * 1024),
+        name="pack",
+    )(extents, right_side, conductance)
+    got = lax.all_to_all(msg, "gz", 0, 0, tiled=True)
     depth = 2 * CX + 2
-    zh, to_low, to_high = call(y_kernel, [(2, CY, CZ), (depth, H, CZ), (depth, H, CZ)], 4, name="rows")(
-        right_side, conductance, z_high, z_low
-    )
+    zh, to_low, to_high, line = call(
+        rows_kernel, [(2, CY, CZ), (depth, H, CZ), (depth, H, CZ), (nx * ny, 1, CZ)], 2, name="rows"
+    )(own, got)
+    first = lax.all_to_all(line, ("gx", "gy"), 0, 0, tiled=True)
+    to_low, to_high, factor, first = lax.optimization_barrier((to_low, to_high, coarse_factor, first))
     y_high, y_low = exchange("gy", to_low, to_high)
-    slab = call(x_kernel, [(depth, EY, CZ)], 5, name="slab")(right_side, conductance, zh, y_high, y_low)[0]
+    nb = factor.shape[0] // CZ
+    diagonal = call(diagonal_kernel, [(nb, CZ, CZ)], 1, name="diagonal")(factor)[0]
+    slab = call(
+        slab_kernel, [(depth, EY, CZ)], 5, in_specs=[VMEM] * 4 + [any_space], name="slab"
+    )(own, zh, y_high, y_low, diagonal)[0]
     x_high, x_low = exchange("gx", slab, slab)
     block = (CX, CY, CZ)
     wide = (EX, EY, EZ)
     half = (EX // 2, EY, EZ)
     third = (3, EY, EZ)
+    inv, ff, f1, fy = call(
+        functools.partial(coarse_kernel, *sizes), [factor.shape] + [third] * 3, 4,
+        in_specs=[VMEM] * 3 + [any_space], name="coarse",
+    )(factor, diagonal, first, slab)
     outs = call(
-        functools.partial(main_kernel, nx, ny, nz),
+        main_kernel,
         [block] * 8 + [(2, CY, CZ), (CY, CZ), (nz, 1, CZ)],
-        5,
-        scratch=[wide] * 6 + [half] * 2 + [wide] * 4 + [third] * 3,
+        6,
+        scratch=[wide] * 6 + [half] * 2 + [wide] * 4,
         name="fields",
-    )(x_low, slab, x_high, first, inv)
-    second = gathered_rows(outs[-1], 8, nx, ny, nz)
-    sol, res = call(functools.partial(final_kernel, nx, ny, nz), [block] * 2, 12, name="final")(
+    )(x_low, slab, x_high, ff, f1, fy)
+    part = lax.all_to_all(outs[-1], "gz", 0, 0, tiled=True)
+    line = call(sum_kernel, [(nx * ny, 1, CZ)], 1, name="sum")(part)[0]
+    second = lax.all_to_all(line, ("gx", "gy"), 0, 0, tiled=True)
+    sol, res = call(functools.partial(final_kernel, *sizes), [block] * 2, 12, name="final")(
         second, inv, *outs[:-1]
     )
     return sol, res

time: 104 us -> 97.8 us (0.940)
  blocking collectives: 41.1 us -> 66.8 us
  starting transfers between devices: 33 us -> 10.6 us
  waiting for transfers between devices: 6.89 us -> 2.5 us
  Pallas kernels: 18.7 us -> 14.4 us
    all_to_all x3 -> x4, blocking collectives: 41.1 us -> 66.8 us  [the longest x1 20.5 us: on_device(): got = lax.all_to_all(msg, 'gz', 0, 0, tiled=True)]
    all_to_all x1 -> x0, starting transfers between devices: 11.7 us -> none  [gathered_rows(): return lax.all_to_all(spread, ('gx', 'gy'), 0, 0, tiled=True)]
    ppermute x6 -> x4, starting transfers between devices: 21.4 us -> 10.6 us  [exchange(): return (lax.ppermute(to_low, axis, down), lax.ppermute(to_high, axis, up))]
    pallas_call x8, Pallas kernels: 18.7 us -> 14.4 us  [the longest x1 7.75 us: on_device(): call(main_kernel, [block] * 8 + [(2, CY, CZ), (CY, CZ), (nz, 1, CZ)], 6,...]
    all_to_all x1 -> x0, waiting for transfers between devices: 4.36 us -> none  [gathered_rows(): return lax.all_to_all(spread, ('gx', 'gy'), 0, 0, tiled=True)]
    ppermute x6 -> x4, waiting for transfers between devices: 2.52 us -> 2.5 us  [exchange(): return (lax.ppermute(to_low, axis, down), lax.ppermute(to_high, axis, up))]
  transfers between devices with their start and end apart: 7 -> 4, of which waited for: 4 -> 2; matrix products, arithmetic and copies ran while one was open for 0% -> 0% of each run, Pallas kernels for 5% -> 5%
where the time goes in v2:
time: 97.8 us; the launch traced here: 97.4 us
  blocking collectives  66.8 us (68%)
  Pallas kernels  14.4 us (15%)
  starting transfers between devices  10.6 us (11%)
  waiting for transfers between devices  2.5 us (3%)
  local copies, waits for them, and re-layouts  1.68 us (2%)
  between operations  1.45 us (1%)
    all_to_all x1, blocking collectives, on_device(): got = lax.all_to_all(msg, 'gz', 0, 0, tiled=True)  20.5 us
    all_to_all x1, blocking collectives, on_device(): first = lax.all_to_all(line, ('gx', 'gy'), 0, 0, tiled=True)  18.1 us
    all_to_all x1, blocking collectives, on_device(): second = lax.all_to_all(line, ('gx', 'gy'), 0, 0, tiled=True)  15.7 us
    all_to_all x1, blocking collectives, on_device(): part = lax.all_to_all(outs[-1], 'gz', 0, 0, tiled=True)  12.5 us
    ppermute x4, starting transfers between devices, exchange(): return (lax.ppermute(to_low, axis, down), lax.ppermute(to_high, axis, up))  10.6 us
    pallas_call x1, Pallas kernels, on_device(): call(main_kernel, [block] * 8 + [(2, CY, CZ), (CY, CZ), (nz, 1, CZ)], 6,...  7.75 us
    pallas_call x1, Pallas kernels, on_device(): call(diagonal_kernel, [(nb, CZ, CZ)], 1, name='diagonal')(factor)[0]  3.31 us
    ppermute x4, waiting for transfers between devices, exchange(): return (lax.ppermute(to_low, axis, down), lax.ppermute(to_high, axis, up))  2.5 us
  transfers between devices with their start and end apart: 4, of which 2 were waited for; matrix products, arithmetic and copies ran while one was open for 0% of the time, Pallas kernels for 5%

profile of v2, /device:TPU:1, one launch (start us, length us, event | category | flops | bytes accessed | tf_op | source)
XLA Modules:
  0.0 97.4 jit_solution(8263268924903051121)
XLA Ops:
  0.6 0.0 copy-start
  1.3 0.0 copy-start.1
  1.4 0.8 copy-done.1
  2.2 0.0 copy-start.2
  2.2 0.8 copy-done.2
  3.0 0.3 pack.1
  3.3 20.5 %all_to_all.20.got = f32[16,16,128]{2,1,0:T(8,128)S(1)} all-to-all(f32[16,16,128]{2,1,0:T(8,128)S(1)} %get-tuple-element.28), channel_id=1, replica_groups=mesh['gx'=4,'gy'=8,'gz'=16] {'gz'}, dimensions={0} | all-to-all | bytes 262144 | tf_op jit(solution)/shard_map/all_to_all | solution.py:490
  23.8 0.2 rows.1
  24.0 18.1 %all_to_all.21.gathered = f32[32,1,128]{2,1,0:T(1,128)S(1)} all-to-all(f32[32,1,128]{2,1,0:T(1,128)S(1)} %get-tuple-element.32), channel_id=1, replica_groups=mesh['gx'=4,'gy'=8,'gz'=16] {'gx','gy'}, dimensions={0} | all-to-all | bytes 32768 | tf_op jit(solution)/shard_map/all_to_all | solution.py:495
  42.1 1.3 %collective-permute-start = (f32[18,8,128]{2,1,0:T(8,128)S(1)}, f32[18,8,128]{2,1,0:T(8,128)S(1)}, u32[]{:S(2)}, u32[]{:S(2)}) collective-permute-start(f32[18,8,128]{2,1,0:T(8,128)S(1)} %get-tuple-element.33), channel_id=1, source_target_pairs={{16,0},{32,16},{48,32},{64,48},{80,64},{96,80},{112,96},{17,1},{33... | collective-permute-start | bytes 221192 | tf_op jit(solution)/shard_map/ppermute | solution.py:474
  43.4 4.0 %collective-permute-start.1 = (f32[18,8,128]{2,1,0:T(8,128)S(1)}, f32[18,8,128]{2,1,0:T(8,128)S(1)}, u32[]{:S(2)}, u32[]{:S(2)}) collective-permute-start(f32[18,8,128]{2,1,0:T(8,128)S(1)} %get-tuple-element.34), channel_id=1, source_target_pairs={{0,16},{16,32},{32,48},{48,64},{64,80},{80,96},{96,112},{1,17},{17... | collective-permute-start | bytes 221192 | tf_op jit(solution)/shard_map/ppermute | solution.py:474
  47.4 0.0 copy-done
  47.4 3.3 %diagonal.1.after = f32[4,128,128]{2,1,0:T(8,128)S(1)} custom-call(bf16[512,512]{1,0:T(8,128)(2,1)S(1)} %copy-done), custom_call_target="tpu_custom_call" | custom-call | tf_op jit(solution)/shard_map/diagonal/pallas_call | solution.py:499
  50.8 0.0 collective-permute-done.from_high
  50.8 0.0 collective-permute-done.1.from_low
  50.8 1.3 %collective-permute-start.3 = (f32[18,32,128]{2,1,0:T(8,128)S(1)}, f32[18,32,128]{2,1,0:T(8,128)S(1)}, u32[]{:S(2)}, u32[]{:S(2)}) collective-permute-start(f32[18,32,128]{2,1,0:T(8,128)S(1)} %slab.1.after.own), channel_id=1, source_target_pairs={{128,0},{256,128},{384,256},{129,1},{257,129},{385,257},{130,2},{2... | collective-permute-start | bytes 884744 | tf_op jit(solution)/shard_map/ppermute | solution.py:474
  52.1 4.0 %collective-permute-start.2 = (f32[18,32,128]{2,1,0:T(8,128)S(1)}, f32[18,32,128]{2,1,0:T(8,128)S(1)}, u32[]{:S(2)}, u32[]{:S(2)}) collective-permute-start(f32[18,32,128]{2,1,0:T(8,128)S(1)} %slab.1.after.own), channel_id=1, source_target_pairs={{0,128},{128,256},{256,384},{1,129},{129,257},{257,385},{2,130},{1... | collective-permute-start | bytes 884744 | tf_op jit(solution)/shard_map/ppermute | solution.py:474
  56.1 1.7 %coarse.1 = (f32[512,512]{1,0:T(8,128)S(1)}, f32[3,32,256]{2,1,0:T(8,128)S(1)}, f32[3,32,256]{2,1,0:T(8,128)S(1)}, f32[3,32,256]{2,1,0:T(8,128)S(1)}) custom-call(bf16[512,512]{1,0:T(8,128)(2,1)S(1)} %copy-done, f32[4,128,128]{2,1,0:T(8,128)S(1)} %diagonal.1.after, f32[32,1,128]{2,1,0:T(1,128)S(1)} %all_to_all.21.gathered, f32[18,32,128]{2,1,0:T(8,128)S(1)} %slab.1.after.own), custom_call_target="tpu_custom_call" | custom-call | tf_op jit(solution)/shard_map/coarse/pallas_call | solution.py:508
  57.8 1.6 %collective-permute-done.3.right = f32[18,32,128]{2,1,0:T(8,128)S(1)} collective-permute-done((f32[18,32,128]{2,1,0:T(8,128)S(1)}, f32[18,32,128]{2,1,0:T(8,128)S(1)}, u32[]{:S(2)}, u32[]{:S(2)}) %collective-permute-start.3) | collective-permute-done | bytes 294944 | tf_op jit(solution)/shard_map/ppermute | solution.py:474
  59.4 0.9 collective-permute-done.2.left
  60.3 7.7 %fields.1 = (f32[8,16,128]{2,1,0:T(8,128)S(1)}, f32[8,16,128]{2,1,0:T(8,128)S(1)}, f32[8,16,128]{2,1,0:T(8,128)S(1)}, f32[8,16,128]{2,1,0:T(8,128)S(1)}, f32[8,1...) custom-call(f32[18,32,128]{2,1,0:T(8,128)S(1)} %collective-permute-d, ...), custom_call_target="tpu_custom_call" | custom-call | tf_op jit(solution)/shard_map/fields/pallas_call | solution.py:512
  68.1 12.5 %all_to_all.22.part = f32[16,1,128]{2,1,0:T(1,128)S(1)} all-to-all(f32[16,1,128]{2,1,0:T(1,128)S(1)} %get-tuple-element.40), channel_id=1, replica_groups=mesh['gx'=4,'gy'=8,'gz'=16] {'gz'}, dimensions={0} | all-to-all | bytes 16384 | tf_op jit(solution)/shard_map/all_to_all | solution.py:519
  80.6 15.7 %all_to_all.23.gathered = f32[32,1,128]{2,1,0:T(1,128)S(1)} all-to-all(f32[32,1,128]{2,1,0:T(1,128)S(1)} %sum.1), channel_id=1, replica_groups=mesh['gx'=4,'gy'=8,'gz'=16] {'gx','gy'}, dimensions={0} | all-to-all | bytes 32768 | tf_op jit(solution)/shard_map/all_to_all | solution.py:521
  96.3 1.1 %final.1 = (f32[8,16,128]{2,1,0:T(8,128)}, f32[8,16,128]{2,1,0:T(8,128)}) custom-call(f32[32,1,128]{2,1,0:T(1,128)S(1)} %all_to_all.23.gathered, f32[512,512]{1,0:T(8,128)S(1)} %get-tuple-element.41.inv, f32[8,16,128]{2,1,0:T(8,128)S(1)} %get-tuple-element.42.d_in, f32[8,16,128]{2,1,0:T(8,128)S(1)} %get-tuple-element.43.t_in, ...), custom_call_target="tpu_custom_call" | custom-call | tf_op jit(solution)/shard_map/final/pallas_call | solution.py:522
  (2 shorter events, 0.0 us)
Async XLA Ops:
  0.6 46.8 %copy-start = (bf16[512,512]{1,0:T(8,128)(2,1)S(1)}, bf16[512,512]{1,0:T(8,128)(2,1)}, u32[]{:S(2)}) copy-start(bf16[512,512]{1,0:T(8,128)(2,1)} %factor.1) | copy-start | bytes 1572868
  1.3 0.8 copy-start.1
  2.2 0.8 copy-start.2
  42.1 8.6 %collective-permute-start = (f32[18,8,128]{2,1,0:T(8,128)S(1)}, f32[18,8,128]{2,1,0:T(8,128)S(1)}, u32[]{:S(2)}, u32[]{:S(2)}) collective-permute-start(f32[18,8,128]{2,1,0:T(8,128)S(1)} %get-tuple-element.33), channel_id=1, source_target_pairs={{16,0},{32,16},{48,32},{64,48},{80,64},{96,80},{112,96},{17,1},{33... | collective-permute-start | bytes 221192 | tf_op jit(solution)/shard_map/ppermute | solution.py:474
  43.4 7.3 %collective-permute-start.1 = (f32[18,8,128]{2,1,0:T(8,128)S(1)}, f32[18,8,128]{2,1,0:T(8,128)S(1)}, u32[]{:S(2)}, u32[]{:S(2)}) collective-permute-start(f32[18,8,128]{2,1,0:T(8,128)S(1)} %get-tuple-element.34), channel_id=1, source_target_pairs={{0,16},{16,32},{32,48},{48,64},{64,80},{80,96},{96,112},{1,17},{17... | collective-permute-start | bytes 221192 | tf_op jit(solution)/shard_map/ppermute | solution.py:474
  50.8 8.6 %collective-permute-start.3 = (f32[18,32,128]{2,1,0:T(8,128)S(1)}, f32[18,32,128]{2,1,0:T(8,128)S(1)}, u32[]{:S(2)}, u32[]{:S(2)}) collective-permute-start(f32[18,32,128]{2,1,0:T(8,128)S(1)} %slab.1.after.own), channel_id=1, source_target_pairs={{128,0},{256,128},{384,256},{129,1},{257,129},{385,257},{130,2},{2... | collective-permute-start | bytes 884744 | tf_op jit(solution)/shard_map/ppermute | solution.py:474
  52.1 8.2 %collective-permute-start.2 = (f32[18,32,128]{2,1,0:T(8,128)S(1)}, f32[18,32,128]{2,1,0:T(8,128)S(1)}, u32[]{:S(2)}, u32[]{:S(2)}) collective-permute-start(f32[18,32,128]{2,1,0:T(8,128)S(1)} %slab.1.after.own), channel_id=1, source_target_pairs={{0,128},{128,256},{256,384},{1,129},{129,257},{257,385},{2,130},{1... | collective-permute-start | bytes 884744 | tf_op jit(solution)/shard_map/ppermute | solution.py:474

commit v3 on v2

--- a/solution.py
+++ b/solution.py
@@ -216,8 +216,9 @@
     return out
 
 
-def planes(low, high, body, most=4):
-    unroll = next(u for u in (most, 5, 4, 3, 2, 1) if (high - low) % u == 0)
+def planes(low, high, body):
+    count = high - low
+    unroll = max(u for u in range(1, count // 2 + 1) if count % u == 0)
 
     def step(i, carry):
         for u in range(unroll):
@@ -322,7 +323,7 @@
             u2[x] = u1[x] + below
             u2[x + 1] = u1[x + 1] + below
 
-        planes(*pair_range, pair, 2)
+        planes(*pair_range, pair)
 
         def last(x):
             put(x, u2[x] + i0[x] * (src[x] - image(u2, x)))
@@ -493,13 +494,13 @@
         rows_kernel, [(2, CY, CZ), (depth, H, CZ), (depth, H, CZ), (nx * ny, 1, CZ)], 2, name="rows"
     )(own, got)
     first = lax.all_to_all(line, ("gx", "gy"), 0, 0, tiled=True)
-    to_low, to_high, factor, first = lax.optimization_barrier((to_low, to_high, coarse_factor, first))
     y_high, y_low = exchange("gy", to_low, to_high)
+    slab = call(
+        slab_kernel, [(depth, EY, CZ)], 5, in_specs=[VMEM] * 4 + [any_space], name="slab"
+    )(own, zh, y_high, y_low, first)[0]
+    slab, factor = lax.optimization_barrier((slab, coarse_factor))
     nb = factor.shape[0] // CZ
     diagonal = call(diagonal_kernel, [(nb, CZ, CZ)], 1, name="diagonal")(factor)[0]
-    slab = call(
-        slab_kernel, [(depth, EY, CZ)], 5, in_specs=[VMEM] * 4 + [any_space], name="slab"
-    )(own, zh, y_high, y_low, diagonal)[0]
     x_high, x_low = exchange("gx", slab, slab)
     block = (CX, CY, CZ)
     wide = (EX, EY, EZ)

time: 97.8 us -> 89.8 us (0.918)
  blocking collectives: 66.8 us -> 63.5 us
  waiting for transfers between devices: 2.5 us -> 0.01 us
  Pallas kernels: 14.4 us -> 12.3 us
    all_to_all x1, blocking collectives: 15.7 us -> 12.4 us  [on_device(): second = lax.all_to_all(line, ('gx', 'gy'), 0, 0, tiled=True)]
    ppermute x4, waiting for transfers between devices: 2.5 us -> 0.01 us  [exchange(): return (lax.ppermute(to_low, axis, down), lax.ppermute(to_high, axis, up))]
    pallas_call x1, Pallas kernels: 7.75 us -> 5.68 us  [on_device(): call(main_kernel, [block] * 8 + [(2, CY, CZ), (CY, CZ), (nz, 1, CZ)], 6,...]
  transfers between devices with their start and end apart: 4 -> 4, of which waited for: 2 -> 0; matrix products, arithmetic and copies ran while one was open for 0% -> 0% of each run, Pallas kernels for 5% -> 6%
where the time goes in v3:
time: 89.8 us; the launch traced here: 89.4 us
  blocking collectives  63.5 us (71%)
  Pallas kernels  12.3 us (14%)
  starting transfers between devices  10.6 us (12%)
  local copies, waits for them, and re-layouts  1.68 us (2%)
  between operations  1.39 us (2%)
    all_to_all x1, blocking collectives, on_device(): got = lax.all_to_all(msg, 'gz', 0, 0, tiled=True)  20.6 us
    all_to_all x1, blocking collectives, on_device(): first = lax.all_to_all(line, ('gx', 'gy'), 0, 0, tiled=True)  18.1 us
    all_to_all x1, blocking collectives, on_device(): second = lax.all_to_all(line, ('gx', 'gy'), 0, 0, tiled=True)  12.4 us
    all_to_all x1, blocking collectives, on_device(): part = lax.all_to_all(outs[-1], 'gz', 0, 0, tiled=True)  12.3 us
    ppermute x4, starting transfers between devices, exchange(): return (lax.ppermute(to_low, axis, down), lax.ppermute(to_high, axis, up))  10.6 us
    pallas_call x1, Pallas kernels, on_device(): call(main_kernel, [block] * 8 + [(2, CY, CZ), (CY, CZ), (nz, 1, CZ)], 6,...  5.68 us
    pallas_call x1, Pallas kernels, on_device(): call(diagonal_kernel, [(nb, CZ, CZ)], 1, name='diagonal')(factor)[0]  3.3 us
  transfers between devices with their start and end apart: 4, of which 0 were waited for; matrix products, arithmetic and copies ran while one was open for 0% of the time, Pallas kernels for 6%

profile of v3, /device:TPU:1, one launch (start us, length us, event | category | flops | bytes accessed | tf_op | source)
XLA Modules:
  0.0 89.4 jit_solution(1241501037890514380)
XLA Ops:
  1.3 0.0 copy-start.1
  1.3 0.8 copy-done.1
  2.1 0.0 copy-start.2
  2.1 0.8 copy-done.2
  3.0 0.3 pack.1
  3.3 0.0 copy-start
  3.3 20.6 %all_to_all.20.got = f32[16,16,128]{2,1,0:T(8,128)S(1)} all-to-all(f32[16,16,128]{2,1,0:T(8,128)S(1)} %get-tuple-element.26), channel_id=1, replica_groups=mesh['gx'=4,'gy'=8,'gz'=16] {'gz'}, dimensions={0} | all-to-all | bytes 262144 | tf_op jit(solution)/shard_map/all_to_all | solution.py:491
  23.9 0.2 rows.1
  24.1 1.3 %collective-permute-start = (f32[18,8,128]{2,1,0:T(8,128)S(1)}, f32[18,8,128]{2,1,0:T(8,128)S(1)}, u32[]{:S(2)}, u32[]{:S(2)}) collective-permute-start(f32[18,8,128]{2,1,0:T(8,128)S(1)} %get-tuple-element.28), channel_id=1, source_target_pairs={{16,0},{32,16},{48,32},{64,48},{80,64},{96,80},{112,96},{17,1},{33... | collective-permute-start | bytes 221192 | tf_op jit(solution)/shard_map/ppermute | solution.py:475
  25.4 4.0 %collective-permute-start.1 = (f32[18,8,128]{2,1,0:T(8,128)S(1)}, f32[18,8,128]{2,1,0:T(8,128)S(1)}, u32[]{:S(2)}, u32[]{:S(2)}) collective-permute-start(f32[18,8,128]{2,1,0:T(8,128)S(1)} %get-tuple-element.29), channel_id=1, source_target_pairs={{0,16},{16,32},{32,48},{48,64},{64,80},{80,96},{96,112},{1,17},{17... | collective-permute-start | bytes 221192 | tf_op jit(solution)/shard_map/ppermute | solution.py:475
  29.4 18.1 %all_to_all.21.after.gathered = f32[32,1,128]{2,1,0:T(1,128)S(1)} all-to-all(f32[32,1,128]{2,1,0:T(1,128)S(1)} %get-tuple-element.30), channel_id=1, replica_groups=mesh['gx'=4,'gy'=8,'gz'=16] {'gx','gy'}, dimensions={0} | all-to-all | bytes 32768 | tf_op jit(solution)/shard_map/all_to_all | solution.py:496
  47.5 0.0 collective-permute-done.from_high
  47.5 0.0 collective-permute-done.1.from_low
  47.5 1.3 %collective-permute-start.3 = (f32[18,32,128]{2,1,0:T(8,128)S(1)}, f32[18,32,128]{2,1,0:T(8,128)S(1)}, u32[]{:S(2)}, u32[]{:S(2)}) collective-permute-start(f32[18,32,128]{2,1,0:T(8,128)S(1)} %slab.1.after.own), channel_id=1, source_target_pairs={{128,0},{256,128},{384,256},{129,1},{257,129},{385,257},{130,2},{2... | collective-permute-start | bytes 884744 | tf_op jit(solution)/shard_map/ppermute | solution.py:475
  48.8 4.0 %collective-permute-start.2 = (f32[18,32,128]{2,1,0:T(8,128)S(1)}, f32[18,32,128]{2,1,0:T(8,128)S(1)}, u32[]{:S(2)}, u32[]{:S(2)}) collective-permute-start(f32[18,32,128]{2,1,0:T(8,128)S(1)} %slab.1.after.own), channel_id=1, source_target_pairs={{0,128},{128,256},{256,384},{1,129},{129,257},{257,385},{2,130},{1... | collective-permute-start | bytes 884744 | tf_op jit(solution)/shard_map/ppermute | solution.py:475
  52.9 0.0 copy-done
  52.9 3.3 %diagonal.1 = f32[4,128,128]{2,1,0:T(8,128)S(1)} custom-call(bf16[512,512]{1,0:T(8,128)(2,1)S(1)} %copy-done), custom_call_target="tpu_custom_call" | custom-call | tf_op jit(solution)/shard_map/diagonal/pallas_call | solution.py:503
  56.2 1.7 %coarse.1 = (f32[512,512]{1,0:T(8,128)S(1)}, f32[3,32,256]{2,1,0:T(8,128)S(1)}, f32[3,32,256]{2,1,0:T(8,128)S(1)}, f32[3,32,256]{2,1,0:T(8,128)S(1)}) custom-call(bf16[512,512]{1,0:T(8,128)(2,1)S(1)} %copy-done, f32[4,128,128]{2,1,0:T(8,128)S(1)} %diagonal.1, f32[32,1,128]{2,1,0:T(1,128)S(1)} %all_to_all.21.after.gathered, f32[18,32,128]{2,1,0:T(8,128)S(1)} %slab.1.after.own), custom_call_target="tpu_custom_call" | custom-call | tf_op jit(solution)/shard_map/coarse/pallas_call | solution.py:509
  57.9 0.0 collective-permute-done.3.right
  57.9 0.0 collective-permute-done.2.left
  57.9 5.7 %fields.1 = (f32[8,16,128]{2,1,0:T(8,128)S(1)}, f32[8,16,128]{2,1,0:T(8,128)S(1)}, f32[8,16,128]{2,1,0:T(8,128)S(1)}, f32[8,16,128]{2,1,0:T(8,128)S(1)}, f32[8,1...) custom-call(f32[18,32,128]{2,1,0:T(8,128)S(1)} %collective-permute-d, ...), custom_call_target="tpu_custom_call" | custom-call | tf_op jit(solution)/shard_map/fields/pallas_call | solution.py:513
  63.6 12.3 %all_to_all.22.part = f32[16,1,128]{2,1,0:T(1,128)S(1)} all-to-all(f32[16,1,128]{2,1,0:T(1,128)S(1)} %get-tuple-element.36), channel_id=1, replica_groups=mesh['gx'=4,'gy'=8,'gz'=16] {'gz'}, dimensions={0} | all-to-all | bytes 16384 | tf_op jit(solution)/shard_map/all_to_all | solution.py:520
  75.9 12.4 %all_to_all.23.gathered = f32[32,1,128]{2,1,0:T(1,128)S(1)} all-to-all(f32[32,1,128]{2,1,0:T(1,128)S(1)} %sum.1), channel_id=1, replica_groups=mesh['gx'=4,'gy'=8,'gz'=16] {'gx','gy'}, dimensions={0} | all-to-all | bytes 32768 | tf_op jit(solution)/shard_map/all_to_all | solution.py:522
  88.3 1.1 %final.1 = (f32[8,16,128]{2,1,0:T(8,128)}, f32[8,16,128]{2,1,0:T(8,128)}) custom-call(f32[32,1,128]{2,1,0:T(1,128)S(1)} %all_to_all.23.gathered, f32[512,512]{1,0:T(8,128)S(1)} %get-tuple-element.37.inv, f32[8,16,128]{2,1,0:T(8,128)S(1)} %get-tuple-element.38.d_in, f32[8,16,128]{2,1,0:T(8,128)S(1)} %get-tuple-element.39.t_in, ...), custom_call_target="tpu_custom_call" | custom-call | tf_op jit(solution)/shard_map/final/pallas_call | solution.py:523
  (2 shorter events, 0.0 us)
Async XLA Ops:
  1.3 0.8 copy-start.1
  2.1 0.8 copy-start.2
  3.3 49.6 %copy-start = (bf16[512,512]{1,0:T(8,128)(2,1)S(1)}, bf16[512,512]{1,0:T(8,128)(2,1)}, u32[]{:S(2)}) copy-start(bf16[512,512]{1,0:T(8,128)(2,1)} %factor.1) | copy-start | bytes 1572868
  24.1 23.4 %collective-permute-start = (f32[18,8,128]{2,1,0:T(8,128)S(1)}, f32[18,8,128]{2,1,0:T(8,128)S(1)}, u32[]{:S(2)}, u32[]{:S(2)}) collective-permute-start(f32[18,8,128]{2,1,0:T(8,128)S(1)} %get-tuple-element.28), channel_id=1, source_target_pairs={{16,0},{32,16},{48,32},{64,48},{80,64},{96,80},{112,96},{17,1},{33... | collective-permute-start | bytes 221192 | tf_op jit(solution)/shard_map/ppermute | solution.py:475
  25.4 22.1 %collective-permute-start.1 = (f32[18,8,128]{2,1,0:T(8,128)S(1)}, f32[18,8,128]{2,1,0:T(8,128)S(1)}, u32[]{:S(2)}, u32[]{:S(2)}) collective-permute-start(f32[18,8,128]{2,1,0:T(8,128)S(1)} %get-tuple-element.29), channel_id=1, source_target_pairs={{0,16},{16,32},{32,48},{48,64},{64,80},{80,96},{96,112},{1,17},{17... | collective-permute-start | bytes 221192 | tf_op jit(solution)/shard_map/ppermute | solution.py:475
  47.5 10.3 %collective-permute-start.3 = (f32[18,32,128]{2,1,0:T(8,128)S(1)}, f32[18,32,128]{2,1,0:T(8,128)S(1)}, u32[]{:S(2)}, u32[]{:S(2)}) collective-permute-start(f32[18,32,128]{2,1,0:T(8,128)S(1)} %slab.1.after.own), channel_id=1, source_target_pairs={{128,0},{256,128},{384,256},{129,1},{257,129},{385,257},{130,2},{2... | collective-permute-start | bytes 884744 | tf_op jit(solution)/shard_map/ppermute | solution.py:475
  48.8 9.1 %collective-permute-start.2 = (f32[18,32,128]{2,1,0:T(8,128)S(1)}, f32[18,32,128]{2,1,0:T(8,128)S(1)}, u32[]{:S(2)}, u32[]{:S(2)}) collective-permute-start(f32[18,32,128]{2,1,0:T(8,128)S(1)} %slab.1.after.own), channel_id=1, source_target_pairs={{0,128},{128,256},{256,384},{1,129},{129,257},{257,385},{2,130},{1... | collective-permute-start | bytes 884744 | tf_op jit(solution)/shard_map/ppermute | solution.py:475

commit v4 on v3

--- a/solution.py
+++ b/solution.py
@@ -8,6 +8,7 @@
 from jax.sharding import PartitionSpec as P
 
 F32 = jnp.float32
+PACK_MIB = 60
 OMEGA = 0.8
 CX, CY, CZ = 8, 16, 128
 CELLS = CX * CY * CZ
@@ -18,7 +19,7 @@
 SMEM = pl.BlockSpec(memory_space=pltpu.SMEM)
 
 
-def call(kernel, out_shapes, n_in, scratch=(), in_specs=None, name=None):
+def call(kernel, out_shapes, n_in, scratch=(), in_specs=None, name=None, aliases=None, mib=24):
     outs = [jax.ShapeDtypeStruct(s, F32) for s in out_shapes]
     return pl.pallas_call(
         kernel,
@@ -26,7 +27,8 @@
         in_specs=in_specs or [VMEM] * n_in,
         out_specs=[VMEM] * len(outs),
         scratch_shapes=[pltpu.VMEM(s, F32) for s in scratch],
-        compiler_params=pltpu.CompilerParams(vmem_limit_bytes=48 * 1024 * 1024),
+        input_output_aliases=aliases or {},
+        compiler_params=pltpu.CompilerParams(vmem_limit_bytes=mib * 1024 * 1024),
         name=name,
     )
 
@@ -43,34 +45,26 @@
     return jnp.sum(jnp.sum(x, axis=0, keepdims=True), axis=1, keepdims=True)
 
 
-def pack_kernel(ext, rhs, cond, own, msg, sems):
-    copies = [
-        pltpu.make_async_copy(cond, own.at[0:CX], sems.at[0]),
-        pltpu.make_async_copy(rhs, own.at[CX : 2 * CX], sems.at[1]),
-    ]
-    for c in copies:
-        c.start()
+def pack_kernel(ext, rhs, cond, msg):
     nz = msg.shape[0]
     lane = iota((CY, CZ), 1)
     row = iota((CY, CZ), 0)
     a = jnp.zeros((CY, CZ), F32)
     b = jnp.zeros((CY, CZ), F32)
     acc = jnp.zeros((CY, CZ), F32)
-    inside = lane < ext[0, 0, 0]
-    count = jnp.full((CY, CZ), ext[0, 0, 0], jnp.int32).astype(F32)
+    count = jnp.broadcast_to(ext[0], (CY, CZ))
+    inside = lane < count
     z = lax.axis_index("gz")
-    for c in copies:
-        c.wait()
     for x in range(CX):
-        k = own[x]
-        r = own[CX + x]
+        k = cond[x]
+        r = rhs[x]
         acc = acc + jnp.where(inside, r, 0.0)
         hi = (lane >= 16 * x) & (lane < 16 * x + H)
         start = (16 * x - H) % CZ
         lo = (lane >= start) & (lane < start + H)
         a = jnp.where(hi, roll(k, 16 * x, 1), jnp.where(lo, roll(r, 16 * x - H, 1), a))
         b = jnp.where(lo, roll(k, 16 * x, 1), jnp.where(hi, roll(r, 16 * x + H, 1), b))
-    info = jnp.where(row == 0, total(acc) / CELLS, count)
+    info = jnp.where(row == 0, total(acc) / CELLS, count.astype(F32))
     a = jnp.where((lane == CZ - 1) & (row < 2), info, a)
     b = jnp.where((lane == 0) & (row < 2), info, b)
     for i in range(nz):
@@ -81,7 +75,7 @@
         msg[z - 1] = a
 
 
-def rows_kernel(own, got, zh, to_low, to_high, line):
+def rows_kernel(rhs, cond, got, zh, to_low, to_high, line):
     nz = got.shape[0]
     z = lax.axis_index("gz")
     low_half = iota((CY, CZ), 1) % 16 < H
@@ -100,16 +94,19 @@
     zr = jnp.where(low_half, roll(a, H, 1), roll(b, -H, 1))
     zh[0] = zk
     zh[1] = zr
-    to_low[0 : 2 * CX] = own[:, 0:H, :]
+    to_low[0:CX] = cond[:, 0:H, :]
+    to_low[CX : 2 * CX] = rhs[:, 0:H, :]
     to_low[2 * CX] = zk[0:H]
     to_low[2 * CX + 1] = zr[0:H]
-    to_high[0 : 2 * CX] = own[:, CY - H : CY, :]
+    to_high[0:CX] = cond[:, CY - H : CY, :]
+    to_high[CX : 2 * CX] = rhs[:, CY - H : CY, :]
     to_high[2 * CX] = zk[CY - H : CY]
     to_high[2 * CX + 1] = zr[CY - H : CY]
 
 
-def slab_kernel(own, zh, from_high, from_low, after, slab):
-    slab[0 : 2 * CX, 0:CY] = own[...]
+def slab_kernel(rhs, cond, zh, from_high, from_low, after, slab):
+    slab[0:CX, 0:CY] = cond[...]
+    slab[CX : 2 * CX, 0:CY] = rhs[...]
     slab[2 * CX : 2 * CX + 2, 0:CY] = zh[...]
     slab[:, CY : CY + H] = from_high[...]
     slab[:, CY + H : EY] = from_low[...]
@@ -216,22 +213,71 @@
     return out
 
 
-def planes(low, high, body):
+def groups(low, high, body, step=1):
     count = high - low
-    unroll = max(u for u in range(1, count // 2 + 1) if count % u == 0)
-
-    def step(i, carry):
-        for u in range(unroll):
-            body(low + i * unroll + u)
+    size = max(u for u in range(1, count // 2 + 1) if count % u == 0)
+
+    def go(i, carry):
+        body([low + i * size + u for u in range(size)])
         return carry
 
-    lax.fori_loop(0, (high - low) // unroll, step, 0)
+    lax.fori_loop(0, count // size, go, 0)
+
+
+def unpack(src, bx, kap, rr, ff):
+    for x in range(CX):
+        at = bx * CX + x
+        kap[at, :, 0:CZ] = src[x]
+        kap[at, :, CZ:EZ] = roll(src[2 * CX], -16 * x, 1)
+        rr[at, :, 0:CZ] = src[CX + x] * ff[bx, :, 0:CZ]
+        rr[at, :, CZ:EZ] = roll(src[2 * CX + 1], -16 * x, 1) * ff[bx, :, CZ:EZ]
+
+
+def pooled(s):
+    even = iota(s.shape, 0) % 2 == 0
+    s = s + jnp.where(even, roll(s, -1, 0), roll(s, 1, 0))
+    even = iota(s.shape, 1) % 2 == 0
+    return s + jnp.where(even, roll(s, -1, 1), roll(s, 1, 1))
+
+
+def coef_x(x, kap, cx):
+    cx[x] = 0.5 * (kap[x] + kap[x + 1])
+
+
+def coef_yz(x, kap, cy, cz):
+    k = kap[x]
+    cy[x] = 0.5 * (k + roll(k, -1, 0))
+    cz[x] = 0.5 * (k + roll(k, -1, 1))
+
+
+def inverse_fine(x, cx, cy, cz, i0, rr, u1, ff):
+    f = ff[x >> 3]
+    b, c = cy[x], cz[x]
+    s = cx[x] + cx[x - 1] + b + roll(b, 1, 0) + c + roll(c, 1, 1)
+    v = OMEGA * f / (s + 1.0 - f)
+    i0[x] = v
+    u1[x] = v * rr[x]
+
+
+def coarse_cond(i, kap, k1):
+    k1[i] = pooled(kap[2 * i] + kap[2 * i + 1]) * 0.125
+
+
+def inverse_coarse(i, k1, i1, f1):
+    k = k1[i]
+    f = f1[i >> 2]
+    s = k1[i - 1] + k1[i + 1] + roll(k, 2, 0) + roll(k, -2, 0) + roll(k, 2, 1) + roll(k, -2, 1)
+    s = 3.0 * k + 0.5 * s
+    i1[i] = OMEGA * f / (4.0 * s + 1.0 - f)
 
 
 ROW_PARTS = ((0, 0), (8, 0), (16, 1), (24, -1))
 
 
-def coarse_kernel(nx, ny, nz, factor, diagonal, gathered, after, inv, ff, f1, fy):
+def coarse_kernel(
+    nx, ny, nz, factor, diagonal, gathered, slab,
+    inv, ff, f1, fy, kap, rr, cx, cy, cz, i0, k1, i1, u1,
+):
     inverse_of(factor, diagonal, inv)
     lane8 = iota((8, CZ), 1)
     lane8f = lane8.astype(F32)
@@ -254,91 +300,93 @@
             fy[bx, r : r + 8, CZ:EZ] = m1 * jnp.where(lane8 < CZ // 2, v[1], v[-1])
 
 
+    unpack(slab, 1, kap, rr, ff)
+    for x in range(CX, 2 * CX):
+        coef_yz(x, kap, cy, cz)
+        if x < 2 * CX - 1:
+            coef_x(x, kap, cx)
+    for x in range(CX + 1, 2 * CX - 1):
+        inverse_fine(x, cx, cy, cz, i0, rr, u1, ff)
+    for i in range(CX // 2, CX):
+        coarse_cond(i, kap, k1)
+    for i in range(CX // 2 + 1, CX - 1):
+        inverse_coarse(i, k1, i1, f1)
+
+
 def main_kernel(
-    left, own, right, ff, f1, fy,
-    d_out, t_out, n_out, an_out, r_out, e0_out, ey_out, ez_out, ex_out, f_out, msg,
-    kap, rr, cx, cy, cz, i0, k1, i1, u1, u2, dd, tt,
+    left, right, ff, f1, fy, *refs
 ):
-    for bx, src in enumerate((left, own, right)):
-        for x in range(CX):
-            at = bx * CX + x
-            kap[at, :, 0:CZ] = src[x]
-            kap[at, :, CZ:EZ] = roll(src[2 * CX], -16 * x, 1)
-            rr[at, :, 0:CZ] = src[CX + x] * ff[bx, :, 0:CZ]
-            rr[at, :, CZ:EZ] = roll(src[2 * CX + 1], -16 * x, 1) * ff[bx, :, CZ:EZ]
-    row_even = iota((EY, EZ), 0) % 2 == 0
-    lane_even = iota((EY, EZ), 1) % 2 == 0
-
-    def pooled(s):
-        s = s + jnp.where(row_even, roll(s, -1, 0), roll(s, 1, 0))
-        return s + jnp.where(lane_even, roll(s, -1, 1), roll(s, 1, 1))
-
-    def coefs(x):
-        k = kap[x]
-        cx[x] = 0.5 * (k + kap[jnp.minimum(x + 1, EX - 1)])
-        cy[x] = 0.5 * (k + roll(k, -1, 0))
-        cz[x] = 0.5 * (k + roll(k, -1, 1))
-
-    planes(0, EX, coefs)
-
-    def inverses(x):
-        f = ff[x >> 3]
-        b, c = cy[x], cz[x]
-        s = cx[x] + cx[x - 1] + b + roll(b, 1, 0) + c + roll(c, 1, 1)
-        i0[x] = OMEGA * f / (s + 1.0 - f)
-
-    planes(1, EX - 1, inverses)
-
-    def coarse_cond(i):
-        k1[i] = pooled(kap[2 * i] + kap[2 * i + 1]) * 0.125
-
-    planes(0, EX // 2, coarse_cond)
-
-    def coarse_inv(i):
-        k = k1[i]
-        f = f1[i >> 2]
-        s = k1[i - 1] + k1[i + 1] + roll(k, 2, 0) + roll(k, -2, 0) + roll(k, 2, 1) + roll(k, -2, 1)
-        s = 3.0 * k + 0.5 * s
-        i1[i] = OMEGA * f / (4.0 * s + 1.0 - f)
-
-    planes(1, EX // 2 - 1, coarse_inv)
-
-    def image(u, x):
-        c = u[x]
-        gx = cx[x] * (c - u[x + 1]) - cx[x - 1] * (u[x - 1] - c)
-        gy = cy[x] * (c - roll(c, -1, 0))
-        gz = cz[x] * (c - roll(c, -1, 1))
-        return ff[x >> 3] * (gx + (gy - roll(gy, 1, 0)) + (gz - roll(gz, 1, 1)))
-
-    def smooth(src, first_range, pair_range, out_range, put):
-        def first(x):
-            u1[x] = i0[x] * src[x]
-
-        planes(*first_range, first)
-
-        def pair(i):
-            x = 2 * i
-            s = (src[x] - image(u1, x)) + (src[x + 1] - image(u1, x + 1))
-            below = ff[x >> 3] * (i1[i] * pooled(s))
-            u2[x] = u1[x] + below
-            u2[x + 1] = u1[x + 1] + below
-
-        planes(*pair_range, pair)
-
-        def last(x):
-            put(x, u2[x] + i0[x] * (src[x] - image(u2, x)))
-
-        planes(*out_range, last)
+    (kap, rr, cx, cy, cz, i0, k1, i1, u1) = refs[9:18]
+    (d_out, t_out, n_out, an_out, r_out, e0_out, ey_out, ez_out, ex_out, f_out, msg) = refs[18:29]
+    u2, dd, tt = refs[29:]
+    unpack(left, 0, kap, rr, ff)
+    unpack(right, 2, kap, rr, ff)
+    coef_x(2 * CX - 1, kap, cx)
+
+    def coefs(us):
+        for u in us:
+            for x in (u, u + 2 * CX):
+                coef_yz(x, kap, cy, cz)
+            coef_x(u, kap, cx)
+            coef_x(jnp.minimum(u + 2 * CX, EX - 2), kap, cx)
+
+    groups(0, CX, coefs)
+
+    def inverses(us):
+        for u in us:
+            for x in (u, u + 2 * CX - 2):
+                inverse_fine(x, cx, cy, cz, i0, rr, u1, ff)
+
+    groups(1, CX + 1, inverses)
+    for i in range(CX // 2):
+        for j in (i, i + CX):
+            coarse_cond(j, kap, k1)
+    for i in range(1, CX // 2 + 1):
+        for j in (i, i + CX - 2):
+            inverse_coarse(j, k1, i1, f1)
+
+    def images(u, xs, masked=True):
+        c = [u[xs[0] - 1]] + [u[x] for x in xs] + [u[xs[-1] + 1]]
+        flux = [cx[x] * (c[i] - c[i + 1]) for i, x in enumerate([xs[0] - 1] + list(xs))]
+        out = []
+        for i, x in enumerate(xs):
+            v = c[i + 1]
+            gy = cy[x] * (v - roll(v, -1, 0))
+            gz = cz[x] * (v - roll(v, -1, 1))
+            w = (flux[i + 1] - flux[i]) + (gy - roll(gy, 1, 0)) + (gz - roll(gz, 1, 1))
+            out.append(ff[x >> 3] * w if masked else w)
+        return out
+
+    def smooth(src, pair_range, out_range, put):
+        def pairs(ps):
+            xs = [2 * ps[0] + j for j in range(2 * len(ps))]
+            im = images(u1, xs)
+            for j, i in enumerate(ps):
+                x, y = xs[2 * j], xs[2 * j + 1]
+                s = (src[x] - im[2 * j]) + (src[y] - im[2 * j + 1])
+                below = ff[x >> 3] * (i1[i] * pooled(s))
+                u2[x] = u1[x] + below
+                u2[y] = u1[y] + below
+
+        groups(*pair_range, pairs)
+
+        def last(xs):
+            for x, w in zip(xs, images(u2, xs, False)):
+                put(x, u2[x] + i0[x] * (src[x] - w))
+
+        groups(*out_range, last)
 
     def put_d(x, v):
         dd[x] = v + fy[x >> 3]
 
-    smooth(rr, (1, EX - 1), (1, EX // 2 - 1), (3, EX - 3), put_d)
-
-    def put_t(x):
-        tt[x] = image(dd, x)
-
-    planes(4, EX - 4, put_t)
+    smooth(rr, (1, EX // 2 - 1), (3, EX - 3), put_d)
+
+    def apply(xs):
+        for x, w in zip(xs, images(dd, xs)):
+            tt[x] = w
+            u1[x] = i0[x] * w
+
+    groups(4, EX - 4, apply)
     for x in range(CX):
         d_out[x] = dd[H + x, 0:CY, 0:CZ]
 
@@ -350,7 +398,7 @@
     for x in range(CX):
         s_rz = s_rz + rr[H + x, 0:CY, 0:CZ] * d_out[x]
         s_dad = s_dad + tt[H + x, 0:CY, 0:CZ] * d_out[x]
-    smooth(tt, (4, EX - 4), (3, EX // 2 - 3), (7, EX - 7), put_n)
+    smooth(tt, (3, EX // 2 - 3), (7, EX - 7), put_n)
     s_x, s_y, s_tau, s_om, s_d, s_cy, s_cz = (zero,) * 7
     f = ff[1]
     row = iota((EY, EZ), 0)
@@ -364,9 +412,10 @@
     f_up_z = roll(f, -1, 1)
     dif_y = mine - roll(mine, -1, 0)
     dif_z = mine - roll(mine, -1, 1)
+    image_n = images(dd, list(range(H, H + CX)))
     for x in range(CX):
         at = H + x
-        an = image(dd, at)[0:CY, 0:CZ]
+        an = image_n[x][0:CY, 0:CZ]
         n = dd[at, 0:CY, 0:CZ]
         t = tt[at, 0:CY, 0:CZ]
         an_out[x] = an
@@ -479,25 +528,17 @@
     nx, ny, nz = (lax.axis_size(a) for a in ("gx", "gy", "gz"))
     sizes = (nx, ny, nz)
     any_space = pl.BlockSpec(memory_space=pl.ANY)
-    own, msg = pl.pallas_call(
-        pack_kernel,
-        out_shape=[jax.ShapeDtypeStruct(s, F32) for s in ((2 * CX, CY, CZ), (nz, CY, CZ))],
-        in_specs=[SMEM, pl.BlockSpec(memory_space=pltpu.HBM), pl.BlockSpec(memory_space=pltpu.HBM)],
-        out_specs=[VMEM, VMEM],
-        scratch_shapes=[pltpu.SemaphoreType.DMA((2,))],
-        compiler_params=pltpu.CompilerParams(vmem_limit_bytes=8 * 1024 * 1024),
-        name="pack",
-    )(extents, right_side, conductance)
+    msg = call(pack_kernel, [(nz, CY, CZ)], 3, name="pack", mib=PACK_MIB)(extents, right_side, conductance)[0]
     got = lax.all_to_all(msg, "gz", 0, 0, tiled=True)
     depth = 2 * CX + 2
     zh, to_low, to_high, line = call(
-        rows_kernel, [(2, CY, CZ), (depth, H, CZ), (depth, H, CZ), (nx * ny, 1, CZ)], 2, name="rows"
-    )(own, got)
+        rows_kernel, [(2, CY, CZ), (depth, H, CZ), (depth, H, CZ), (nx * ny, 1, CZ)], 3, name="rows"
+    )(right_side, conductance, got)
     first = lax.all_to_all(line, ("gx", "gy"), 0, 0, tiled=True)
     y_high, y_low = exchange("gy", to_low, to_high)
     slab = call(
-        slab_kernel, [(depth, EY, CZ)], 5, in_specs=[VMEM] * 4 + [any_space], name="slab"
-    )(own, zh, y_high, y_low, first)[0]
+        slab_kernel, [(depth, EY, CZ)], 6, in_specs=[VMEM] * 5 + [any_space], name="slab"
+    )(right_side, conductance, zh, y_high, y_low, first)[0]
     slab, factor = lax.optimization_barrier((slab, coarse_factor))
     nb = factor.shape[0] // CZ
     diagonal = call(diagonal_kernel, [(nb, CZ, CZ)], 1, name="diagonal")(factor)[0]
@@ -506,17 +547,18 @@
     wide = (EX, EY, EZ)
     half = (EX // 2, EY, EZ)
     third = (3, EY, EZ)
-    inv, ff, f1, fy = call(
-        functools.partial(coarse_kernel, *sizes), [factor.shape] + [third] * 3, 4,
-        in_specs=[VMEM] * 3 + [any_space], name="coarse",
+    arrays = [wide] * 6 + [half] * 2 + [wide]
+    inv, ff, f1, fy, *fields = call(
+        functools.partial(coarse_kernel, *sizes), [factor.shape] + [third] * 3 + arrays, 4, name="coarse"
     )(factor, diagonal, first, slab)
     outs = call(
         main_kernel,
-        [block] * 8 + [(2, CY, CZ), (CY, CZ), (nz, 1, CZ)],
-        6,
-        scratch=[wide] * 6 + [half] * 2 + [wide] * 4,
+        arrays + [block] * 8 + [(2, CY, CZ), (CY, CZ), (nz, 1, CZ)],
+        14,
+        scratch=[wide] * 3,
+        aliases={5 + i: i for i in range(9)},
         name="fields",
-    )(x_low, slab, x_high, ff, f1, fy)
+    )(x_low, x_high, ff, f1, fy, *fields)[9:]
     part = lax.all_to_all(outs[-1], "gz", 0, 0, tiled=True)
     line = call(sum_kernel, [(nx * ny, 1, CZ)], 1, name="sum")(part)[0]
     second = lax.all_to_all(line, ("gx", "gy"), 0, 0, tiled=True)

time: 89.8 us -> 89.6 us (level)
  local copies, waits for them, and re-layouts: 1.68 us -> 0.01 us
  Pallas kernels: 12.3 us -> 13.6 us
    unnamed x6, local copies, waits for them, and re-layouts: 1.68 us -> 0.01 us
    pallas_call x3, Pallas kernels: 5.99 us -> 7.23 us  [the longest x1 5.48 us: on_device(): call(main_kernel, arrays + [block] * 8 + [(2, CY, CZ), (CY, CZ), (nz, 1,...]
where the time goes in v4:
time: 89.6 us; the launch traced here: 89.1 us
  blocking collectives  63.5 us (71%)
  Pallas kernels  13.6 us (15%)
  starting transfers between devices  10.6 us (12%)
  between operations  1.38 us (2%)
    all_to_all x1, blocking collectives, on_device(): got = lax.all_to_all(msg, 'gz', 0, 0, tiled=True)  20.8 us
    all_to_all x1, blocking collectives, on_device(): first = lax.all_to_all(line, ('gx', 'gy'), 0, 0, tiled=True)  18.1 us
    all_to_all x1, blocking collectives, on_device(): second = lax.all_to_all(line, ('gx', 'gy'), 0, 0, tiled=True)  12.3 us
    all_to_all x1, blocking collectives, on_device(): part = lax.all_to_all(outs[-1], 'gz', 0, 0, tiled=True)  12.3 us
    ppermute x4, starting transfers between devices, exchange(): return (lax.ppermute(to_low, axis, down), lax.ppermute(to_high, axis, up))  10.6 us
    pallas_call x1, Pallas kernels, on_device(): call(main_kernel, arrays + [block] * 8 + [(2, CY, CZ), (CY, CZ), (nz, 1,...  5.48 us
    pallas_call x1, Pallas kernels, on_device(): call(diagonal_kernel, [(nb, CZ, CZ)], 1, name='diagonal')(factor)[0]  3.31 us
    pallas_call x1, Pallas kernels, on_device(): call(functools.partial(coarse_kernel, *sizes), [factor.shape] + [third] *...  1.83 us
  transfers between devices with their start and end apart: 4, of which 0 were waited for; matrix products, arithmetic and copies ran while one was open for 0% of the time, Pallas kernels for 6%

profile of v4, /device:TPU:1, one launch (start us, length us, event | category | flops | bytes accessed | tf_op | source)
XLA Modules:
  0.0 89.1 jit_solution(6012460466792648858)
XLA Ops:
  1.3 0.0 copy-start.1
  1.3 0.0 copy-start.2
  1.3 1.7 %pack.1 = f32[16,16,128]{2,1,0:T(8,128)} custom-call(s32[1,1,1]{2,1,0:T(1,128)S(6)} %copy.24.ext, f32[8,16,128]{2,1,0:T(8,128)} %rhs.5, f32[8,16,128]{2,1,0:T(8,128)} %cond.5), custom_call_target="tpu_custom_call" | custom-call | tf_op jit(solution)/shard_map/pack/pallas_call | solution.py:531
  3.0 0.0 copy-start
  3.0 20.8 %all_to_all.20.got = f32[16,16,128]{2,1,0:T(8,128)S(1)} all-to-all(f32[16,16,128]{2,1,0:T(8,128)} %pack.1), channel_id=1, replica_groups=mesh['gx'=4,'gy'=8,'gz'=16] {'gz'}, dimensions={0} | all-to-all | bytes 262144 | tf_op jit(solution)/shard_map/all_to_all | solution.py:532
  23.9 0.0 copy-done.1
  23.9 0.0 copy-done.2
  23.9 0.2 rows.1
  24.0 1.3 %collective-permute-start = (f32[18,8,128]{2,1,0:T(8,128)S(1)}, f32[18,8,128]{2,1,0:T(8,128)S(1)}, u32[]{:S(2)}, u32[]{:S(2)}) collective-permute-start(f32[18,8,128]{2,1,0:T(8,128)S(1)} %get-tuple-element.33), channel_id=1, source_target_pairs={{16,0},{32,16},{48,32},{64,48},{80,64},{96,80},{112,96},{17,1},{33... | collective-permute-start | bytes 221192 | tf_op jit(solution)/shard_map/ppermute | solution.py:524
  25.3 4.0 %collective-permute-start.1 = (f32[18,8,128]{2,1,0:T(8,128)S(1)}, f32[18,8,128]{2,1,0:T(8,128)S(1)}, u32[]{:S(2)}, u32[]{:S(2)}) collective-permute-start(f32[18,8,128]{2,1,0:T(8,128)S(1)} %get-tuple-element.34), channel_id=1, source_target_pairs={{0,16},{16,32},{32,48},{48,64},{64,80},{80,96},{96,112},{1,17},{17... | collective-permute-start | bytes 221192 | tf_op jit(solution)/shard_map/ppermute | solution.py:524
  29.3 18.1 %all_to_all.21.after.gathered = f32[32,1,128]{2,1,0:T(1,128)S(1)} all-to-all(f32[32,1,128]{2,1,0:T(1,128)S(1)} %get-tuple-element.35), channel_id=1, replica_groups=mesh['gx'=4,'gy'=8,'gz'=16] {'gx','gy'}, dimensions={0} | all-to-all | bytes 32768 | tf_op jit(solution)/shard_map/all_to_all | solution.py:537
  47.5 0.0 collective-permute-done.from_high
  47.5 0.0 collective-permute-done.1.from_low
  47.5 1.3 %collective-permute-start.3 = (f32[18,32,128]{2,1,0:T(8,128)S(1)}, f32[18,32,128]{2,1,0:T(8,128)S(1)}, u32[]{:S(2)}, u32[]{:S(2)}) collective-permute-start(f32[18,32,128]{2,1,0:T(8,128)S(1)} %slab.1), channel_id=1, source_target_pairs={{128,0},{256,128},{384,256},{129,1},{257,129},{385,257},{130,2},{2... | collective-permute-start | bytes 884744 | tf_op jit(solution)/shard_map/ppermute | solution.py:524
  48.8 4.0 %collective-permute-start.2 = (f32[18,32,128]{2,1,0:T(8,128)S(1)}, f32[18,32,128]{2,1,0:T(8,128)S(1)}, u32[]{:S(2)}, u32[]{:S(2)}) collective-permute-start(f32[18,32,128]{2,1,0:T(8,128)S(1)} %slab.1), channel_id=1, source_target_pairs={{0,128},{128,256},{256,384},{1,129},{129,257},{257,385},{2,130},{1... | collective-permute-start | bytes 884744 | tf_op jit(solution)/shard_map/ppermute | solution.py:524
  52.8 0.0 copy-done
  52.8 3.3 %diagonal.1 = f32[4,128,128]{2,1,0:T(8,128)S(1)} custom-call(bf16[512,512]{1,0:T(8,128)(2,1)S(1)} %copy-done), custom_call_target="tpu_custom_call" | custom-call | tf_op jit(solution)/shard_map/diagonal/pallas_call | solution.py:544
  56.1 1.8 %coarse.1 = (f32[512,512]{1,0:T(8,128)S(1)}, f32[3,32,256]{2,1,0:T(8,128)S(1)}, f32[3,32,256]{2,1,0:T(8,128)S(1)}, f32[3,32,256]{2,1,0:T(8,128)S(1)}, f32[24,32,...) custom-call(bf16[512,512]{1,0:T(8,128)(2,1)S(1)} %copy-done, ...), custom_call_target="tpu_custom_call" | custom-call | tf_op jit(solution)/shard_map/coarse/pallas_call | solution.py:551
  58.0 0.0 collective-permute-done.3.right
  58.0 0.0 collective-permute-done.2.left
  58.0 5.5 %fields.1 = (f32[24,32,256]{2,1,0:T(8,128)S(1)}, f32[24,32,256]{2,1,0:T(8,128)S(1)}, f32[24,32,256]{2,1,0:T(8,128)S(1)}, f32[24,32,256]{2,1,0:T(8,128)S(1)}, f32...) custom-call(f32[18,32,128]{2,1,0:T(8,128)S(1)} %collective-permute-d, ...), custom_call_target="tpu_custom_call", output_to_operand_aliasing={{0}: (5, {}), {1}: (6, {}), {2}: (7, {}), {3}: (8, {}), {4}... | custom-call | tf_op jit(solution)/shard_map/fields/pallas_call | solution.py:554
  63.5 12.3 %all_to_all.22.part = f32[16,1,128]{2,1,0:T(1,128)S(1)} all-to-all(f32[16,1,128]{2,1,0:T(1,128)S(1)} %get-tuple-element.50), channel_id=1, replica_groups=mesh['gx'=4,'gy'=8,'gz'=16] {'gz'}, dimensions={0} | all-to-all | bytes 16384 | tf_op jit(solution)/shard_map/all_to_all | solution.py:562
  75.8 12.3 %all_to_all.23.gathered = f32[32,1,128]{2,1,0:T(1,128)S(1)} all-to-all(f32[32,1,128]{2,1,0:T(1,128)S(1)} %sum.1), channel_id=1, replica_groups=mesh['gx'=4,'gy'=8,'gz'=16] {'gx','gy'}, dimensions={0} | all-to-all | bytes 32768 | tf_op jit(solution)/shard_map/all_to_all | solution.py:564
  88.1 1.1 %final.1 = (f32[8,16,128]{2,1,0:T(8,128)}, f32[8,16,128]{2,1,0:T(8,128)}) custom-call(f32[32,1,128]{2,1,0:T(1,128)S(1)} %all_to_all.23.gathered, f32[512,512]{1,0:T(8,128)S(1)} %get-tuple-element.51.inv, f32[8,16,128]{2,1,0:T(8,128)S(1)} %get-tuple-element.52.d_in, f32[8,16,128]{2,1,0:T(8,128)S(1)} %get-tuple-element.53.t_in, ...), custom_call_target="tpu_custom_call" | custom-call | tf_op jit(solution)/shard_map/final/pallas_call | solution.py:565
  (2 shorter events, 0.0 us)
Async XLA Ops:
  1.3 22.6 %copy-start.1 = (f32[8,16,128]{2,1,0:T(8,128)S(1)}, f32[8,16,128]{2,1,0:T(8,128)}, u32[]{:S(2)}) copy-start(f32[8,16,128]{2,1,0:T(8,128)} %rhs.5) | copy-start | bytes 196612
  1.3 22.6 %copy-start.2 = (f32[8,16,128]{2,1,0:T(8,128)S(1)}, f32[8,16,128]{2,1,0:T(8,128)}, u32[]{:S(2)}) copy-start(f32[8,16,128]{2,1,0:T(8,128)} %cond.5) | copy-start | bytes 196612
  3.0 49.8 %copy-start = (bf16[512,512]{1,0:T(8,128)(2,1)S(1)}, bf16[512,512]{1,0:T(8,128)(2,1)}, u32[]{:S(2)}) copy-start(bf16[512,512]{1,0:T(8,128)(2,1)} %factor.1) | copy-start | bytes 1572868
  24.0 23.4 %collective-permute-start = (f32[18,8,128]{2,1,0:T(8,128)S(1)}, f32[18,8,128]{2,1,0:T(8,128)S(1)}, u32[]{:S(2)}, u32[]{:S(2)}) collective-permute-start(f32[18,8,128]{2,1,0:T(8,128)S(1)} %get-tuple-element.33), channel_id=1, source_target_pairs={{16,0},{32,16},{48,32},{64,48},{80,64},{96,80},{112,96},{17,1},{33... | collective-permute-start | bytes 221192 | tf_op jit(solution)/shard_map/ppermute | solution.py:524
  25.3 22.1 %collective-permute-start.1 = (f32[18,8,128]{2,1,0:T(8,128)S(1)}, f32[18,8,128]{2,1,0:T(8,128)S(1)}, u32[]{:S(2)}, u32[]{:S(2)}) collective-permute-start(f32[18,8,128]{2,1,0:T(8,128)S(1)} %get-tuple-element.34), channel_id=1, source_target_pairs={{0,16},{16,32},{32,48},{48,64},{64,80},{80,96},{96,112},{1,17},{17... | collective-permute-start | bytes 221192 | tf_op jit(solution)/shard_map/ppermute | solution.py:524
  47.5 10.5 %collective-permute-start.3 = (f32[18,32,128]{2,1,0:T(8,128)S(1)}, f32[18,32,128]{2,1,0:T(8,128)S(1)}, u32[]{:S(2)}, u32[]{:S(2)}) collective-permute-start(f32[18,32,128]{2,1,0:T(8,128)S(1)} %slab.1), channel_id=1, source_target_pairs={{128,0},{256,128},{384,256},{129,1},{257,129},{385,257},{130,2},{2... | collective-permute-start | bytes 884744 | tf_op jit(solution)/shard_map/ppermute | solution.py:524
  48.8 9.2 %collective-permute-start.2 = (f32[18,32,128]{2,1,0:T(8,128)S(1)}, f32[18,32,128]{2,1,0:T(8,128)S(1)}, u32[]{:S(2)}, u32[]{:S(2)}) collective-permute-start(f32[18,32,128]{2,1,0:T(8,128)S(1)} %slab.1), channel_id=1, source_target_pairs={{0,128},{128,256},{256,384},{1,129},{129,257},{257,385},{2,130},{1... | collective-permute-start | bytes 884744 | tf_op jit(solution)/shard_map/ppermute | solution.py:524

commit v5 on v4

--- a/solution.py
+++ b/solution.py
@@ -75,7 +75,7 @@
         msg[z - 1] = a
 
 
-def rows_kernel(rhs, cond, got, zh, to_low, to_high, line):
+def rows_kernel(rhs, cond, got, slab, line):
     nz = got.shape[0]
     z = lax.axis_index("gz")
     low_half = iota((CY, CZ), 1) % 16 < H
@@ -90,26 +90,17 @@
     info = jnp.where(lane == z + 1, pltpu.roll(a[0:8], z + 2, 1), info)
     info = jnp.where(lane < nz, info, 0.0)
     line[...] = jnp.broadcast_to((info[0:1] + roll(info[1:2], SLOT, 1))[None], line.shape)
-    zk = jnp.where(low_half, a, b)
-    zr = jnp.where(low_half, roll(a, H, 1), roll(b, -H, 1))
-    zh[0] = zk
-    zh[1] = zr
-    to_low[0:CX] = cond[:, 0:H, :]
-    to_low[CX : 2 * CX] = rhs[:, 0:H, :]
-    to_low[2 * CX] = zk[0:H]
-    to_low[2 * CX + 1] = zr[0:H]
-    to_high[0:CX] = cond[:, CY - H : CY, :]
-    to_high[CX : 2 * CX] = rhs[:, CY - H : CY, :]
-    to_high[2 * CX] = zk[CY - H : CY]
-    to_high[2 * CX + 1] = zr[CY - H : CY]
-
-
-def slab_kernel(rhs, cond, zh, from_high, from_low, after, slab):
-    slab[0:CX, 0:CY] = cond[...]
-    slab[CX : 2 * CX, 0:CY] = rhs[...]
-    slab[2 * CX : 2 * CX + 2, 0:CY] = zh[...]
-    slab[:, CY : CY + H] = from_high[...]
-    slab[:, CY + H : EY] = from_low[...]
+    slab[0:CX] = cond[...]
+    slab[CX : 2 * CX] = rhs[...]
+    slab[2 * CX] = jnp.where(low_half, a, b)
+    slab[2 * CX + 1] = jnp.where(low_half, roll(a, H, 1), roll(b, -H, 1))
+
+
+def y_kernel(left, own, right, after, to_low, to_high):
+    n = own.shape[0]
+    for i, src in enumerate((left, own, right)):
+        to_low[i * n : (i + 1) * n] = src[:, 0:H]
+        to_high[i * n : (i + 1) * n] = src[:, CY - H : CY]
 
 
 def sum_kernel(part, line):
@@ -224,13 +215,19 @@
     lax.fori_loop(0, count // size, go, 0)
 
 
-def unpack(src, bx, kap, rr, ff):
-    for x in range(CX):
-        at = bx * CX + x
-        kap[at, :, 0:CZ] = src[x]
-        kap[at, :, CZ:EZ] = roll(src[2 * CX], -16 * x, 1)
-        rr[at, :, 0:CZ] = src[CX + x] * ff[bx, :, 0:CZ]
-        rr[at, :, CZ:EZ] = roll(src[2 * CX + 1], -16 * x, 1) * ff[bx, :, CZ:EZ]
+def unpack(src, high, low, bx, kap, rr, ff):
+    n = src.shape[0]
+    for rows, part, at in ((slice(0, CY), src, 0), (slice(CY, CY + H), high, bx * n), (slice(CY + H, EY), low, bx * n)):
+        zk = part[at + 2 * CX]
+        zr = part[at + 2 * CX + 1]
+        f0 = ff[bx, rows, 0:CZ]
+        f1 = ff[bx, rows, CZ:EZ]
+        for x in range(CX):
+            to = bx * CX + x
+            kap[to, rows, 0:CZ] = part[at + x]
+            kap[to, rows, CZ:EZ] = roll(zk, -16 * x, 1)
+            rr[to, rows, 0:CZ] = part[at + CX + x] * f0
+            rr[to, rows, CZ:EZ] = roll(zr, -16 * x, 1) * f1
 
 
 def pooled(s):
@@ -274,10 +271,7 @@
 ROW_PARTS = ((0, 0), (8, 0), (16, 1), (24, -1))
 
 
-def coarse_kernel(
-    nx, ny, nz, factor, diagonal, gathered, slab,
-    inv, ff, f1, fy, kap, rr, cx, cy, cz, i0, k1, i1, u1,
-):
+def coarse_kernel(nx, ny, nz, factor, diagonal, gathered, inv, ff, f1, fy):
     inverse_of(factor, diagonal, inv)
     lane8 = iota((8, CZ), 1)
     lane8f = lane8.astype(F32)
@@ -300,50 +294,37 @@
             fy[bx, r : r + 8, CZ:EZ] = m1 * jnp.where(lane8 < CZ // 2, v[1], v[-1])
 
 
-    unpack(slab, 1, kap, rr, ff)
-    for x in range(CX, 2 * CX):
-        coef_yz(x, kap, cy, cz)
-        if x < 2 * CX - 1:
-            coef_x(x, kap, cx)
-    for x in range(CX + 1, 2 * CX - 1):
-        inverse_fine(x, cx, cy, cz, i0, rr, u1, ff)
-    for i in range(CX // 2, CX):
-        coarse_cond(i, kap, k1)
-    for i in range(CX // 2 + 1, CX - 1):
-        inverse_coarse(i, k1, i1, f1)
-
-
-def main_kernel(
-    left, right, ff, f1, fy, *refs
-):
-    (kap, rr, cx, cy, cz, i0, k1, i1, u1) = refs[9:18]
-    (d_out, t_out, n_out, an_out, r_out, e0_out, ey_out, ez_out, ex_out, f_out, msg) = refs[18:29]
-    u2, dd, tt = refs[29:]
-    unpack(left, 0, kap, rr, ff)
-    unpack(right, 2, kap, rr, ff)
-    coef_x(2 * CX - 1, kap, cx)
-
-    def coefs(us):
-        for u in us:
-            for x in (u, u + 2 * CX):
-                coef_yz(x, kap, cy, cz)
-            coef_x(u, kap, cx)
-            coef_x(jnp.minimum(u + 2 * CX, EX - 2), kap, cx)
-
-    groups(0, CX, coefs)
-
-    def inverses(us):
-        for u in us:
-            for x in (u, u + 2 * CX - 2):
-                inverse_fine(x, cx, cy, cz, i0, rr, u1, ff)
-
-    groups(1, CX + 1, inverses)
-    for i in range(CX // 2):
-        for j in (i, i + CX):
-            coarse_cond(j, kap, k1)
-    for i in range(1, CX // 2 + 1):
-        for j in (i, i + CX - 2):
-            inverse_coarse(j, k1, i1, f1)
+def main_kernel(left, own, right, high, low, ff, f1, fy, *refs):
+    (d_out, t_out, n_out, an_out, r_out, e0_out, ey_out, ez_out, ex_out, f_out, msg) = refs[:11]
+    kap, rr, cx, cy, cz, i0, u1, u2, dd, tt, k1, i1 = refs[11:]
+    for bx, src in enumerate((left, own, right)):
+        unpack(src, high, low, bx, kap, rr, ff)
+
+    def coefs(xs):
+        for x in xs:
+            k = kap[x]
+            cx[x] = 0.5 * (k + kap[jnp.minimum(x + 1, EX - 1)])
+            coef_yz(x, kap, cy, cz)
+
+    groups(0, EX, coefs)
+
+    def inverses(xs):
+        for x in xs:
+            inverse_fine(x, cx, cy, cz, i0, rr, u1, ff)
+
+    groups(1, EX - 1, inverses)
+
+    def conds(xs):
+        for i in xs:
+            coarse_cond(i, kap, k1)
+
+    groups(0, EX // 2, conds)
+
+    def coarse_inverses(xs):
+        for i in xs:
+            inverse_coarse(i, k1, i1, f1)
+
+    groups(1, EX // 2 - 1, coarse_inverses)
 
     def images(u, xs, masked=True):
         c = [u[xs[0] - 1]] + [u[x] for x in xs] + [u[xs[-1] + 1]]
@@ -531,34 +512,31 @@
     msg = call(pack_kernel, [(nz, CY, CZ)], 3, name="pack", mib=PACK_MIB)(extents, right_side, conductance)[0]
     got = lax.all_to_all(msg, "gz", 0, 0, tiled=True)
     depth = 2 * CX + 2
-    zh, to_low, to_high, line = call(
-        rows_kernel, [(2, CY, CZ), (depth, H, CZ), (depth, H, CZ), (nx * ny, 1, CZ)], 3, name="rows"
-    )(right_side, conductance, got)
+    depth = 2 * CX + 2
+    slab, line = call(rows_kernel, [(depth, CY, CZ), (nx * ny, 1, CZ)], 3, name="rows")(right_side, conductance, got)
+    x_high, x_low = exchange("gx", slab, slab)
     first = lax.all_to_all(line, ("gx", "gy"), 0, 0, tiled=True)
+    to_low, to_high = call(
+        y_kernel, [(3 * depth, H, CZ)] * 2, 4, in_specs=[VMEM] * 3 + [any_space], name="faces"
+    )(x_low, slab, x_high, first)
+    to_low, to_high, factor = lax.optimization_barrier((to_low, to_high, coarse_factor))
     y_high, y_low = exchange("gy", to_low, to_high)
-    slab = call(
-        slab_kernel, [(depth, EY, CZ)], 6, in_specs=[VMEM] * 5 + [any_space], name="slab"
-    )(right_side, conductance, zh, y_high, y_low, first)[0]
-    slab, factor = lax.optimization_barrier((slab, coarse_factor))
     nb = factor.shape[0] // CZ
     diagonal = call(diagonal_kernel, [(nb, CZ, CZ)], 1, name="diagonal")(factor)[0]
-    x_high, x_low = exchange("gx", slab, slab)
     block = (CX, CY, CZ)
     wide = (EX, EY, EZ)
     half = (EX // 2, EY, EZ)
     third = (3, EY, EZ)
-    arrays = [wide] * 6 + [half] * 2 + [wide]
-    inv, ff, f1, fy, *fields = call(
-        functools.partial(coarse_kernel, *sizes), [factor.shape] + [third] * 3 + arrays, 4, name="coarse"
-    )(factor, diagonal, first, slab)
+    inv, ff, f1, fy = call(
+        functools.partial(coarse_kernel, *sizes), [factor.shape] + [third] * 3, 3, name="coarse"
+    )(factor, diagonal, first)
     outs = call(
         main_kernel,
-        arrays + [block] * 8 + [(2, CY, CZ), (CY, CZ), (nz, 1, CZ)],
-        14,
-        scratch=[wide] * 3,
-        aliases={5 + i: i for i in range(9)},
+        [block] * 8 + [(2, CY, CZ), (CY, CZ), (nz, 1, CZ)],
+        8,
+        scratch=[wide] * 10 + [half] * 2,
         name="fields",
-    )(x_low, x_high, ff, f1, fy, *fields)[9:]
+    )(x_low, slab, x_high, y_high, y_low, ff, f1, fy)
     part = lax.all_to_all(outs[-1], "gz", 0, 0, tiled=True)
     line = call(sum_kernel, [(nx * ny, 1, CZ)], 1, name="sum")(part)[0]
     second = lax.all_to_all(line, ("gx", "gy"), 0, 0, tiled=True)

time: 89.6 us -> 91.5 us (1.021)
  blocking collectives: 63.5 us -> 65.1 us
    all_to_all x1, blocking collectives: 12.3 us -> 13.9 us  [on_device(): second = lax.all_to_all(line, ('gx', 'gy'), 0, 0, tiled=True)]
where the time goes in v5:
time: 91.5 us; the launch traced here: 91 us
  blocking collectives  65.1 us (71%)
  Pallas kernels  13.9 us (15%)
  starting transfers between devices  10.6 us (12%)
  between operations  1.38 us (2%)
    all_to_all x1, blocking collectives, on_device(): got = lax.all_to_all(msg, 'gz', 0, 0, tiled=True)  20.8 us
    all_to_all x1, blocking collectives, on_device(): first = lax.all_to_all(line, ('gx', 'gy'), 0, 0, tiled=True)  18.1 us
    all_to_all x1, blocking collectives, on_device(): second = lax.all_to_all(line, ('gx', 'gy'), 0, 0, tiled=True)  13.9 us
    all_to_all x1, blocking collectives, on_device(): part = lax.all_to_all(outs[-1], 'gz', 0, 0, tiled=True)  12.3 us
    ppermute x4, starting transfers between devices, exchange(): return (lax.ppermute(to_low, axis, down), lax.ppermute(to_high, axis, up))  10.6 us
    pallas_call x1, Pallas kernels, on_device(): call(main_kernel, [block] * 8 + [(2, CY, CZ), (CY, CZ), (nz, 1, CZ)], 8,...  5.89 us
    pallas_call x1, Pallas kernels, on_device(): call(diagonal_kernel, [(nb, CZ, CZ)], 1, name='diagonal')(factor)[0]  3.3 us
  transfers between devices with their start and end apart: 4, of which 0 were waited for; matrix products, arithmetic and copies ran while one was open for 0% of the time, Pallas kernels for 6%

profile of v5, /device:TPU:1, one launch (start us, length us, event | category | flops | bytes accessed | tf_op | source)
XLA Modules:
  0.0 91.0 jit_solution(2092925600149346533)
XLA Ops:
  1.3 0.0 copy-start.1
  1.3 0.0 copy-start.2
  1.3 1.7 %pack.1 = f32[16,16,128]{2,1,0:T(8,128)} custom-call(s32[1,1,1]{2,1,0:T(1,128)S(6)} %copy.6.ext, f32[8,16,128]{2,1,0:T(8,128)} %rhs.3, f32[8,16,128]{2,1,0:T(8,128)} %cond.3), custom_call_target="tpu_custom_call" | custom-call | tf_op jit(solution)/shard_map/pack/pallas_call | solution.py:512
  3.0 0.0 copy-start
  3.0 20.8 %all_to_all.20.got = f32[16,16,128]{2,1,0:T(8,128)S(1)} all-to-all(f32[16,16,128]{2,1,0:T(8,128)} %pack.1), channel_id=1, replica_groups=mesh['gx'=4,'gy'=8,'gz'=16] {'gz'}, dimensions={0} | all-to-all | bytes 262144 | tf_op jit(solution)/shard_map/all_to_all | solution.py:513
  23.9 0.0 copy-done.1
  23.9 0.0 copy-done.2
  23.9 0.2 rows.1
  24.0 1.3 %collective-permute-start.1 = (f32[18,16,128]{2,1,0:T(8,128)S(1)}, f32[18,16,128]{2,1,0:T(8,128)S(1)}, u32[]{:S(2)}, u32[]{:S(2)}) collective-permute-start(f32[18,16,128]{2,1,0:T(8,128)S(1)} %get-tuple-element.24.own), channel_id=1, source_target_pairs={{128,0},{256,128},{384,256},{129,1},{257,129},{385,257},{130,2},{2... | collective-permute-start | bytes 442376 | tf_op jit(solution)/shard_map/ppermute | solution.py:505
  25.3 4.0 %collective-permute-start = (f32[18,16,128]{2,1,0:T(8,128)S(1)}, f32[18,16,128]{2,1,0:T(8,128)S(1)}, u32[]{:S(2)}, u32[]{:S(2)}) collective-permute-start(f32[18,16,128]{2,1,0:T(8,128)S(1)} %get-tuple-element.24.own), channel_id=1, source_target_pairs={{0,128},{128,256},{256,384},{1,129},{129,257},{257,385},{2,130},{1... | collective-permute-start | bytes 442376 | tf_op jit(solution)/shard_map/ppermute | solution.py:505
  29.3 18.1 %all_to_all.21.after.gathered = f32[32,1,128]{2,1,0:T(1,128)S(1)} all-to-all(f32[32,1,128]{2,1,0:T(1,128)S(1)} %get-tuple-element.25), channel_id=1, replica_groups=mesh['gx'=4,'gy'=8,'gz'=16] {'gx','gy'}, dimensions={0} | all-to-all | bytes 32768 | tf_op jit(solution)/shard_map/all_to_all | solution.py:518
  47.5 0.0 collective-permute-done.1.right
  47.5 0.0 collective-permute-done.left
  47.5 1.3 %collective-permute-start.2 = (f32[54,8,128]{2,1,0:T(8,128)S(1)}, f32[54,8,128]{2,1,0:T(8,128)S(1)}, u32[]{:S(2)}, u32[]{:S(2)}) collective-permute-start(f32[54,8,128]{2,1,0:T(8,128)S(1)} %get-tuple-element.28), channel_id=1, source_target_pairs={{16,0},{32,16},{48,32},{64,48},{80,64},{96,80},{112,96},{17,1},{33... | collective-permute-start | bytes 663560 | tf_op jit(solution)/shard_map/ppermute | solution.py:505
  48.8 4.0 %collective-permute-start.3 = (f32[54,8,128]{2,1,0:T(8,128)S(1)}, f32[54,8,128]{2,1,0:T(8,128)S(1)}, u32[]{:S(2)}, u32[]{:S(2)}) collective-permute-start(f32[54,8,128]{2,1,0:T(8,128)S(1)} %get-tuple-element.29), channel_id=1, source_target_pairs={{0,16},{16,32},{32,48},{48,64},{64,80},{80,96},{96,112},{1,17},{17... | collective-permute-start | bytes 663560 | tf_op jit(solution)/shard_map/ppermute | solution.py:505
  52.8 0.0 copy-done
  52.8 3.3 %diagonal.1 = f32[4,128,128]{2,1,0:T(8,128)S(1)} custom-call(bf16[512,512]{1,0:T(8,128)(2,1)S(1)} %copy-done), custom_call_target="tpu_custom_call" | custom-call | tf_op jit(solution)/shard_map/diagonal/pallas_call | solution.py:525
  56.1 1.7 %coarse.1 = (f32[512,512]{1,0:T(8,128)S(1)}, f32[3,32,256]{2,1,0:T(8,128)S(1)}, f32[3,32,256]{2,1,0:T(8,128)S(1)}, f32[3,32,256]{2,1,0:T(8,128)S(1)}) custom-call(bf16[512,512]{1,0:T(8,128)(2,1)S(1)} %copy-done, f32[4,128,128]{2,1,0:T(8,128)S(1)} %diagonal.1, f32[32,1,128]{2,1,0:T(1,128)S(1)} %all_to_all.21.after.gathered), custom_call_target="tpu_custom_call" | custom-call | tf_op jit(solution)/shard_map/coarse/pallas_call | solution.py:530
  57.9 0.0 collective-permute-done.2.high
  57.9 0.0 collective-permute-done.3.low
  57.9 5.9 %fields.1 = (f32[8,16,128]{2,1,0:T(8,128)S(1)}, f32[8,16,128]{2,1,0:T(8,128)S(1)}, f32[8,16,128]{2,1,0:T(8,128)S(1)}, f32[8,16,128]{2,1,0:T(8,128)S(1)}, f32[8,1...) custom-call(f32[18,16,128]{2,1,0:T(8,128)S(1)} %collective-permute-d, ...), custom_call_target="tpu_custom_call" | custom-call | tf_op jit(solution)/shard_map/fields/pallas_call | solution.py:533
  63.8 12.3 %all_to_all.22.part = f32[16,1,128]{2,1,0:T(1,128)S(1)} all-to-all(f32[16,1,128]{2,1,0:T(1,128)S(1)} %get-tuple-element.34), channel_id=1, replica_groups=mesh['gx'=4,'gy'=8,'gz'=16] {'gz'}, dimensions={0} | all-to-all | bytes 16384 | tf_op jit(solution)/shard_map/all_to_all | solution.py:540
  76.1 13.9 %all_to_all.23.gathered = f32[32,1,128]{2,1,0:T(1,128)S(1)} all-to-all(f32[32,1,128]{2,1,0:T(1,128)S(1)} %sum.1), channel_id=1, replica_groups=mesh['gx'=4,'gy'=8,'gz'=16] {'gx','gy'}, dimensions={0} | all-to-all | bytes 32768 | tf_op jit(solution)/shard_map/all_to_all | solution.py:542
  89.9 1.1 %final.1 = (f32[8,16,128]{2,1,0:T(8,128)}, f32[8,16,128]{2,1,0:T(8,128)}) custom-call(f32[32,1,128]{2,1,0:T(1,128)S(1)} %all_to_all.23.gathered, f32[512,512]{1,0:T(8,128)S(1)} %get-tuple-element.35.inv, f32[8,16,128]{2,1,0:T(8,128)S(1)} %get-tuple-element.36.d_in, f32[8,16,128]{2,1,0:T(8,128)S(1)} %get-tuple-element.37.t_in, ...), custom_call_target="tpu_custom_call" | custom-call | tf_op jit(solution)/shard_map/final/pallas_call | solution.py:543
  (2 shorter events, 0.1 us)
Async XLA Ops:
  1.3 22.6 %copy-start.1 = (f32[8,16,128]{2,1,0:T(8,128)S(1)}, f32[8,16,128]{2,1,0:T(8,128)}, u32[]{:S(2)}) copy-start(f32[8,16,128]{2,1,0:T(8,128)} %rhs.3) | copy-start | bytes 196612
  1.3 22.6 %copy-start.2 = (f32[8,16,128]{2,1,0:T(8,128)S(1)}, f32[8,16,128]{2,1,0:T(8,128)}, u32[]{:S(2)}) copy-start(f32[8,16,128]{2,1,0:T(8,128)} %cond.3) | copy-start | bytes 196612
  3.0 49.8 %copy-start = (bf16[512,512]{1,0:T(8,128)(2,1)S(1)}, bf16[512,512]{1,0:T(8,128)(2,1)}, u32[]{:S(2)}) copy-start(bf16[512,512]{1,0:T(8,128)(2,1)} %factor.1) | copy-start | bytes 1572868
  24.0 23.4 %collective-permute-start.1 = (f32[18,16,128]{2,1,0:T(8,128)S(1)}, f32[18,16,128]{2,1,0:T(8,128)S(1)}, u32[]{:S(2)}, u32[]{:S(2)}) collective-permute-start(f32[18,16,128]{2,1,0:T(8,128)S(1)} %get-tuple-element.24.own), channel_id=1, source_target_pairs={{128,0},{256,128},{384,256},{129,1},{257,129},{385,257},{130,2},{2... | collective-permute-start | bytes 442376 | tf_op jit(solution)/shard_map/ppermute | solution.py:505
  25.3 22.1 %collective-permute-start = (f32[18,16,128]{2,1,0:T(8,128)S(1)}, f32[18,16,128]{2,1,0:T(8,128)S(1)}, u32[]{:S(2)}, u32[]{:S(2)}) collective-permute-start(f32[18,16,128]{2,1,0:T(8,128)S(1)} %get-tuple-element.24.own), channel_id=1, source_target_pairs={{0,128},{128,256},{256,384},{1,129},{129,257},{257,385},{2,130},{1... | collective-permute-start | bytes 442376 | tf_op jit(solution)/shard_map/ppermute | solution.py:505
  47.5 10.3 %collective-permute-start.2 = (f32[54,8,128]{2,1,0:T(8,128)S(1)}, f32[54,8,128]{2,1,0:T(8,128)S(1)}, u32[]{:S(2)}, u32[]{:S(2)}) collective-permute-start(f32[54,8,128]{2,1,0:T(8,128)S(1)} %get-tuple-element.28), channel_id=1, source_target_pairs={{16,0},{32,16},{48,32},{64,48},{80,64},{96,80},{112,96},{17,1},{33... | collective-permute-start | bytes 663560 | tf_op jit(solution)/shard_map/ppermute | solution.py:505
  48.8 9.1 %collective-permute-start.3 = (f32[54,8,128]{2,1,0:T(8,128)S(1)}, f32[54,8,128]{2,1,0:T(8,128)S(1)}, u32[]{:S(2)}, u32[]{:S(2)}) collective-permute-start(f32[54,8,128]{2,1,0:T(8,128)S(1)} %get-tuple-element.29), channel_id=1, source_target_pairs={{0,16},{16,32},{32,48},{48,64},{64,80},{80,96},{96,112},{1,17},{17... | collective-permute-start | bytes 663560 | tf_op jit(solution)/shard_map/ppermute | solution.py:505

commit v6 on v4

--- a/solution.py
+++ b/solution.py
@@ -8,7 +8,7 @@
 from jax.sharding import PartitionSpec as P
 
 F32 = jnp.float32
-PACK_MIB = 60
+PACK_MIB = 48
 OMEGA = 0.8
 CX, CY, CZ = 8, 16, 128
 CELLS = CX * CY * CZ
@@ -104,12 +104,49 @@
     to_high[2 * CX + 1] = zr[CY - H : CY]
 
 
-def slab_kernel(rhs, cond, zh, from_high, from_low, after, slab):
+def x_tiles():
+    at = 0
+    cond, rhs = {}, {}
+    for layer in range(1, H + 1):
+        for part, whole, none in ((cond, 5, 9), (rhs, 4, 8)):
+            n = 4 if layer <= whole else 3 if layer < none else 0
+            part[layer] = (at, n)
+            at += n
+    return cond, rhs, at
+
+
+X_TILES = x_tiles()[2] + 8
+
+
+def slab_kernel(rhs, cond, zh, from_high, from_low, after, slab, to_low, to_high):
     slab[0:CX, 0:CY] = cond[...]
     slab[CX : 2 * CX, 0:CY] = rhs[...]
     slab[2 * CX : 2 * CX + 2, 0:CY] = zh[...]
     slab[:, CY : CY + H] = from_high[...]
     slab[:, CY + H : EY] = from_low[...]
+    in_cond, in_rhs, z_at = x_tiles()
+    near = iota((8, CZ), 0) < 4
+    for msg, flip in ((to_low, False), (to_high, True)):
+        for x in range(CX):
+            layer = H - x if flip else x + 1
+            for part, base, src in ((in_cond, 0, cond), (in_rhs, CX, rhs)):
+                at, n = part[layer]
+                if n == 0:
+                    continue
+                msg[at] = src[x, 0:8]
+                msg[at + 1] = src[x, 8:16]
+                high, low = from_high[base + x], from_low[base + x]
+                if n == 4:
+                    msg[at + 2] = high
+                    msg[at + 3] = low
+                else:
+                    msg[at + 2] = jnp.where(near, high, low)
+        for i in range(2):
+            at = z_at + 4 * i
+            msg[at] = zh[i, 0:8]
+            msg[at + 1] = zh[i, 8:16]
+            msg[at + 2] = from_high[2 * CX + i]
+            msg[at + 3] = from_low[2 * CX + i]
 
 
 def sum_kernel(part, line):
@@ -231,6 +268,25 @@
         kap[at, :, CZ:EZ] = roll(src[2 * CX], -16 * x, 1)
         rr[at, :, 0:CZ] = src[CX + x] * ff[bx, :, 0:CZ]
         rr[at, :, CZ:EZ] = roll(src[2 * CX + 1], -16 * x, 1) * ff[bx, :, CZ:EZ]
+
+
+def unpack_message(msg, flip, bx, kap, rr, ff):
+    in_cond, in_rhs, z_at = x_tiles()
+    for tile in range(4):
+        rows = slice(8 * tile, 8 * tile + 8)
+        for part, to, i in ((in_cond, kap, 0), (in_rhs, rr, 1)):
+            packed = msg[z_at + 4 * i + tile]
+            for x in range(CX):
+                at, n = part[H - x if flip else x + 1]
+                if n == 0:
+                    continue
+                v = msg[at + min(tile, n - 1)]
+                q = roll(packed, -16 * x, 1)
+                if i:
+                    v = v * ff[bx, rows, 0:CZ]
+                    q = q * ff[bx, rows, CZ:EZ]
+                to[bx * CX + x, rows, 0:CZ] = v
+                to[bx * CX + x, rows, CZ:EZ] = q
 
 
 def pooled(s):
@@ -319,8 +375,8 @@
     (kap, rr, cx, cy, cz, i0, k1, i1, u1) = refs[9:18]
     (d_out, t_out, n_out, an_out, r_out, e0_out, ey_out, ez_out, ex_out, f_out, msg) = refs[18:29]
     u2, dd, tt = refs[29:]
-    unpack(left, 0, kap, rr, ff)
-    unpack(right, 2, kap, rr, ff)
+    unpack_message(left, True, 0, kap, rr, ff)
+    unpack_message(right, False, 2, kap, rr, ff)
     coef_x(2 * CX - 1, kap, cx)
 
     def coefs(us):
@@ -536,13 +592,13 @@
     )(right_side, conductance, got)
     first = lax.all_to_all(line, ("gx", "gy"), 0, 0, tiled=True)
     y_high, y_low = exchange("gy", to_low, to_high)
-    slab = call(
-        slab_kernel, [(depth, EY, CZ)], 6, in_specs=[VMEM] * 5 + [any_space], name="slab"
-    )(right_side, conductance, zh, y_high, y_low, first)[0]
-    slab, factor = lax.optimization_barrier((slab, coarse_factor))
+    slab, to_low, to_high = call(
+        slab_kernel, [(depth, EY, CZ)] + [(X_TILES, 8, CZ)] * 2, 6, in_specs=[VMEM] * 5 + [any_space], name="slab"
+    )(right_side, conductance, zh, y_high, y_low, first)
+    to_low, to_high, factor = lax.optimization_barrier((to_low, to_high, coarse_factor))
     nb = factor.shape[0] // CZ
     diagonal = call(diagonal_kernel, [(nb, CZ, CZ)], 1, name="diagonal")(factor)[0]
-    x_high, x_low = exchange("gx", slab, slab)
+    x_high, x_low = exchange("gx", to_low, to_high)
     block = (CX, CY, CZ)
     wide = (EX, EY, EZ)
     half = (EX // 2, EY, EZ)

time: 89.6 us -> 88.4 us (0.987)
  Pallas kernels: 13.6 us -> 11.8 us
  starting transfers between devices: 10.6 us -> 8.83 us
  local copies, waits for them, and re-layouts: 0.01 us -> 1.68 us
  waiting for transfers between devices: 0.01 us -> 1.01 us
    ppermute x4, starting transfers between devices: 10.6 us -> 8.83 us  [exchange(): return (lax.ppermute(to_low, axis, down), lax.ppermute(to_high, axis, up))]
    unnamed x6, local copies, waits for them, and re-layouts: 0.01 us -> 1.68 us
    pallas_call x1, Pallas kernels: 1.73 us -> 0.17 us  [on_device(): call(pack_kernel, [(nz, CY, CZ)], 3, name='pack', mib=PACK_MIB)]
    ppermute x4, waiting for transfers between devices: 0.01 us -> 1.01 us  [exchange(): return (lax.ppermute(to_low, axis, down), lax.ppermute(to_high, axis, up))]
  transfers between devices with their start and end apart: 4 -> 4, of which waited for: 0 -> 1; matrix products, arithmetic and copies ran while one was open for 0% -> 0% of each run, Pallas kernels for 6% -> 6%
where the time goes in v6:
time: 88.4 us; the launch traced here: 88 us
  blocking collectives  63.3 us (72%)
  Pallas kernels  11.8 us (13%)
  starting transfers between devices  8.83 us (10%)
  local copies, waits for them, and re-layouts  1.68 us (2%)
  between operations  1.38 us (2%)
  waiting for transfers between devices  1.01 us (1%)
    all_to_all x1, blocking collectives, on_device(): got = lax.all_to_all(msg, 'gz', 0, 0, tiled=True)  20.5 us
    all_to_all x1, blocking collectives, on_device(): first = lax.all_to_all(line, ('gx', 'gy'), 0, 0, tiled=True)  18.1 us
    all_to_all x1, blocking collectives, on_device(): part = lax.all_to_all(outs[-1], 'gz', 0, 0, tiled=True)  12.7 us
    all_to_all x1, blocking collectives, on_device(): second = lax.all_to_all(line, ('gx', 'gy'), 0, 0, tiled=True)  11.9 us
    ppermute x4, starting transfers between devices, exchange(): return (lax.ppermute(to_low, axis, down), lax.ppermute(to_high, axis, up))  8.83 us
    pallas_call x1, Pallas kernels, on_device(): call(main_kernel, arrays + [block] * 8 + [(2, CY, CZ), (CY, CZ), (nz, 1,...  5.17 us
    pallas_call x1, Pallas kernels, on_device(): call(diagonal_kernel, [(nb, CZ, CZ)], 1, name='diagonal')(factor)[0]  3.31 us
    pallas_call x1, Pallas kernels, on_device(): call(functools.partial(coarse_kernel, *sizes), [factor.shape] + [third] *...  1.8 us
  transfers between devices with their start and end apart: 4, of which 1 were waited for; matrix products, arithmetic and copies ran while one was open for 0% of the time, Pallas kernels for 6%

profile of v6, /device:TPU:1, one launch (start us, length us, event | category | flops | bytes accessed | tf_op | source)
XLA Modules:
  0.0 88.0 jit_solution(3646951061489597070)
XLA Ops:
  1.3 0.0 copy-start.1
  1.3 0.8 copy-done.1
  2.1 0.0 copy-start.2
  2.1 0.8 copy-done.2
  3.0 0.0 copy-start
  3.0 0.2 pack.1
  3.1 20.5 %all_to_all.20.got = f32[16,16,128]{2,1,0:T(8,128)S(1)} all-to-all(f32[16,16,128]{2,1,0:T(8,128)S(1)} %pack.1), channel_id=1, replica_groups=mesh['gx'=4,'gy'=8,'gz'=16] {'gz'}, dimensions={0} | all-to-all | bytes 262144 | tf_op jit(solution)/shard_map/all_to_all | solution.py:588
  23.6 0.2 rows.1
  23.8 1.3 %collective-permute-start = (f32[18,8,128]{2,1,0:T(8,128)S(1)}, f32[18,8,128]{2,1,0:T(8,128)S(1)}, u32[]{:S(2)}, u32[]{:S(2)}) collective-permute-start(f32[18,8,128]{2,1,0:T(8,128)S(1)} %get-tuple-element.37), channel_id=1, source_target_pairs={{16,0},{32,16},{48,32},{64,48},{80,64},{96,80},{112,96},{17,1},{33... | collective-permute-start | bytes 221192 | tf_op jit(solution)/shard_map/ppermute | solution.py:580
  25.1 4.0 %collective-permute-start.1 = (f32[18,8,128]{2,1,0:T(8,128)S(1)}, f32[18,8,128]{2,1,0:T(8,128)S(1)}, u32[]{:S(2)}, u32[]{:S(2)}) collective-permute-start(f32[18,8,128]{2,1,0:T(8,128)S(1)} %get-tuple-element.38), channel_id=1, source_target_pairs={{0,16},{16,32},{32,48},{48,64},{64,80},{80,96},{96,112},{1,17},{17... | collective-permute-start | bytes 221192 | tf_op jit(solution)/shard_map/ppermute | solution.py:580
  29.1 18.1 %all_to_all.21.after.gathered = f32[32,1,128]{2,1,0:T(1,128)S(1)} all-to-all(f32[32,1,128]{2,1,0:T(1,128)S(1)} %get-tuple-element.39), channel_id=1, replica_groups=mesh['gx'=4,'gy'=8,'gz'=16] {'gx','gy'}, dimensions={0} | all-to-all | bytes 32768 | tf_op jit(solution)/shard_map/all_to_all | solution.py:593
  47.2 0.0 collective-permute-done.from_high
  47.2 0.0 collective-permute-done.1.from_low
  47.3 0.1 slab.1
  47.3 2.3 %collective-permute-start.2 = (f32[62,8,128]{2,1,0:T(8,128)S(1)}, f32[62,8,128]{2,1,0:T(8,128)S(1)}, u32[]{:S(2)}, u32[]{:S(2)}) collective-permute-start(f32[62,8,128]{2,1,0:T(8,128)S(1)} %get-tuple-element.42), channel_id=1, source_target_pairs={{0,128},{128,256},{256,384},{1,129},{129,257},{257,385},{2,130},{1... | collective-permute-start | bytes 761864 | tf_op jit(solution)/shard_map/ppermute | solution.py:580
  49.6 1.3 %collective-permute-start.3 = (f32[62,8,128]{2,1,0:T(8,128)S(1)}, f32[62,8,128]{2,1,0:T(8,128)S(1)}, u32[]{:S(2)}, u32[]{:S(2)}) collective-permute-start(f32[62,8,128]{2,1,0:T(8,128)S(1)} %get-tuple-element.43), channel_id=1, source_target_pairs={{128,0},{256,128},{384,256},{129,1},{257,129},{385,257},{130,2},{2... | collective-permute-start | bytes 761864 | tf_op jit(solution)/shard_map/ppermute | solution.py:580
  50.9 0.0 copy-done
  50.9 3.3 %diagonal.1 = f32[4,128,128]{2,1,0:T(8,128)S(1)} custom-call(bf16[512,512]{1,0:T(8,128)(2,1)S(1)} %copy-done), custom_call_target="tpu_custom_call" | custom-call | tf_op jit(solution)/shard_map/diagonal/pallas_call | solution.py:600
  54.2 1.8 %coarse.1 = (f32[512,512]{1,0:T(8,128)S(1)}, f32[3,32,256]{2,1,0:T(8,128)S(1)}, f32[3,32,256]{2,1,0:T(8,128)S(1)}, f32[3,32,256]{2,1,0:T(8,128)S(1)}, f32[24,32,...) custom-call(bf16[512,512]{1,0:T(8,128)(2,1)S(1)} %copy-done, ...), custom_call_target="tpu_custom_call" | custom-call | tf_op jit(solution)/shard_map/coarse/pallas_call | solution.py:607
  56.0 0.0 collective-permute-done.2.left
  56.0 1.0 %collective-permute-done.3.right = f32[62,8,128]{2,1,0:T(8,128)S(1)} collective-permute-done((f32[62,8,128]{2,1,0:T(8,128)S(1)}, f32[62,8,128]{2,1,0:T(8,128)S(1)}, u32[]{:S(2)}, u32[]{:S(2)}) %collective-permute-start.3) | collective-permute-done | bytes 253984 | tf_op jit(solution)/shard_map/ppermute | solution.py:580
  57.0 5.2 %fields.1 = (f32[24,32,256]{2,1,0:T(8,128)S(1)}, f32[24,32,256]{2,1,0:T(8,128)S(1)}, f32[24,32,256]{2,1,0:T(8,128)S(1)}, f32[24,32,256]{2,1,0:T(8,128)S(1)}, f32...) custom-call(f32[62,8,128]{2,1,0:T(8,128)S(1)} %collective-permute-do, ...), custom_call_target="tpu_custom_call", output_to_operand_aliasing={{0}: (5, {}), {1}: (6, {}), {2}: (7, {}), {3}: (8, {}), {4}... | custom-call | tf_op jit(solution)/shard_map/fields/pallas_call | solution.py:610
  62.2 12.7 %all_to_all.22.part = f32[16,1,128]{2,1,0:T(1,128)S(1)} all-to-all(f32[16,1,128]{2,1,0:T(1,128)S(1)} %get-tuple-element.58), channel_id=1, replica_groups=mesh['gx'=4,'gy'=8,'gz'=16] {'gz'}, dimensions={0} | all-to-all | bytes 16384 | tf_op jit(solution)/shard_map/all_to_all | solution.py:618
  75.0 11.9 %all_to_all.23.gathered = f32[32,1,128]{2,1,0:T(1,128)S(1)} all-to-all(f32[32,1,128]{2,1,0:T(1,128)S(1)} %sum.1), channel_id=1, replica_groups=mesh['gx'=4,'gy'=8,'gz'=16] {'gx','gy'}, dimensions={0} | all-to-all | bytes 32768 | tf_op jit(solution)/shard_map/all_to_all | solution.py:620
  86.9 1.1 %final.1 = (f32[8,16,128]{2,1,0:T(8,128)}, f32[8,16,128]{2,1,0:T(8,128)}) custom-call(f32[32,1,128]{2,1,0:T(1,128)S(1)} %all_to_all.23.gathered, f32[512,512]{1,0:T(8,128)S(1)} %get-tuple-element.59.inv, f32[8,16,128]{2,1,0:T(8,128)S(1)} %get-tuple-element.60.d_in, f32[8,16,128]{2,1,0:T(8,128)S(1)} %get-tuple-element.61.t_in, ...), custom_call_target="tpu_custom_call" | custom-call | tf_op jit(solution)/shard_map/final/pallas_call | solution.py:621
  (1 shorter events, 0.0 us)
Async XLA Ops:
  1.3 0.8 copy-start.1
  2.1 0.8 copy-start.2
  3.0 47.9 %copy-start = (bf16[512,512]{1,0:T(8,128)(2,1)S(1)}, bf16[512,512]{1,0:T(8,128)(2,1)}, u32[]{:S(2)}) copy-start(bf16[512,512]{1,0:T(8,128)(2,1)} %factor.1) | copy-start | bytes 1572868
  23.8 23.4 %collective-permute-start = (f32[18,8,128]{2,1,0:T(8,128)S(1)}, f32[18,8,128]{2,1,0:T(8,128)S(1)}, u32[]{:S(2)}, u32[]{:S(2)}) collective-permute-start(f32[18,8,128]{2,1,0:T(8,128)S(1)} %get-tuple-element.37), channel_id=1, source_target_pairs={{16,0},{32,16},{48,32},{64,48},{80,64},{96,80},{112,96},{17,1},{33... | collective-permute-start | bytes 221192 | tf_op jit(solution)/shard_map/ppermute | solution.py:580
  25.1 22.1 %collective-permute-start.1 = (f32[18,8,128]{2,1,0:T(8,128)S(1)}, f32[18,8,128]{2,1,0:T(8,128)S(1)}, u32[]{:S(2)}, u32[]{:S(2)}) collective-permute-start(f32[18,8,128]{2,1,0:T(8,128)S(1)} %get-tuple-element.38), channel_id=1, source_target_pairs={{0,16},{16,32},{32,48},{48,64},{64,80},{80,96},{96,112},{1,17},{17... | collective-permute-start | bytes 221192 | tf_op jit(solution)/shard_map/ppermute | solution.py:580
  47.3 8.7 %collective-permute-start.2 = (f32[62,8,128]{2,1,0:T(8,128)S(1)}, f32[62,8,128]{2,1,0:T(8,128)S(1)}, u32[]{:S(2)}, u32[]{:S(2)}) collective-permute-start(f32[62,8,128]{2,1,0:T(8,128)S(1)} %get-tuple-element.42), channel_id=1, source_target_pairs={{0,128},{128,256},{256,384},{1,129},{129,257},{257,385},{2,130},{1... | collective-permute-start | bytes 761864 | tf_op jit(solution)/shard_map/ppermute | solution.py:580
  49.6 7.5 %collective-permute-start.3 = (f32[62,8,128]{2,1,0:T(8,128)S(1)}, f32[62,8,128]{2,1,0:T(8,128)S(1)}, u32[]{:S(2)}, u32[]{:S(2)}) collective-permute-start(f32[62,8,128]{2,1,0:T(8,128)S(1)} %get-tuple-element.43), channel_id=1, source_target_pairs={{128,0},{256,128},{384,256},{129,1},{257,129},{385,257},{130,2},{2... | collective-permute-start | bytes 761864 | tf_op jit(solution)/shard_map/ppermute | solution.py:580

commit v7 on v6

--- a/solution.py
+++ b/solution.py
@@ -332,7 +332,7 @@
 
 def coarse_kernel(
     nx, ny, nz, factor, diagonal, gathered, slab,
-    inv, ff, f1, fy, kap, rr, cx, cy, cz, i0, k1, i1, u1,
+    inv, ff, f1, fy, ey_out, ez_out, f_out, sums, e0, kap, rr, cx, cy, cz, i0, k1, i1, u1,
 ):
     inverse_of(factor, diagonal, inv)
     lane8 = iota((8, CZ), 1)
@@ -367,14 +367,46 @@
         coarse_cond(i, kap, k1)
     for i in range(CX // 2 + 1, CX - 1):
         inverse_coarse(i, k1, i1, f1)
+    f_y = ff[1, :, 0:CZ]
+    f_z = ff[1, 0:CY]
+    own_f = f_z[:, 0:CZ]
+    f_out[...] = own_f
+    mine_y = jnp.where(iota((EY, CZ), 0) < CY, f_y, 0.0)
+    mine_z = jnp.where(iota((CY, EZ), 1) < CZ, f_z, 0.0)
+    dif_y = mine_y - roll(mine_y, -1, 0)
+    dif_z = mine_z - roll(mine_z, -1, 1)
+    up_y = roll(f_y, -1, 0)[0:CY]
+    up_z = roll(f_z, -1, 1)[:, 0:CZ]
+    row_o = iota((CY, CZ), 0)
+    lane_o = iota((CY, CZ), 1)
+    s_d = s_y = s_z = jnp.zeros((CY, CZ), F32)
+    for x in range(CX):
+        b = cy[H + x, :, 0:CZ]
+        c = cz[H + x, 0:CY]
+        gy = b * dif_y
+        gz = c * dif_z
+        e = ((gy - roll(gy, 1, 0))[0:CY] + (gz - roll(gz, 1, 1))[:, 0:CZ]) * own_f
+        low_y = roll(b * f_y, 1, 0)[0:CY]
+        low_z = roll(c * f_z, 1, 1)[:, 0:CZ]
+        cut_y = jnp.where(row_o == CY - 1, b[0:CY] * up_y, jnp.where(row_o == 0, low_y, 0.0)) * own_f
+        cut_z = jnp.where(lane_o == CZ - 1, c[:, 0:CZ] * up_z, jnp.where(lane_o == 0, low_z, 0.0)) * own_f
+        e0[x] = e
+        ey_out[x] = cut_y
+        ez_out[x] = cut_z
+        s_d = s_d + e
+        s_y = s_y + cut_y
+        s_z = s_z + cut_z
+    sums[0] = s_d
+    sums[1] = jnp.where(row_o == CY - 1, s_y, 0.0)
+    sums[2] = jnp.where(lane_o == CZ - 1, s_z, 0.0)
 
 
 def main_kernel(
-    left, right, ff, f1, fy, *refs
+    left, right, ff, f1, fy, sums, *refs
 ):
-    (kap, rr, cx, cy, cz, i0, k1, i1, u1) = refs[9:18]
-    (d_out, t_out, n_out, an_out, r_out, e0_out, ey_out, ez_out, ex_out, f_out, msg) = refs[18:29]
-    u2, dd, tt = refs[29:]
+    (e0, kap, rr, cx, cy, cz, i0, k1, i1, u1) = refs[10:20]
+    (d_out, t_out, n_out, an_out, r_out, ex_out, msg) = refs[20:27]
+    u2, dd, tt = refs[27:]
     unpack_message(left, True, 0, kap, rr, ff)
     unpack_message(right, False, 2, kap, rr, ff)
     coef_x(2 * CX - 1, kap, cx)
@@ -455,19 +487,8 @@
         s_rz = s_rz + rr[H + x, 0:CY, 0:CZ] * d_out[x]
         s_dad = s_dad + tt[H + x, 0:CY, 0:CZ] * d_out[x]
     smooth(tt, (3, EX // 2 - 3), (7, EX - 7), put_n)
-    s_x, s_y, s_tau, s_om, s_d, s_cy, s_cz = (zero,) * 7
-    f = ff[1]
-    row = iota((EY, EZ), 0)
-    lane = iota((EY, EZ), 1)
-    mine = jnp.where((row < CY) & (lane < CZ), f, 0.0)
-    own_f = f[0:CY, 0:CZ]
-    row_o = iota((CY, CZ), 0)
-    lane_o = iota((CY, CZ), 1)
-    f_out[...] = own_f
-    f_up_y = roll(f, -1, 0)
-    f_up_z = roll(f, -1, 1)
-    dif_y = mine - roll(mine, -1, 0)
-    dif_z = mine - roll(mine, -1, 1)
+    s_x, s_y, s_tau, s_om = (zero,) * 4
+    own_f = ff[1, 0:CY, 0:CZ]
     image_n = images(dd, list(range(H, H + CX)))
     for x in range(CX):
         at = H + x
@@ -478,41 +499,21 @@
         n_out[x] = n
         t_out[x] = t
         r_out[x] = rr[at, 0:CY, 0:CZ]
-        b, c = cy[at], cz[at]
-        gy = b * dif_y
-        gz = c * dif_z
-        e = ((gy - roll(gy, 1, 0)) + (gz - roll(gz, 1, 1)))[0:CY, 0:CZ]
-        if x == 0:
-            e = e + cx[H - 1, 0:CY, 0:CZ] * own_f
-        if x == CX - 1:
-            e = e + cx[at, 0:CY, 0:CZ] * own_f
-        e = e * own_f
-        e0_out[x] = e
-        cut_y = jnp.where(
-            row_o == CY - 1, (b * f_up_y)[0:CY, 0:CZ], jnp.where(row_o == 0, roll(b * f, 1, 0)[0:CY, 0:CZ], 0.0)
-        ) * own_f
-        cut_z = jnp.where(
-            lane_o == CZ - 1, (c * f_up_z)[0:CY, 0:CZ], jnp.where(lane_o == 0, roll(c * f, 1, 1)[0:CY, 0:CZ], 0.0)
-        ) * own_f
-        ey_out[x] = cut_y
-        ez_out[x] = cut_z
         s_x = s_x + t * n
         s_y = s_y + n * an
         s_tau = s_tau + t
         s_om = s_om + an
-        s_d = s_d + e * own_f
-        s_cy = s_cy + cut_y
-        s_cz = s_cz + cut_z
-    ex0 = cx[H - 1, 0:CY, 0:CZ] * own_f * ff[0, 0:CY, 0:CZ]
-    ex1 = cx[H + CX - 1, 0:CY, 0:CZ] * own_f * ff[2, 0:CY, 0:CZ]
+    side0 = cx[H - 1, 0:CY, 0:CZ] * own_f
+    side1 = cx[H + CX - 1, 0:CY, 0:CZ] * own_f
+    e0[0] = e0[0] + side0
+    e0[CX - 1] = e0[CX - 1] + side1
+    ex0 = side0 * ff[0, 0:CY, 0:CZ]
+    ex1 = side1 * ff[2, 0:CY, 0:CZ]
     ex_out[0] = ex0
     ex_out[1] = ex1
     at = iota((1, CZ), 1)
     z = lax.axis_index("gz")
-    vectors = (
-        s_tau, s_om, s_d, ex1,
-        jnp.where(row_o == CY - 1, s_cy, 0.0), jnp.where(lane_o == CZ - 1, s_cz, 0.0),
-    )
+    vectors = (s_tau, s_om, sums[0] + side0 + side1, ex1, sums[1], sums[2])
     line = jnp.zeros((1, CZ), F32)
     for i, v in enumerate(vectors):
         line = line + jnp.where(at == SLOT * i + z, total(v), 0.0)
@@ -603,23 +604,25 @@
     wide = (EX, EY, EZ)
     half = (EX // 2, EY, EZ)
     third = (3, EY, EZ)
-    arrays = [wide] * 6 + [half] * 2 + [wide]
-    inv, ff, f1, fy, *fields = call(
-        functools.partial(coarse_kernel, *sizes), [factor.shape] + [third] * 3 + arrays, 4, name="coarse"
+    arrays = [block] + [wide] * 6 + [half] * 2 + [wide]
+    inv, ff, f1, fy, ey, ez, fluid, sums, *fields = call(
+        functools.partial(coarse_kernel, *sizes),
+        [factor.shape] + [third] * 3 + [block] * 2 + [(CY, CZ), (3, CY, CZ)] + arrays, 4, name="coarse",
     )(factor, diagonal, first, slab)
-    outs = call(
+    e0, *outs = call(
         main_kernel,
-        arrays + [block] * 8 + [(2, CY, CZ), (CY, CZ), (nz, 1, CZ)],
-        14,
+        arrays + [block] * 5 + [(2, CY, CZ), (nz, 1, CZ)],
+        16,
         scratch=[wide] * 3,
-        aliases={5 + i: i for i in range(9)},
+        aliases={6 + i: i for i in range(10)},
         name="fields",
-    )(x_low, x_high, ff, f1, fy, *fields)[9:]
-    part = lax.all_to_all(outs[-1], "gz", 0, 0, tiled=True)
+    )(x_low, x_high, ff, f1, fy, sums, *fields)
+    d0, t0, n0, an0, r0, ex, msg = outs[9:]
+    part = lax.all_to_all(msg, "gz", 0, 0, tiled=True)
     line = call(sum_kernel, [(nx * ny, 1, CZ)], 1, name="sum")(part)[0]
     second = lax.all_to_all(line, ("gx", "gy"), 0, 0, tiled=True)
     sol, res = call(functools.partial(final_kernel, *sizes), [block] * 2, 12, name="final")(
-        second, inv, *outs[:-1]
+        second, inv, d0, t0, n0, an0, r0, e0, ey, ez, ex, fluid
     )
     return sol, res
 

time: 88.4 us -> 88.4 us (level)
  no operation moved by 1% of the time
where the time goes in v7:
time: 88.4 us; the launch traced here: 88 us
  blocking collectives  63.3 us (72%)
  Pallas kernels  11.8 us (13%)
  starting transfers between devices  8.83 us (10%)
  local copies, waits for them, and re-layouts  1.68 us (2%)
  between operations  1.38 us (2%)
  waiting for transfers between devices  0.99 us (1%)
    all_to_all x1, blocking collectives, on_device(): got = lax.all_to_all(msg, 'gz', 0, 0, tiled=True)  20.5 us
    all_to_all x1, blocking collectives, on_device(): first = lax.all_to_all(line, ('gx', 'gy'), 0, 0, tiled=True)  18.1 us
    all_to_all x1, blocking collectives, on_device(): part = lax.all_to_all(msg, 'gz', 0, 0, tiled=True)  12.7 us
    all_to_all x1, blocking collectives, on_device(): second = lax.all_to_all(line, ('gx', 'gy'), 0, 0, tiled=True)  11.9 us
    ppermute x4, starting transfers between devices, exchange(): return (lax.ppermute(to_low, axis, down), lax.ppermute(to_high, axis, up))  8.83 us
    pallas_call x1, Pallas kernels, on_device(): call(main_kernel, arrays + [block] * 5 + [(2, CY, CZ), (nz, 1, CZ)], 16,...  5.17 us
    pallas_call x1, Pallas kernels, on_device(): call(diagonal_kernel, [(nb, CZ, CZ)], 1, name='diagonal')(factor)[0]  3.3 us
    pallas_call x1, Pallas kernels, on_device(): call(functools.partial(coarse_kernel, *sizes), [factor.shape] + [third] *...  1.84 us
  transfers between devices with their start and end apart: 4, of which 1 were waited for; matrix products, arithmetic and copies ran while one was open for 0% of the time, Pallas kernels for 6%

profile of v7, /device:TPU:1, one launch (start us, length us, event | category | flops | bytes accessed | tf_op | source)
XLA Modules:
  0.0 88.0 jit_solution(10695288567852513614)
XLA Ops:
  1.3 0.0 copy-start.1
  1.3 0.8 copy-done.1
  2.1 0.0 copy-start.2
  2.1 0.8 copy-done.2
  3.0 0.0 copy-start
  3.0 0.2 pack.1
  3.1 20.5 %all_to_all.20.got = f32[16,16,128]{2,1,0:T(8,128)S(1)} all-to-all(f32[16,16,128]{2,1,0:T(8,128)S(1)} %pack.1), channel_id=1, replica_groups=mesh['gx'=4,'gy'=8,'gz'=16] {'gz'}, dimensions={0} | all-to-all | bytes 262144 | tf_op jit(solution)/shard_map/all_to_all | solution.py:589
  23.6 0.2 rows.1
  23.8 1.3 %collective-permute-start = (f32[18,8,128]{2,1,0:T(8,128)S(1)}, f32[18,8,128]{2,1,0:T(8,128)S(1)}, u32[]{:S(2)}, u32[]{:S(2)}) collective-permute-start(f32[18,8,128]{2,1,0:T(8,128)S(1)} %get-tuple-element.39), channel_id=1, source_target_pairs={{16,0},{32,16},{48,32},{64,48},{80,64},{96,80},{112,96},{17,1},{33... | collective-permute-start | bytes 221192 | tf_op jit(solution)/shard_map/ppermute | solution.py:581
  25.1 4.0 %collective-permute-start.1 = (f32[18,8,128]{2,1,0:T(8,128)S(1)}, f32[18,8,128]{2,1,0:T(8,128)S(1)}, u32[]{:S(2)}, u32[]{:S(2)}) collective-permute-start(f32[18,8,128]{2,1,0:T(8,128)S(1)} %get-tuple-element.40), channel_id=1, source_target_pairs={{0,16},{16,32},{32,48},{48,64},{64,80},{80,96},{96,112},{1,17},{17... | collective-permute-start | bytes 221192 | tf_op jit(solution)/shard_map/ppermute | solution.py:581
  29.1 18.1 %all_to_all.21.after.gathered = f32[32,1,128]{2,1,0:T(1,128)S(1)} all-to-all(f32[32,1,128]{2,1,0:T(1,128)S(1)} %get-tuple-element.41), channel_id=1, replica_groups=mesh['gx'=4,'gy'=8,'gz'=16] {'gx','gy'}, dimensions={0} | all-to-all | bytes 32768 | tf_op jit(solution)/shard_map/all_to_all | solution.py:594
  47.2 0.0 collective-permute-done.from_high
  47.2 0.0 collective-permute-done.1.from_low
  47.3 0.1 slab.1
  47.3 2.3 %collective-permute-start.2 = (f32[62,8,128]{2,1,0:T(8,128)S(1)}, f32[62,8,128]{2,1,0:T(8,128)S(1)}, u32[]{:S(2)}, u32[]{:S(2)}) collective-permute-start(f32[62,8,128]{2,1,0:T(8,128)S(1)} %get-tuple-element.44), channel_id=1, source_target_pairs={{0,128},{128,256},{256,384},{1,129},{129,257},{257,385},{2,130},{1... | collective-permute-start | bytes 761864 | tf_op jit(solution)/shard_map/ppermute | solution.py:581
  49.6 1.3 %collective-permute-start.3 = (f32[62,8,128]{2,1,0:T(8,128)S(1)}, f32[62,8,128]{2,1,0:T(8,128)S(1)}, u32[]{:S(2)}, u32[]{:S(2)}) collective-permute-start(f32[62,8,128]{2,1,0:T(8,128)S(1)} %get-tuple-element.45), channel_id=1, source_target_pairs={{128,0},{256,128},{384,256},{129,1},{257,129},{385,257},{130,2},{2... | collective-permute-start | bytes 761864 | tf_op jit(solution)/shard_map/ppermute | solution.py:581
  50.9 0.0 copy-done
  50.9 3.3 %diagonal.1 = f32[4,128,128]{2,1,0:T(8,128)S(1)} custom-call(bf16[512,512]{1,0:T(8,128)(2,1)S(1)} %copy-done), custom_call_target="tpu_custom_call" | custom-call | tf_op jit(solution)/shard_map/diagonal/pallas_call | solution.py:601
  54.2 1.8 %coarse.1 = (f32[512,512]{1,0:T(8,128)S(1)}, f32[3,32,256]{2,1,0:T(8,128)S(1)}, f32[3,32,256]{2,1,0:T(8,128)S(1)}, f32[3,32,256]{2,1,0:T(8,128)S(1)}, f32[8,16,1...) custom-call(bf16[512,512]{1,0:T(8,128)(2,1)S(1)} %copy-done, ...), custom_call_target="tpu_custom_call" | custom-call | tf_op jit(solution)/shard_map/coarse/pallas_call | solution.py:608
  56.0 0.0 collective-permute-done.2.left
  56.1 1.0 %collective-permute-done.3.right = f32[62,8,128]{2,1,0:T(8,128)S(1)} collective-permute-done((f32[62,8,128]{2,1,0:T(8,128)S(1)}, f32[62,8,128]{2,1,0:T(8,128)S(1)}, u32[]{:S(2)}, u32[]{:S(2)}) %collective-permute-start.3) | collective-permute-done | bytes 253984 | tf_op jit(solution)/shard_map/ppermute | solution.py:581
  57.0 5.2 %fields.1 = (f32[8,16,128]{2,1,0:T(8,128)S(1)}, f32[24,32,256]{2,1,0:T(8,128)S(1)}, f32[24,32,256]{2,1,0:T(8,128)S(1)}, f32[24,32,256]{2,1,0:T(8,128)S(1)}, f32[...) custom-call(f32[62,8,128]{2,1,0:T(8,128)S(1)} %collective-permute-do, ...), custom_call_target="tpu_custom_call", output_to_operand_aliasing={{0}: (6, {}), {1}: (7, {}), {2}: (8, {}), {3}: (9, {}), {4}... | custom-call | tf_op jit(solution)/shard_map/fields/pallas_call | solution.py:612
  62.2 12.7 %all_to_all.22.part = f32[16,1,128]{2,1,0:T(1,128)S(1)} all-to-all(f32[16,1,128]{2,1,0:T(1,128)S(1)} %get-tuple-element.62), channel_id=1, replica_groups=mesh['gx'=4,'gy'=8,'gz'=16] {'gz'}, dimensions={0} | all-to-all | bytes 16384 | tf_op jit(solution)/shard_map/all_to_all | solution.py:621
  75.0 11.9 %all_to_all.23.gathered = f32[32,1,128]{2,1,0:T(1,128)S(1)} all-to-all(f32[32,1,128]{2,1,0:T(1,128)S(1)} %sum.1), channel_id=1, replica_groups=mesh['gx'=4,'gy'=8,'gz'=16] {'gx','gy'}, dimensions={0} | all-to-all | bytes 32768 | tf_op jit(solution)/shard_map/all_to_all | solution.py:623
  86.9 1.1 %final.1 = (f32[8,16,128]{2,1,0:T(8,128)}, f32[8,16,128]{2,1,0:T(8,128)}) custom-call(f32[32,1,128]{2,1,0:T(1,128)S(1)} %all_to_all.23.gathered, f32[512,512]{1,0:T(8,128)S(1)} %get-tuple-element.63.inv, f32[8,16,128]{2,1,0:T(8,128)S(1)} %get-tuple-element.64.d_in, f32[8,16,128]{2,1,0:T(8,128)S(1)} %get-tuple-element.65.t_in, ...), custom_call_target="tpu_custom_call" | custom-call | tf_op jit(solution)/shard_map/final/pallas_call | solution.py:624
  (1 shorter events, 0.0 us)
Async XLA Ops:
  1.3 0.8 copy-start.1
  2.1 0.8 copy-start.2
  3.0 47.9 %copy-start = (bf16[512,512]{1,0:T(8,128)(2,1)S(1)}, bf16[512,512]{1,0:T(8,128)(2,1)}, u32[]{:S(2)}) copy-start(bf16[512,512]{1,0:T(8,128)(2,1)} %factor.1) | copy-start | bytes 1572868
  23.8 23.4 %collective-permute-start = (f32[18,8,128]{2,1,0:T(8,128)S(1)}, f32[18,8,128]{2,1,0:T(8,128)S(1)}, u32[]{:S(2)}, u32[]{:S(2)}) collective-permute-start(f32[18,8,128]{2,1,0:T(8,128)S(1)} %get-tuple-element.39), channel_id=1, source_target_pairs={{16,0},{32,16},{48,32},{64,48},{80,64},{96,80},{112,96},{17,1},{33... | collective-permute-start | bytes 221192 | tf_op jit(solution)/shard_map/ppermute | solution.py:581
  25.1 22.1 %collective-permute-start.1 = (f32[18,8,128]{2,1,0:T(8,128)S(1)}, f32[18,8,128]{2,1,0:T(8,128)S(1)}, u32[]{:S(2)}, u32[]{:S(2)}) collective-permute-start(f32[18,8,128]{2,1,0:T(8,128)S(1)} %get-tuple-element.40), channel_id=1, source_target_pairs={{0,16},{16,32},{32,48},{48,64},{64,80},{80,96},{96,112},{1,17},{17... | collective-permute-start | bytes 221192 | tf_op jit(solution)/shard_map/ppermute | solution.py:581
  47.3 8.7 %collective-permute-start.2 = (f32[62,8,128]{2,1,0:T(8,128)S(1)}, f32[62,8,128]{2,1,0:T(8,128)S(1)}, u32[]{:S(2)}, u32[]{:S(2)}) collective-permute-start(f32[62,8,128]{2,1,0:T(8,128)S(1)} %get-tuple-element.44), channel_id=1, source_target_pairs={{0,128},{128,256},{256,384},{1,129},{129,257},{257,385},{2,130},{1... | collective-permute-start | bytes 761864 | tf_op jit(solution)/shard_map/ppermute | solution.py:581
  49.6 7.5 %collective-permute-start.3 = (f32[62,8,128]{2,1,0:T(8,128)S(1)}, f32[62,8,128]{2,1,0:T(8,128)S(1)}, u32[]{:S(2)}, u32[]{:S(2)}) collective-permute-start(f32[62,8,128]{2,1,0:T(8,128)S(1)} %get-tuple-element.45), channel_id=1, source_target_pairs={{128,0},{256,128},{384,256},{129,1},{257,129},{385,257},{130,2},{2... | collective-permute-start | bytes 761864 | tf_op jit(solution)/shard_map/ppermute | solution.py:581

commit v8 on v7

--- a/solution.py
+++ b/solution.py
@@ -447,11 +447,15 @@
 
     def smooth(src, pair_range, out_range, put):
         def pairs(ps):
-            xs = [2 * ps[0] + j for j in range(2 * len(ps))]
-            im = images(u1, xs)
+            faces = [2 * i - 1 for i in ps] + [2 * ps[-1] + 1]
+            flux = [cx[x] * (u1[x] - u1[x + 1]) for x in faces]
             for j, i in enumerate(ps):
-                x, y = xs[2 * j], xs[2 * j + 1]
-                s = (src[x] - im[2 * j]) + (src[y] - im[2 * j + 1])
+                x, y = 2 * i, 2 * i + 1
+                v, w = u1[x], u1[y]
+                gy = cy[x] * (v - roll(v, -1, 0)) + cy[y] * (w - roll(w, -1, 0))
+                gz = cz[x] * (v - roll(v, -1, 1)) + cz[y] * (w - roll(w, -1, 1))
+                both = (flux[j + 1] - flux[j]) + (gy - roll(gy, 1, 0)) + (gz - roll(gz, 1, 1))
+                s = (src[x] + src[y]) - ff[x >> 3] * both
                 below = ff[x >> 3] * (i1[i] * pooled(s))
                 u2[x] = u1[x] + below
                 u2[y] = u1[y] + below

time: 88.4 us -> 87.8 us (level)
  no operation moved by 1% of the time
where the time goes in v8:
time: 87.8 us; the launch traced here: 87.4 us
  blocking collectives  63.3 us (72%)
  Pallas kernels  11.2 us (13%)
  starting transfers between devices  8.83 us (10%)
  local copies, waits for them, and re-layouts  1.68 us (2%)
  between operations  1.38 us (2%)
  waiting for transfers between devices  0.99 us (1%)
    all_to_all x1, blocking collectives, on_device(): got = lax.all_to_all(msg, 'gz', 0, 0, tiled=True)  20.5 us
    all_to_all x1, blocking collectives, on_device(): first = lax.all_to_all(line, ('gx', 'gy'), 0, 0, tiled=True)  18.1 us
    all_to_all x1, blocking collectives, on_device(): part = lax.all_to_all(msg, 'gz', 0, 0, tiled=True)  12.7 us
    all_to_all x1, blocking collectives, on_device(): second = lax.all_to_all(line, ('gx', 'gy'), 0, 0, tiled=True)  11.9 us
    ppermute x4, starting transfers between devices, exchange(): return (lax.ppermute(to_low, axis, down), lax.ppermute(to_high, axis, up))  8.83 us
    pallas_call x1, Pallas kernels, on_device(): call(main_kernel, arrays + [block] * 5 + [(2, CY, CZ), (nz, 1, CZ)], 16,...  4.57 us
    pallas_call x1, Pallas kernels, on_device(): call(diagonal_kernel, [(nb, CZ, CZ)], 1, name='diagonal')(factor)[0]  3.3 us
    pallas_call x1, Pallas kernels, on_device(): call(functools.partial(coarse_kernel, *sizes), [factor.shape] + [third] *...  1.84 us
  transfers between devices with their start and end apart: 4, of which 1 were waited for; matrix products, arithmetic and copies ran while one was open for 0% of the time, Pallas kernels for 6%

profile of v8, /device:TPU:1, one launch (start us, length us, event | category | flops | bytes accessed | tf_op | source)
XLA Modules:
  0.0 87.4 jit_solution(11416848024048992324)
XLA Ops:
  1.3 0.0 copy-start.1
  1.3 0.8 copy-done.1
  2.1 0.0 copy-start.2
  2.1 0.8 copy-done.2
  3.0 0.0 copy-start
  3.0 0.2 pack.1
  3.1 20.5 %all_to_all.20.got = f32[16,16,128]{2,1,0:T(8,128)S(1)} all-to-all(f32[16,16,128]{2,1,0:T(8,128)S(1)} %pack.1), channel_id=1, replica_groups=mesh['gx'=4,'gy'=8,'gz'=16] {'gz'}, dimensions={0} | all-to-all | bytes 262144 | tf_op jit(solution)/shard_map/all_to_all | solution.py:593
  23.6 0.2 rows.1
  23.8 1.3 %collective-permute-start = (f32[18,8,128]{2,1,0:T(8,128)S(1)}, f32[18,8,128]{2,1,0:T(8,128)S(1)}, u32[]{:S(2)}, u32[]{:S(2)}) collective-permute-start(f32[18,8,128]{2,1,0:T(8,128)S(1)} %get-tuple-element.39), channel_id=1, source_target_pairs={{16,0},{32,16},{48,32},{64,48},{80,64},{96,80},{112,96},{17,1},{33... | collective-permute-start | bytes 221192 | tf_op jit(solution)/shard_map/ppermute | solution.py:585
  25.1 4.0 %collective-permute-start.1 = (f32[18,8,128]{2,1,0:T(8,128)S(1)}, f32[18,8,128]{2,1,0:T(8,128)S(1)}, u32[]{:S(2)}, u32[]{:S(2)}) collective-permute-start(f32[18,8,128]{2,1,0:T(8,128)S(1)} %get-tuple-element.40), channel_id=1, source_target_pairs={{0,16},{16,32},{32,48},{48,64},{64,80},{80,96},{96,112},{1,17},{17... | collective-permute-start | bytes 221192 | tf_op jit(solution)/shard_map/ppermute | solution.py:585
  29.1 18.1 %all_to_all.21.after.gathered = f32[32,1,128]{2,1,0:T(1,128)S(1)} all-to-all(f32[32,1,128]{2,1,0:T(1,128)S(1)} %get-tuple-element.41), channel_id=1, replica_groups=mesh['gx'=4,'gy'=8,'gz'=16] {'gx','gy'}, dimensions={0} | all-to-all | bytes 32768 | tf_op jit(solution)/shard_map/all_to_all | solution.py:598
  47.2 0.0 collective-permute-done.from_high
  47.2 0.0 collective-permute-done.1.from_low
  47.3 0.1 slab.1
  47.3 2.3 %collective-permute-start.2 = (f32[62,8,128]{2,1,0:T(8,128)S(1)}, f32[62,8,128]{2,1,0:T(8,128)S(1)}, u32[]{:S(2)}, u32[]{:S(2)}) collective-permute-start(f32[62,8,128]{2,1,0:T(8,128)S(1)} %get-tuple-element.44), channel_id=1, source_target_pairs={{0,128},{128,256},{256,384},{1,129},{129,257},{257,385},{2,130},{1... | collective-permute-start | bytes 761864 | tf_op jit(solution)/shard_map/ppermute | solution.py:585
  49.6 1.3 %collective-permute-start.3 = (f32[62,8,128]{2,1,0:T(8,128)S(1)}, f32[62,8,128]{2,1,0:T(8,128)S(1)}, u32[]{:S(2)}, u32[]{:S(2)}) collective-permute-start(f32[62,8,128]{2,1,0:T(8,128)S(1)} %get-tuple-element.45), channel_id=1, source_target_pairs={{128,0},{256,128},{384,256},{129,1},{257,129},{385,257},{130,2},{2... | collective-permute-start | bytes 761864 | tf_op jit(solution)/shard_map/ppermute | solution.py:585
  50.9 0.0 copy-done
  50.9 3.3 %diagonal.1 = f32[4,128,128]{2,1,0:T(8,128)S(1)} custom-call(bf16[512,512]{1,0:T(8,128)(2,1)S(1)} %copy-done), custom_call_target="tpu_custom_call" | custom-call | tf_op jit(solution)/shard_map/diagonal/pallas_call | solution.py:605
  54.2 1.8 %coarse.1 = (f32[512,512]{1,0:T(8,128)S(1)}, f32[3,32,256]{2,1,0:T(8,128)S(1)}, f32[3,32,256]{2,1,0:T(8,128)S(1)}, f32[3,32,256]{2,1,0:T(8,128)S(1)}, f32[8,16,1...) custom-call(bf16[512,512]{1,0:T(8,128)(2,1)S(1)} %copy-done, ...), custom_call_target="tpu_custom_call" | custom-call | tf_op jit(solution)/shard_map/coarse/pallas_call | solution.py:612
  56.0 0.0 collective-permute-done.2.left
  56.1 1.0 %collective-permute-done.3.right = f32[62,8,128]{2,1,0:T(8,128)S(1)} collective-permute-done((f32[62,8,128]{2,1,0:T(8,128)S(1)}, f32[62,8,128]{2,1,0:T(8,128)S(1)}, u32[]{:S(2)}, u32[]{:S(2)}) %collective-permute-start.3) | collective-permute-done | bytes 253984 | tf_op jit(solution)/shard_map/ppermute | solution.py:585
  57.0 4.6 %fields.1 = (f32[8,16,128]{2,1,0:T(8,128)S(1)}, f32[24,32,256]{2,1,0:T(8,128)S(1)}, f32[24,32,256]{2,1,0:T(8,128)S(1)}, f32[24,32,256]{2,1,0:T(8,128)S(1)}, f32[...) custom-call(f32[62,8,128]{2,1,0:T(8,128)S(1)} %collective-permute-do, ...), custom_call_target="tpu_custom_call", output_to_operand_aliasing={{0}: (6, {}), {1}: (7, {}), {2}: (8, {}), {3}: (9, {}), {4}... | custom-call | tf_op jit(solution)/shard_map/fields/pallas_call | solution.py:616
  61.6 12.7 %all_to_all.22.part = f32[16,1,128]{2,1,0:T(1,128)S(1)} all-to-all(f32[16,1,128]{2,1,0:T(1,128)S(1)} %get-tuple-element.62), channel_id=1, replica_groups=mesh['gx'=4,'gy'=8,'gz'=16] {'gz'}, dimensions={0} | all-to-all | bytes 16384 | tf_op jit(solution)/shard_map/all_to_all | solution.py:625
  74.4 11.9 %all_to_all.23.gathered = f32[32,1,128]{2,1,0:T(1,128)S(1)} all-to-all(f32[32,1,128]{2,1,0:T(1,128)S(1)} %sum.1), channel_id=1, replica_groups=mesh['gx'=4,'gy'=8,'gz'=16] {'gx','gy'}, dimensions={0} | all-to-all | bytes 32768 | tf_op jit(solution)/shard_map/all_to_all | solution.py:627
  86.3 1.1 %final.1 = (f32[8,16,128]{2,1,0:T(8,128)}, f32[8,16,128]{2,1,0:T(8,128)}) custom-call(f32[32,1,128]{2,1,0:T(1,128)S(1)} %all_to_all.23.gathered, f32[512,512]{1,0:T(8,128)S(1)} %get-tuple-element.63.inv, f32[8,16,128]{2,1,0:T(8,128)S(1)} %get-tuple-element.64.d_in, f32[8,16,128]{2,1,0:T(8,128)S(1)} %get-tuple-element.65.t_in, ...), custom_call_target="tpu_custom_call" | custom-call | tf_op jit(solution)/shard_map/final/pallas_call | solution.py:628
  (1 shorter events, 0.0 us)
Async XLA Ops:
  1.3 0.8 copy-start.1
  2.1 0.8 copy-start.2
  3.0 47.9 %copy-start = (bf16[512,512]{1,0:T(8,128)(2,1)S(1)}, bf16[512,512]{1,0:T(8,128)(2,1)}, u32[]{:S(2)}) copy-start(bf16[512,512]{1,0:T(8,128)(2,1)} %factor.1) | copy-start | bytes 1572868
  23.8 23.4 %collective-permute-start = (f32[18,8,128]{2,1,0:T(8,128)S(1)}, f32[18,8,128]{2,1,0:T(8,128)S(1)}, u32[]{:S(2)}, u32[]{:S(2)}) collective-permute-start(f32[18,8,128]{2,1,0:T(8,128)S(1)} %get-tuple-element.39), channel_id=1, source_target_pairs={{16,0},{32,16},{48,32},{64,48},{80,64},{96,80},{112,96},{17,1},{33... | collective-permute-start | bytes 221192 | tf_op jit(solution)/shard_map/ppermute | solution.py:585
  25.1 22.1 %collective-permute-start.1 = (f32[18,8,128]{2,1,0:T(8,128)S(1)}, f32[18,8,128]{2,1,0:T(8,128)S(1)}, u32[]{:S(2)}, u32[]{:S(2)}) collective-permute-start(f32[18,8,128]{2,1,0:T(8,128)S(1)} %get-tuple-element.40), channel_id=1, source_target_pairs={{0,16},{16,32},{32,48},{48,64},{64,80},{80,96},{96,112},{1,17},{17... | collective-permute-start | bytes 221192 | tf_op jit(solution)/shard_map/ppermute | solution.py:585
  47.3 8.7 %collective-permute-start.2 = (f32[62,8,128]{2,1,0:T(8,128)S(1)}, f32[62,8,128]{2,1,0:T(8,128)S(1)}, u32[]{:S(2)}, u32[]{:S(2)}) collective-permute-start(f32[62,8,128]{2,1,0:T(8,128)S(1)} %get-tuple-element.44), channel_id=1, source_target_pairs={{0,128},{128,256},{256,384},{1,129},{129,257},{257,385},{2,130},{1... | collective-permute-start | bytes 761864 | tf_op jit(solution)/shard_map/ppermute | solution.py:585
  49.6 7.5 %collective-permute-start.3 = (f32[62,8,128]{2,1,0:T(8,128)S(1)}, f32[62,8,128]{2,1,0:T(8,128)S(1)}, u32[]{:S(2)}, u32[]{:S(2)}) collective-permute-start(f32[62,8,128]{2,1,0:T(8,128)S(1)} %get-tuple-element.45), channel_id=1, source_target_pairs={{128,0},{256,128},{384,256},{129,1},{257,129},{385,257},{130,2},{2... | collective-permute-start | bytes 761864 | tf_op jit(solution)/shard_map/ppermute | solution.py:585

commit v9 on v7

--- a/solution.py
+++ b/solution.py
@@ -319,12 +319,27 @@
     k1[i] = pooled(kap[2 * i] + kap[2 * i + 1]) * 0.125
 
 
-def inverse_coarse(i, k1, i1, f1):
+def pair_step(ps, src, u1, u2, cx, cy, cz, ff, i1):
+    faces = [2 * i - 1 for i in ps] + [2 * ps[-1] + 1]
+    flux = [cx[x] * (u1[x] - u1[x + 1]) for x in faces]
+    for j, i in enumerate(ps):
+        x, y = 2 * i, 2 * i + 1
+        v, w = u1[x], u1[y]
+        gy = cy[x] * (v - roll(v, -1, 0)) + cy[y] * (w - roll(w, -1, 0))
+        gz = cz[x] * (v - roll(v, -1, 1)) + cz[y] * (w - roll(w, -1, 1))
+        both = (flux[j + 1] - flux[j]) + (gy - roll(gy, 1, 0)) + (gz - roll(gz, 1, 1))
+        s = (src[x] + src[y]) - ff[x >> 3] * both
+        below = i1[i] * pooled(s)
+        u2[x] = u1[x] + below
+        u2[y] = u1[y] + below
+
+
+def inverse_coarse(i, k1, i1, f1, ff):
     k = k1[i]
     f = f1[i >> 2]
     s = k1[i - 1] + k1[i + 1] + roll(k, 2, 0) + roll(k, -2, 0) + roll(k, 2, 1) + roll(k, -2, 1)
     s = 3.0 * k + 0.5 * s
-    i1[i] = OMEGA * f / (4.0 * s + 1.0 - f)
+    i1[i] = OMEGA * f / (4.0 * s + 1.0 - f) * ff[i >> 2]
 
 
 ROW_PARTS = ((0, 0), (8, 0), (16, 1), (24, -1))
@@ -332,7 +347,7 @@
 
 def coarse_kernel(
     nx, ny, nz, factor, diagonal, gathered, slab,
-    inv, ff, f1, fy, ey_out, ez_out, f_out, sums, e0, kap, rr, cx, cy, cz, i0, k1, i1, u1,
+    inv, ff, f1, fy, ey_out, ez_out, f_out, sums, e0, kap, rr, cx, cy, cz, i0, k1, i1, u1, u2,
 ):
     inverse_of(factor, diagonal, inv)
     lane8 = iota((8, CZ), 1)
@@ -366,7 +381,8 @@
     for i in range(CX // 2, CX):
         coarse_cond(i, kap, k1)
     for i in range(CX // 2 + 1, CX - 1):
-        inverse_coarse(i, k1, i1, f1)
+        inverse_coarse(i, k1, i1, f1, ff)
+    pair_step([CX // 2 + 1, CX // 2 + 2], rr, u1, u2, cx, cy, cz, ff, i1)
     f_y = ff[1, :, 0:CZ]
     f_z = ff[1, 0:CY]
     own_f = f_z[:, 0:CZ]
@@ -404,9 +420,9 @@
 def main_kernel(
     left, right, ff, f1, fy, sums, *refs
 ):
-    (e0, kap, rr, cx, cy, cz, i0, k1, i1, u1) = refs[10:20]
-    (d_out, t_out, n_out, an_out, r_out, ex_out, msg) = refs[20:27]
-    u2, dd, tt = refs[27:]
+    (e0, kap, rr, cx, cy, cz, i0, k1, i1, u1, u2) = refs[11:22]
+    (d_out, t_out, n_out, an_out, r_out, ex_out, msg) = refs[22:29]
+    dd, tt = refs[29:]
     unpack_message(left, True, 0, kap, rr, ff)
     unpack_message(right, False, 2, kap, rr, ff)
     coef_x(2 * CX - 1, kap, cx)
@@ -431,7 +447,7 @@
             coarse_cond(j, kap, k1)
     for i in range(1, CX // 2 + 1):
         for j in (i, i + CX - 2):
-            inverse_coarse(j, k1, i1, f1)
+            inverse_coarse(j, k1, i1, f1, ff)
 
     def images(u, xs, masked=True):
         c = [u[xs[0] - 1]] + [u[x] for x in xs] + [u[xs[-1] + 1]]
@@ -445,18 +461,8 @@
             out.append(ff[x >> 3] * w if masked else w)
         return out
 
-    def smooth(src, pair_range, out_range, put):
-        def pairs(ps):
-            xs = [2 * ps[0] + j for j in range(2 * len(ps))]
-            im = images(u1, xs)
-            for j, i in enumerate(ps):
-                x, y = xs[2 * j], xs[2 * j + 1]
-                s = (src[x] - im[2 * j]) + (src[y] - im[2 * j + 1])
-                below = ff[x >> 3] * (i1[i] * pooled(s))
-                u2[x] = u1[x] + below
-                u2[y] = u1[y] + below
-
-        groups(*pair_range, pairs)
+    def smooth(src, run_pairs, out_range, put):
+        run_pairs()
 
         def last(xs):
             for x, w in zip(xs, images(u2, xs, False)):
@@ -467,7 +473,11 @@
     def put_d(x, v):
         dd[x] = v + fy[x >> 3]
 
-    smooth(rr, (1, EX // 2 - 1), (3, EX - 3), put_d)
+    def outer(us):
+        for skip in (0, CX // 2 + 2):
+            pair_step([u + skip for u in us], rr, u1, u2, cx, cy, cz, ff, i1)
+
+    smooth(rr, lambda: groups(1, CX // 2 + 1, outer), (3, EX - 3), put_d)
 
     def apply(xs):
         for x, w in zip(xs, images(dd, xs)):
@@ -486,7 +496,10 @@
     for x in range(CX):
         s_rz = s_rz + rr[H + x, 0:CY, 0:CZ] * d_out[x]
         s_dad = s_dad + tt[H + x, 0:CY, 0:CZ] * d_out[x]
-    smooth(tt, (3, EX // 2 - 3), (7, EX - 7), put_n)
+    def inner(ps):
+        pair_step(ps, tt, u1, u2, cx, cy, cz, ff, i1)
+
+    smooth(tt, lambda: groups(3, EX // 2 - 3, inner), (7, EX - 7), put_n)
     s_x, s_y, s_tau, s_om = (zero,) * 4
     own_f = ff[1, 0:CY, 0:CZ]
     image_n = images(dd, list(range(H, H + CX)))
@@ -604,7 +617,7 @@
     wide = (EX, EY, EZ)
     half = (EX // 2, EY, EZ)
     third = (3, EY, EZ)
-    arrays = [block] + [wide] * 6 + [half] * 2 + [wide]
+    arrays = [block] + [wide] * 6 + [half] * 2 + [wide] * 2
     inv, ff, f1, fy, ey, ez, fluid, sums, *fields = call(
         functools.partial(coarse_kernel, *sizes),
         [factor.shape] + [third] * 3 + [block] * 2 + [(CY, CZ), (3, CY, CZ)] + arrays, 4, name="coarse",
@@ -612,12 +625,12 @@
     e0, *outs = call(
         main_kernel,
         arrays + [block] * 5 + [(2, CY, CZ), (nz, 1, CZ)],
-        16,
-        scratch=[wide] * 3,
-        aliases={6 + i: i for i in range(10)},
+        17,
+        scratch=[wide] * 2,
+        aliases={6 + i: i for i in range(11)},
         name="fields",
     )(x_low, x_high, ff, f1, fy, sums, *fields)
-    d0, t0, n0, an0, r0, ex, msg = outs[9:]
+    d0, t0, n0, an0, r0, ex, msg = outs[10:]
     part = lax.all_to_all(msg, "gz", 0, 0, tiled=True)
     line = call(sum_kernel, [(nx * ny, 1, CZ)], 1, name="sum")(part)[0]
     second = lax.all_to_all(line, ("gx", "gy"), 0, 0, tiled=True)

time: 88.4 us -> 87.6 us (level)
  no operation moved by 1% of the time
where the time goes in v9:
time: 87.6 us; the launch traced here: 87.2 us
  blocking collectives  63.3 us (72%)
  Pallas kernels  11.1 us (13%)
  starting transfers between devices  8.83 us (10%)
  local copies, waits for them, and re-layouts  1.68 us (2%)
  between operations  1.38 us (2%)
  waiting for transfers between devices  0.92 us (1%)
    all_to_all x1, blocking collectives, on_device(): got = lax.all_to_all(msg, 'gz', 0, 0, tiled=True)  20.5 us
    all_to_all x1, blocking collectives, on_device(): first = lax.all_to_all(line, ('gx', 'gy'), 0, 0, tiled=True)  18.1 us
    all_to_all x1, blocking collectives, on_device(): part = lax.all_to_all(msg, 'gz', 0, 0, tiled=True)  12.7 us
    all_to_all x1, blocking collectives, on_device(): second = lax.all_to_all(line, ('gx', 'gy'), 0, 0, tiled=True)  11.9 us
    ppermute x4, starting transfers between devices, exchange(): return (lax.ppermute(to_low, axis, down), lax.ppermute(to_high, axis, up))  8.83 us
    pallas_call x1, Pallas kernels, on_device(): call(main_kernel, arrays + [block] * 5 + [(2, CY, CZ), (nz, 1, CZ)], 17,...  4.36 us
    pallas_call x1, Pallas kernels, on_device(): call(diagonal_kernel, [(nb, CZ, CZ)], 1, name='diagonal')(factor)[0]  3.31 us
    pallas_call x1, Pallas kernels, on_device(): call(functools.partial(coarse_kernel, *sizes), [factor.shape] + [third] *...  1.89 us
  transfers between devices with their start and end apart: 4, of which 1 were waited for; matrix products, arithmetic and copies ran while one was open for 0% of the time, Pallas kernels for 6%

profile of v9, /device:TPU:1, one launch (start us, length us, event | category | flops | bytes accessed | tf_op | source)
XLA Modules:
  0.0 87.2 jit_solution(12938712896940181852)
XLA Ops:
  1.3 0.0 copy-start.1
  1.3 0.8 copy-done.1
  2.1 0.0 copy-start.2
  2.1 0.8 copy-done.2
  3.0 0.0 copy-start
  3.0 0.2 pack.1
  3.1 20.5 %all_to_all.20.got = f32[16,16,128]{2,1,0:T(8,128)S(1)} all-to-all(f32[16,16,128]{2,1,0:T(8,128)S(1)} %pack.1), channel_id=1, replica_groups=mesh['gx'=4,'gy'=8,'gz'=16] {'gz'}, dimensions={0} | all-to-all | bytes 262144 | tf_op jit(solution)/shard_map/all_to_all | solution.py:602
  23.6 0.2 rows.1
  23.8 1.3 %collective-permute-start = (f32[18,8,128]{2,1,0:T(8,128)S(1)}, f32[18,8,128]{2,1,0:T(8,128)S(1)}, u32[]{:S(2)}, u32[]{:S(2)}) collective-permute-start(f32[18,8,128]{2,1,0:T(8,128)S(1)} %get-tuple-element.40), channel_id=1, source_target_pairs={{16,0},{32,16},{48,32},{64,48},{80,64},{96,80},{112,96},{17,1},{33... | collective-permute-start | bytes 221192 | tf_op jit(solution)/shard_map/ppermute | solution.py:594
  25.1 4.0 %collective-permute-start.1 = (f32[18,8,128]{2,1,0:T(8,128)S(1)}, f32[18,8,128]{2,1,0:T(8,128)S(1)}, u32[]{:S(2)}, u32[]{:S(2)}) collective-permute-start(f32[18,8,128]{2,1,0:T(8,128)S(1)} %get-tuple-element.41), channel_id=1, source_target_pairs={{0,16},{16,32},{32,48},{48,64},{64,80},{80,96},{96,112},{1,17},{17... | collective-permute-start | bytes 221192 | tf_op jit(solution)/shard_map/ppermute | solution.py:594
  29.1 18.1 %all_to_all.21.after.gathered = f32[32,1,128]{2,1,0:T(1,128)S(1)} all-to-all(f32[32,1,128]{2,1,0:T(1,128)S(1)} %get-tuple-element.42), channel_id=1, replica_groups=mesh['gx'=4,'gy'=8,'gz'=16] {'gx','gy'}, dimensions={0} | all-to-all | bytes 32768 | tf_op jit(solution)/shard_map/all_to_all | solution.py:607
  47.2 0.0 collective-permute-done.from_high
  47.2 0.0 collective-permute-done.1.from_low
  47.3 0.1 slab.1
  47.3 2.3 %collective-permute-start.2 = (f32[62,8,128]{2,1,0:T(8,128)S(1)}, f32[62,8,128]{2,1,0:T(8,128)S(1)}, u32[]{:S(2)}, u32[]{:S(2)}) collective-permute-start(f32[62,8,128]{2,1,0:T(8,128)S(1)} %get-tuple-element.45), channel_id=1, source_target_pairs={{0,128},{128,256},{256,384},{1,129},{129,257},{257,385},{2,130},{1... | collective-permute-start | bytes 761864 | tf_op jit(solution)/shard_map/ppermute | solution.py:594
  49.6 1.3 %collective-permute-start.3 = (f32[62,8,128]{2,1,0:T(8,128)S(1)}, f32[62,8,128]{2,1,0:T(8,128)S(1)}, u32[]{:S(2)}, u32[]{:S(2)}) collective-permute-start(f32[62,8,128]{2,1,0:T(8,128)S(1)} %get-tuple-element.46), channel_id=1, source_target_pairs={{128,0},{256,128},{384,256},{129,1},{257,129},{385,257},{130,2},{2... | collective-permute-start | bytes 761864 | tf_op jit(solution)/shard_map/ppermute | solution.py:594
  50.9 0.0 copy-done
  50.9 3.3 %diagonal.1 = f32[4,128,128]{2,1,0:T(8,128)S(1)} custom-call(bf16[512,512]{1,0:T(8,128)(2,1)S(1)} %copy-done), custom_call_target="tpu_custom_call" | custom-call | tf_op jit(solution)/shard_map/diagonal/pallas_call | solution.py:614
  54.2 1.9 %coarse.1 = (f32[512,512]{1,0:T(8,128)S(1)}, f32[3,32,256]{2,1,0:T(8,128)S(1)}, f32[3,32,256]{2,1,0:T(8,128)S(1)}, f32[3,32,256]{2,1,0:T(8,128)S(1)}, f32[8,16,1...) custom-call(bf16[512,512]{1,0:T(8,128)(2,1)S(1)} %copy-done, ...), custom_call_target="tpu_custom_call" | custom-call | tf_op jit(solution)/shard_map/coarse/pallas_call | solution.py:621
  56.1 0.0 collective-permute-done.2.left
  56.1 0.9 %collective-permute-done.3.right = f32[62,8,128]{2,1,0:T(8,128)S(1)} collective-permute-done((f32[62,8,128]{2,1,0:T(8,128)S(1)}, f32[62,8,128]{2,1,0:T(8,128)S(1)}, u32[]{:S(2)}, u32[]{:S(2)}) %collective-permute-start.3) | collective-permute-done | bytes 253984 | tf_op jit(solution)/shard_map/ppermute | solution.py:594
  57.0 4.4 %fields.1 = (f32[8,16,128]{2,1,0:T(8,128)S(1)}, f32[24,32,256]{2,1,0:T(8,128)S(1)}, f32[24,32,256]{2,1,0:T(8,128)S(1)}, f32[24,32,256]{2,1,0:T(8,128)S(1)}, f32[...) custom-call(f32[62,8,128]{2,1,0:T(8,128)S(1)} %collective-permute-do, ...), custom_call_target="tpu_custom_call", output_to_operand_aliasing={{0}: (6, {}), {1}: (7, {}), {2}: (8, {}), {3}: (9, {}), {4}... | custom-call | tf_op jit(solution)/shard_map/fields/pallas_call | solution.py:625
  61.4 12.7 %all_to_all.22.part = f32[16,1,128]{2,1,0:T(1,128)S(1)} all-to-all(f32[16,1,128]{2,1,0:T(1,128)S(1)} %get-tuple-element.64), channel_id=1, replica_groups=mesh['gx'=4,'gy'=8,'gz'=16] {'gz'}, dimensions={0} | all-to-all | bytes 16384 | tf_op jit(solution)/shard_map/all_to_all | solution.py:634
  74.2 11.9 %all_to_all.23.gathered = f32[32,1,128]{2,1,0:T(1,128)S(1)} all-to-all(f32[32,1,128]{2,1,0:T(1,128)S(1)} %sum.1), channel_id=1, replica_groups=mesh['gx'=4,'gy'=8,'gz'=16] {'gx','gy'}, dimensions={0} | all-to-all | bytes 32768 | tf_op jit(solution)/shard_map/all_to_all | solution.py:636
  86.1 1.1 %final.1 = (f32[8,16,128]{2,1,0:T(8,128)}, f32[8,16,128]{2,1,0:T(8,128)}) custom-call(f32[32,1,128]{2,1,0:T(1,128)S(1)} %all_to_all.23.gathered, f32[512,512]{1,0:T(8,128)S(1)} %get-tuple-element.65.inv, f32[8,16,128]{2,1,0:T(8,128)S(1)} %get-tuple-element.66.d_in, f32[8,16,128]{2,1,0:T(8,128)S(1)} %get-tuple-element.67.t_in, ...), custom_call_target="tpu_custom_call" | custom-call | tf_op jit(solution)/shard_map/final/pallas_call | solution.py:637
  (1 shorter events, 0.0 us)
Async XLA Ops:
  1.3 0.8 copy-start.1
  2.1 0.8 copy-start.2
  3.0 47.9 %copy-start = (bf16[512,512]{1,0:T(8,128)(2,1)S(1)}, bf16[512,512]{1,0:T(8,128)(2,1)}, u32[]{:S(2)}) copy-start(bf16[512,512]{1,0:T(8,128)(2,1)} %factor.1) | copy-start | bytes 1572868
  23.8 23.4 %collective-permute-start = (f32[18,8,128]{2,1,0:T(8,128)S(1)}, f32[18,8,128]{2,1,0:T(8,128)S(1)}, u32[]{:S(2)}, u32[]{:S(2)}) collective-permute-start(f32[18,8,128]{2,1,0:T(8,128)S(1)} %get-tuple-element.40), channel_id=1, source_target_pairs={{16,0},{32,16},{48,32},{64,48},{80,64},{96,80},{112,96},{17,1},{33... | collective-permute-start | bytes 221192 | tf_op jit(solution)/shard_map/ppermute | solution.py:594
  25.1 22.1 %collective-permute-start.1 = (f32[18,8,128]{2,1,0:T(8,128)S(1)}, f32[18,8,128]{2,1,0:T(8,128)S(1)}, u32[]{:S(2)}, u32[]{:S(2)}) collective-permute-start(f32[18,8,128]{2,1,0:T(8,128)S(1)} %get-tuple-element.41), channel_id=1, source_target_pairs={{0,16},{16,32},{32,48},{48,64},{64,80},{80,96},{96,112},{1,17},{17... | collective-permute-start | bytes 221192 | tf_op jit(solution)/shard_map/ppermute | solution.py:594
  47.3 8.8 %collective-permute-start.2 = (f32[62,8,128]{2,1,0:T(8,128)S(1)}, f32[62,8,128]{2,1,0:T(8,128)S(1)}, u32[]{:S(2)}, u32[]{:S(2)}) collective-permute-start(f32[62,8,128]{2,1,0:T(8,128)S(1)} %get-tuple-element.45), channel_id=1, source_target_pairs={{0,128},{128,256},{256,384},{1,129},{129,257},{257,385},{2,130},{1... | collective-permute-start | bytes 761864 | tf_op jit(solution)/shard_map/ppermute | solution.py:594
  49.6 7.5 %collective-permute-start.3 = (f32[62,8,128]{2,1,0:T(8,128)S(1)}, f32[62,8,128]{2,1,0:T(8,128)S(1)}, u32[]{:S(2)}, u32[]{:S(2)}) collective-permute-start(f32[62,8,128]{2,1,0:T(8,128)S(1)} %get-tuple-element.46), channel_id=1, source_target_pairs={{128,0},{256,128},{384,256},{129,1},{257,129},{385,257},{130,2},{2... | collective-permute-start | bytes 761864 | tf_op jit(solution)/shard_map/ppermute | solution.py:594

commit v10 on v8

--- a/solution.py
+++ b/solution.py
@@ -319,12 +319,12 @@
     k1[i] = pooled(kap[2 * i] + kap[2 * i + 1]) * 0.125
 
 
-def inverse_coarse(i, k1, i1, f1):
+def inverse_coarse(i, k1, i1, f1, ff):
     k = k1[i]
     f = f1[i >> 2]
     s = k1[i - 1] + k1[i + 1] + roll(k, 2, 0) + roll(k, -2, 0) + roll(k, 2, 1) + roll(k, -2, 1)
     s = 3.0 * k + 0.5 * s
-    i1[i] = OMEGA * f / (4.0 * s + 1.0 - f)
+    i1[i] = OMEGA * f / (4.0 * s + 1.0 - f) * ff[i >> 2]
 
 
 ROW_PARTS = ((0, 0), (8, 0), (16, 1), (24, -1))
@@ -366,7 +366,7 @@
     for i in range(CX // 2, CX):
         coarse_cond(i, kap, k1)
     for i in range(CX // 2 + 1, CX - 1):
-        inverse_coarse(i, k1, i1, f1)
+        inverse_coarse(i, k1, i1, f1, ff)
     f_y = ff[1, :, 0:CZ]
     f_z = ff[1, 0:CY]
     own_f = f_z[:, 0:CZ]
@@ -431,7 +431,7 @@
             coarse_cond(j, kap, k1)
     for i in range(1, CX // 2 + 1):
         for j in (i, i + CX - 2):
-            inverse_coarse(j, k1, i1, f1)
+            inverse_coarse(j, k1, i1, f1, ff)
 
     def images(u, xs, masked=True):
         c = [u[xs[0] - 1]] + [u[x] for x in xs] + [u[xs[-1] + 1]]
@@ -456,7 +456,7 @@
                 gz = cz[x] * (v - roll(v, -1, 1)) + cz[y] * (w - roll(w, -1, 1))
                 both = (flux[j + 1] - flux[j]) + (gy - roll(gy, 1, 0)) + (gz - roll(gz, 1, 1))
                 s = (src[x] + src[y]) - ff[x >> 3] * both
-                below = ff[x >> 3] * (i1[i] * pooled(s))
+                below = i1[i] * pooled(s)
                 u2[x] = u1[x] + below
                 u2[y] = u1[y] + below
 

time: 87.8 us -> 87.8 us (level)
  no operation moved by 1% of the time
where the time goes in v10:
time: 87.8 us; the launch traced here: 87.4 us
  blocking collectives  63.3 us (72%)
  Pallas kernels  11.2 us (13%)
  starting transfers between devices  8.83 us (10%)
  local copies, waits for them, and re-layouts  1.68 us (2%)
  between operations  1.38 us (2%)
  waiting for transfers between devices  0.99 us (1%)
    all_to_all x1, blocking collectives, on_device(): got = lax.all_to_all(msg, 'gz', 0, 0, tiled=True)  20.5 us
    all_to_all x1, blocking collectives, on_device(): first = lax.all_to_all(line, ('gx', 'gy'), 0, 0, tiled=True)  18.1 us
    all_to_all x1, blocking collectives, on_device(): part = lax.all_to_all(msg, 'gz', 0, 0, tiled=True)  12.7 us
    all_to_all x1, blocking collectives, on_device(): second = lax.all_to_all(line, ('gx', 'gy'), 0, 0, tiled=True)  11.9 us
    ppermute x4, starting transfers between devices, exchange(): return (lax.ppermute(to_low, axis, down), lax.ppermute(to_high, axis, up))  8.83 us
    pallas_call x1, Pallas kernels, on_device(): call(main_kernel, arrays + [block] * 5 + [(2, CY, CZ), (nz, 1, CZ)], 16,...  4.56 us
    pallas_call x1, Pallas kernels, on_device(): call(diagonal_kernel, [(nb, CZ, CZ)], 1, name='diagonal')(factor)[0]  3.3 us
    pallas_call x1, Pallas kernels, on_device(): call(functools.partial(coarse_kernel, *sizes), [factor.shape] + [third] *...  1.84 us
  transfers between devices with their start and end apart: 4, of which 1 were waited for; matrix products, arithmetic and copies ran while one was open for 0% of the time, Pallas kernels for 6%

profile of v10, /device:TPU:1, one launch (start us, length us, event | category | flops | bytes accessed | tf_op | source)
XLA Modules:
  0.0 87.4 jit_solution(7130085283441225670)
XLA Ops:
  1.3 0.0 copy-start.1
  1.3 0.8 copy-done.1
  2.1 0.0 copy-start.2
  2.1 0.8 copy-done.2
  3.0 0.0 copy-start
  3.0 0.2 pack.1
  3.1 20.5 %all_to_all.20.got = f32[16,16,128]{2,1,0:T(8,128)S(1)} all-to-all(f32[16,16,128]{2,1,0:T(8,128)S(1)} %pack.1), channel_id=1, replica_groups=mesh['gx'=4,'gy'=8,'gz'=16] {'gz'}, dimensions={0} | all-to-all | bytes 262144 | tf_op jit(solution)/shard_map/all_to_all | solution.py:593
  23.6 0.2 rows.1
  23.8 1.3 %collective-permute-start = (f32[18,8,128]{2,1,0:T(8,128)S(1)}, f32[18,8,128]{2,1,0:T(8,128)S(1)}, u32[]{:S(2)}, u32[]{:S(2)}) collective-permute-start(f32[18,8,128]{2,1,0:T(8,128)S(1)} %get-tuple-element.39), channel_id=1, source_target_pairs={{16,0},{32,16},{48,32},{64,48},{80,64},{96,80},{112,96},{17,1},{33... | collective-permute-start | bytes 221192 | tf_op jit(solution)/shard_map/ppermute | solution.py:585
  25.1 4.0 %collective-permute-start.1 = (f32[18,8,128]{2,1,0:T(8,128)S(1)}, f32[18,8,128]{2,1,0:T(8,128)S(1)}, u32[]{:S(2)}, u32[]{:S(2)}) collective-permute-start(f32[18,8,128]{2,1,0:T(8,128)S(1)} %get-tuple-element.40), channel_id=1, source_target_pairs={{0,16},{16,32},{32,48},{48,64},{64,80},{80,96},{96,112},{1,17},{17... | collective-permute-start | bytes 221192 | tf_op jit(solution)/shard_map/ppermute | solution.py:585
  29.1 18.1 %all_to_all.21.after.gathered = f32[32,1,128]{2,1,0:T(1,128)S(1)} all-to-all(f32[32,1,128]{2,1,0:T(1,128)S(1)} %get-tuple-element.41), channel_id=1, replica_groups=mesh['gx'=4,'gy'=8,'gz'=16] {'gx','gy'}, dimensions={0} | all-to-all | bytes 32768 | tf_op jit(solution)/shard_map/all_to_all | solution.py:598
  47.2 0.0 collective-permute-done.from_high
  47.2 0.0 collective-permute-done.1.from_low
  47.3 0.1 slab.1
  47.3 2.3 %collective-permute-start.2 = (f32[62,8,128]{2,1,0:T(8,128)S(1)}, f32[62,8,128]{2,1,0:T(8,128)S(1)}, u32[]{:S(2)}, u32[]{:S(2)}) collective-permute-start(f32[62,8,128]{2,1,0:T(8,128)S(1)} %get-tuple-element.44), channel_id=1, source_target_pairs={{0,128},{128,256},{256,384},{1,129},{129,257},{257,385},{2,130},{1... | collective-permute-start | bytes 761864 | tf_op jit(solution)/shard_map/ppermute | solution.py:585
  49.6 1.3 %collective-permute-start.3 = (f32[62,8,128]{2,1,0:T(8,128)S(1)}, f32[62,8,128]{2,1,0:T(8,128)S(1)}, u32[]{:S(2)}, u32[]{:S(2)}) collective-permute-start(f32[62,8,128]{2,1,0:T(8,128)S(1)} %get-tuple-element.45), channel_id=1, source_target_pairs={{128,0},{256,128},{384,256},{129,1},{257,129},{385,257},{130,2},{2... | collective-permute-start | bytes 761864 | tf_op jit(solution)/shard_map/ppermute | solution.py:585
  50.9 0.0 copy-done
  50.9 3.3 %diagonal.1 = f32[4,128,128]{2,1,0:T(8,128)S(1)} custom-call(bf16[512,512]{1,0:T(8,128)(2,1)S(1)} %copy-done), custom_call_target="tpu_custom_call" | custom-call | tf_op jit(solution)/shard_map/diagonal/pallas_call | solution.py:605
  54.2 1.8 %coarse.1 = (f32[512,512]{1,0:T(8,128)S(1)}, f32[3,32,256]{2,1,0:T(8,128)S(1)}, f32[3,32,256]{2,1,0:T(8,128)S(1)}, f32[3,32,256]{2,1,0:T(8,128)S(1)}, f32[8,16,1...) custom-call(bf16[512,512]{1,0:T(8,128)(2,1)S(1)} %copy-done, ...), custom_call_target="tpu_custom_call" | custom-call | tf_op jit(solution)/shard_map/coarse/pallas_call | solution.py:612
  56.1 0.0 collective-permute-done.2.left
  56.1 1.0 %collective-permute-done.3.right = f32[62,8,128]{2,1,0:T(8,128)S(1)} collective-permute-done((f32[62,8,128]{2,1,0:T(8,128)S(1)}, f32[62,8,128]{2,1,0:T(8,128)S(1)}, u32[]{:S(2)}, u32[]{:S(2)}) %collective-permute-start.3) | collective-permute-done | bytes 253984 | tf_op jit(solution)/shard_map/ppermute | solution.py:585
  57.0 4.6 %fields.1 = (f32[8,16,128]{2,1,0:T(8,128)S(1)}, f32[24,32,256]{2,1,0:T(8,128)S(1)}, f32[24,32,256]{2,1,0:T(8,128)S(1)}, f32[24,32,256]{2,1,0:T(8,128)S(1)}, f32[...) custom-call(f32[62,8,128]{2,1,0:T(8,128)S(1)} %collective-permute-do, ...), custom_call_target="tpu_custom_call", output_to_operand_aliasing={{0}: (6, {}), {1}: (7, {}), {2}: (8, {}), {3}: (9, {}), {4}... | custom-call | tf_op jit(solution)/shard_map/fields/pallas_call | solution.py:616
  61.6 12.7 %all_to_all.22.part = f32[16,1,128]{2,1,0:T(1,128)S(1)} all-to-all(f32[16,1,128]{2,1,0:T(1,128)S(1)} %get-tuple-element.62), channel_id=1, replica_groups=mesh['gx'=4,'gy'=8,'gz'=16] {'gz'}, dimensions={0} | all-to-all | bytes 16384 | tf_op jit(solution)/shard_map/all_to_all | solution.py:625
  74.3 11.9 %all_to_all.23.gathered = f32[32,1,128]{2,1,0:T(1,128)S(1)} all-to-all(f32[32,1,128]{2,1,0:T(1,128)S(1)} %sum.1), channel_id=1, replica_groups=mesh['gx'=4,'gy'=8,'gz'=16] {'gx','gy'}, dimensions={0} | all-to-all | bytes 32768 | tf_op jit(solution)/shard_map/all_to_all | solution.py:627
  86.3 1.1 %final.1 = (f32[8,16,128]{2,1,0:T(8,128)}, f32[8,16,128]{2,1,0:T(8,128)}) custom-call(f32[32,1,128]{2,1,0:T(1,128)S(1)} %all_to_all.23.gathered, f32[512,512]{1,0:T(8,128)S(1)} %get-tuple-element.63.inv, f32[8,16,128]{2,1,0:T(8,128)S(1)} %get-tuple-element.64.d_in, f32[8,16,128]{2,1,0:T(8,128)S(1)} %get-tuple-element.65.t_in, ...), custom_call_target="tpu_custom_call" | custom-call | tf_op jit(solution)/shard_map/final/pallas_call | solution.py:628
  (1 shorter events, 0.0 us)
Async XLA Ops:
  1.3 0.8 copy-start.1
  2.1 0.8 copy-start.2
  3.0 47.9 %copy-start = (bf16[512,512]{1,0:T(8,128)(2,1)S(1)}, bf16[512,512]{1,0:T(8,128)(2,1)}, u32[]{:S(2)}) copy-start(bf16[512,512]{1,0:T(8,128)(2,1)} %factor.1) | copy-start | bytes 1572868
  23.8 23.4 %collective-permute-start = (f32[18,8,128]{2,1,0:T(8,128)S(1)}, f32[18,8,128]{2,1,0:T(8,128)S(1)}, u32[]{:S(2)}, u32[]{:S(2)}) collective-permute-start(f32[18,8,128]{2,1,0:T(8,128)S(1)} %get-tuple-element.39), channel_id=1, source_target_pairs={{16,0},{32,16},{48,32},{64,48},{80,64},{96,80},{112,96},{17,1},{33... | collective-permute-start | bytes 221192 | tf_op jit(solution)/shard_map/ppermute | solution.py:585
  25.1 22.1 %collective-permute-start.1 = (f32[18,8,128]{2,1,0:T(8,128)S(1)}, f32[18,8,128]{2,1,0:T(8,128)S(1)}, u32[]{:S(2)}, u32[]{:S(2)}) collective-permute-start(f32[18,8,128]{2,1,0:T(8,128)S(1)} %get-tuple-element.40), channel_id=1, source_target_pairs={{0,16},{16,32},{32,48},{48,64},{64,80},{80,96},{96,112},{1,17},{17... | collective-permute-start | bytes 221192 | tf_op jit(solution)/shard_map/ppermute | solution.py:585
  47.3 8.7 %collective-permute-start.2 = (f32[62,8,128]{2,1,0:T(8,128)S(1)}, f32[62,8,128]{2,1,0:T(8,128)S(1)}, u32[]{:S(2)}, u32[]{:S(2)}) collective-permute-start(f32[62,8,128]{2,1,0:T(8,128)S(1)} %get-tuple-element.44), channel_id=1, source_target_pairs={{0,128},{128,256},{256,384},{1,129},{129,257},{257,385},{2,130},{1... | collective-permute-start | bytes 761864 | tf_op jit(solution)/shard_map/ppermute | solution.py:585
  49.6 7.5 %collective-permute-start.3 = (f32[62,8,128]{2,1,0:T(8,128)S(1)}, f32[62,8,128]{2,1,0:T(8,128)S(1)}, u32[]{:S(2)}, u32[]{:S(2)}) collective-permute-start(f32[62,8,128]{2,1,0:T(8,128)S(1)} %get-tuple-element.45), channel_id=1, source_target_pairs={{128,0},{256,128},{384,256},{129,1},{257,129},{385,257},{130,2},{2... | collective-permute-start | bytes 761864 | tf_op jit(solution)/shard_map/ppermute | solution.py:585
